TPU v7x, 128 devices: a whole 4x4x4 slice. The times are simulated.
128 devices in a mesh: cuts: 32 (over y, z, core), rank: 4 (over x).
Axes of the slice: x: 4, y: 4, z: 4, core: 2. Of those that a mesh axis runs over, the one named last changes fastest.
Arguments:
- core_left: float32 [512, 512, 512], P('rank', 'cuts'), may hold values from -6 to 6
- core_mid: float32 [512, 512, 512], P('rank', 'cuts'), may hold values from -0.25 to 0.25
- core_right: float32 [512, 512, 512], P('rank', 'cuts'), may hold values from -6 to 6
- sketch_mid: float32 [256, 512, 256], P(None, 'cuts'), may hold values from -0.015625 to 0.015625
- sketch_right: float32 [256, 512, 256], P(None, 'cuts'), may hold values from -0.015625 to 0.015625
- tail_sketch: float32 [512, 256], replicated, may hold values from -0.25 to 0.25
- stencil: float32 [3, 512], P(None, 'cuts'), may hold values from 0.25 to 1
Outputs:
- ortho_core: float32 [512, 512, 256], P('rank', 'cuts')
- next_core: float32 [256, 512, 512], P('rank', 'cuts')
All inputs are finite; a program needn't handle non-finite values.
Results may differ from a plain program's by a relative error of at most 0.00014.
Values sent between devices are 32-bit elements; how exact they have to be, the bound alone decides.
No kernel may reach another device: no remote copies, remote signals or barrier semaphores. Data moves between devices by JAX's collectives and lax.ppermute only.
A program may use at most 128 MiB of HBM per device.

v0:
```python
import functools
import math

import jax
import jax.numpy as jnp
from jax import lax
from jax.experimental import pallas as pl
from jax.experimental.pallas import tpu as pltpu
from jax.sharding import Mesh
from jax.sharding import PartitionSpec as P

CUTS = ("cuts_0", "cuts_1", "cuts_2")
EVERY = ("rank", "cuts_0", "cuts_1", "cuts_2")
HIGHEST = lax.Precision.HIGHEST
HIGH = lax.Precision.HIGH
F32 = jnp.float32
BF16 = jnp.bfloat16
LANES = 128
TILE = 8
BLOCK = 64

NN = (((1,), (0,)), ((), ()))
NT = (((1,), (1,)), ((), ()))
TN = (((0,), (0,)), ((), ()))


def halves(x):
    high = x.astype(BF16)
    return high, (x - high.astype(F32)).astype(BF16)


def dot3(a, b, dims):
    (ah, al), (bh, bl) = a, b
    dot = functools.partial(lax.dot_general, dimension_numbers=dims, preferred_element_type=F32)
    return dot(ah, bh) + (dot(ah, bl) + dot(al, bh))


def exact(a, b, dims):
    return lax.dot_general(a, b, dims, precision=HIGHEST, preferred_element_type=F32)


def whole_block(shape):
    return pl.BlockSpec(shape, lambda *_: (0,) * len(shape))


def contract_kernel(core_ref, part_ref, *refs):
    *sketch_refs, out_ref, applied_ref = refs
    quarters, rows, slices, width = core_ref.shape
    part = halves(part_ref[...])
    core = [core_ref[q].reshape(rows * slices, width) for q in range(quarters)]
    core = core[0] if quarters == 1 else jnp.concatenate(core, axis=1)
    applied = dot3(halves(core), part, NN)
    for h in range(len(sketch_refs)):
        applied_ref[h] = applied[:, h * LANES : (h + 1) * LANES]
    sketch_rows = sketch_refs[0].shape[0]
    sketches = [ref.reshape(sketch_rows * slices, LANES) for ref in sketch_refs]
    total = None
    for i in range(slices):
        left = [applied_ref.at[h][pl.ds(i, rows, stride=slices), :] for h in range(len(sketches))]
        right = [ref[pl.ds(i, sketch_rows, stride=slices), :] for ref in sketches]
        term = dot3(halves(jnp.concatenate(left, axis=1)), halves(jnp.concatenate(right, axis=1)), NT)
        total = term if total is None else total + term

    @pl.when(pl.program_id(0) == 0)
    def _():
        out_ref[...] = total

    @pl.when(pl.program_id(0) > 0)
    def _():
        out_ref[...] += total


def contract_back(core, part, sketch):
    quarters, rows, slices, width = core.shape
    sketch_rows, _, sketch_cols = sketch.shape
    pieces = sketch_cols // LANES
    return pl.pallas_call(
        contract_kernel,
        grid=(slices // TILE,),
        in_specs=[
            pl.BlockSpec((quarters, rows, TILE, width), lambda g: (0, 0, g, 0)),
            whole_block(part.shape),
            *[pl.BlockSpec((sketch_rows, TILE, LANES), lambda g, h=h: (0, g, h)) for h in range(pieces)],
        ],
        out_specs=whole_block((rows, sketch_rows)),
        out_shape=jax.ShapeDtypeStruct((rows, sketch_rows), F32),
        scratch_shapes=[pltpu.VMEM((pieces, rows * TILE, LANES), F32)],
        name="contract",
    )(core, part, *[sketch] * pieces)


def stencil_kernel(core_ref, below_ref, above_ref, coef_ref, out_ref):
    rows, slices, _ = core_ref.shape
    place = lax.broadcasted_iota(jnp.int32, (rows * slices, LANES), 0) % slices
    for q in range(out_ref.shape[0]):
        cols = pl.ds(q * LANES, LANES)
        core = core_ref[:, :, cols].reshape(rows * slices, LANES)
        first = jnp.broadcast_to(below_ref[:, cols][:, None, :], (rows, slices, LANES)).reshape(rows * slices, LANES)
        last = jnp.broadcast_to(above_ref[:, cols][:, None, :], (rows, slices, LANES)).reshape(rows * slices, LANES)
        below = jnp.where(place == 0, first, pltpu.roll(core, 1, 0))
        above = jnp.where(place == slices - 1, last, pltpu.roll(core, rows * slices - 1, 0))
        coef = [jnp.broadcast_to(coef_ref[k][None], (rows, slices, LANES)).reshape(rows * slices, LANES) for k in range(3)]
        stepped = coef[0] * below + coef[1] * core + coef[2] * above
        out_ref[q] = stepped.reshape(rows, slices, LANES)


def step_core(core, below, above, stencil):
    rows, slices, width = core.shape
    group = 16
    quarters = width // LANES
    coef = jnp.broadcast_to(stencil[:, :, None], (3, slices, LANES))
    return pl.pallas_call(
        stencil_kernel,
        grid=(rows // group,),
        in_specs=[
            pl.BlockSpec((group, slices, width), lambda g: (g, 0, 0)),
            pl.BlockSpec((group, width), lambda g: (g, 0)),
            pl.BlockSpec((group, width), lambda g: (g, 0)),
            whole_block(coef.shape),
        ],
        out_specs=pl.BlockSpec((quarters, group, slices, LANES), lambda g: (0, g, 0, 0)),
        out_shape=jax.ShapeDtypeStruct((quarters, rows, slices, LANES), F32),
        name="stencil",
    )(core, below, above, coef)


def invert_factor(work_ref):
    size = work_ref.shape[0]
    lane_tiles = size // LANES
    sub = lax.broadcasted_iota(jnp.int32, (TILE, LANES), 0)
    lane = lax.broadcasted_iota(jnp.int32, (TILE, LANES), 1)
    for block in range(0, size, BLOCK):
        count = BLOCK // TILE
        tiles = [
            [work_ref[pl.ds(block + t * TILE, TILE), pl.ds(h * LANES, LANES)] for h in range(lane_tiles)]
            for t in range(count)
        ]
        for p in range(count):
            k = block + p * TILE
            home, at = divmod(k, LANES)
            cols = {
                (t, j): jnp.broadcast_to(tiles[t][home][:, at + j : at + j + 1], (TILE, LANES))
                for t in range(p, count)
                for j in range(TILE)
            }
            inside = (lane >= at) & (lane < at + TILE)
            for t in range(p, count):
                fresh = jnp.where(lane - at == sub, 1.0, 0.0) if t == p else jnp.zeros((TILE, LANES), F32)
                tiles[t][home] = jnp.where(inside, fresh, tiles[t][home])
            for j in range(TILE):

                def row(x, j=j):
                    return jnp.broadcast_to(x[j : j + 1, :], (TILE, LANES))

                scale = lax.rsqrt(row(cols[p, j]))
                pivots = {jj: row(cols[p, jj]) * scale for jj in range(j + 1, TILE)}
                lines = [row(tiles[p][h]) * scale for h in range(lane_tiles)]
                for t in range(p, count):
                    m = cols[t, j] * scale
                    if t == p:
                        m = jnp.where(sub > j, m, 0.0)
                    for jj in range(j + 1, TILE):
                        cols[t, jj] = cols[t, jj] - m * pivots[jj]
                    for h in range(lane_tiles):
                        new = tiles[t][h] - m * lines[h]
                        tiles[t][h] = jnp.where(sub == j, lines[h], new) if t == p else new
        for t in range(count):
            for h in range(lane_tiles):
                work_ref[pl.ds(block + t * TILE, TILE), pl.ds(h * LANES, LANES)] = tiles[t][h]
        end = block + BLOCK
        if end < size:
            done = work_ref[pl.ds(block, BLOCK), :]
            col = lax.broadcasted_iota(jnp.int32, (size, size), 1)
            own_row = lax.broadcasted_iota(jnp.int32, (BLOCK, size), 0) + block
            own_col = lax.broadcasted_iota(jnp.int32, (BLOCK, size), 1)
            change = exact(done, jnp.where((own_col > own_row) & (own_col < end), 0.0, done), TN)
            rest = jnp.where((col >= block) & (col < end), 0.0, work_ref[...])
            rest = rest - change
            work_ref[pl.ds(end, size - end), :] = rest[end:, :]


def factor_kernel(scale, mid_ref, gram_ref, left_ref, project_ref, work_ref):
    mid = mid_ref[...]
    cross = exact(gram_ref[...], mid, NN)
    work_ref[...] = exact(mid, cross, TN)
    invert_factor(work_ref)
    row = lax.broadcasted_iota(jnp.int32, work_ref.shape, 0)
    col = lax.broadcasted_iota(jnp.int32, work_ref.shape, 1)
    inverse = jnp.where(row >= col, work_ref[...], 0.0)
    left_ref[...] = exact(mid, inverse, NT) * scale
    project_ref[...] = exact(inverse, cross, NT)


def factored(mid_sum, gram_left, scale):
    rank_width, sketch_width = mid_sum.shape
    return pl.pallas_call(
        functools.partial(factor_kernel, scale),
        out_shape=(
            jax.ShapeDtypeStruct((rank_width, sketch_width), F32),
            jax.ShapeDtypeStruct((sketch_width, rank_width), F32),
        ),
        scratch_shapes=[pltpu.VMEM((sketch_width, sketch_width), F32)],
        name="factor",
    )(mid_sum, gram_left)


def apply_kernel(rows_ref, right_ref, out_ref):
    out_ref[...] = dot3(halves(rows_ref[...]), halves(right_ref[...]), NN)


def apply_right(rows, right):
    count, depth = rows.shape
    width = right.shape[1]
    group = 512
    return pl.pallas_call(
        apply_kernel,
        grid=(count // group,),
        in_specs=[pl.BlockSpec((group, depth), lambda g: (g, 0)), whole_block(right.shape)],
        out_specs=pl.BlockSpec((group, width), lambda g: (g, 0)),
        out_shape=jax.ShapeDtypeStruct((count, width), F32),
        name="ortho",
    )(rows, right)


def project_kernel(project_ref, stepped_ref, out_ref):
    depth, slices, _ = stepped_ref.shape
    rows = project_ref.shape[0]
    project = halves(project_ref[...])
    stepped = stepped_ref.reshape(depth * slices, LANES)
    out = out_ref.reshape(rows * slices, LANES)
    for i in range(0, slices, 2):
        pair = jnp.concatenate([stepped[pl.ds(i + d, depth, stride=slices), :] for d in range(2)], axis=1)
        product = dot3(project, halves(pair), NN)
        for d in range(2):
            out[pl.ds(i + d, rows, stride=slices), :] = product[:, d * LANES : (d + 1) * LANES]


def projected(project, stepped):
    depth, slices, _ = stepped.shape
    rows = project.shape[0]
    return pl.pallas_call(
        project_kernel,
        grid=(slices // TILE,),
        in_specs=[whole_block(project.shape), pl.BlockSpec((depth, TILE, LANES), lambda g: (0, g, 0))],
        out_specs=pl.BlockSpec((rows, TILE, LANES), lambda g: (0, g, 0)),
        out_shape=jax.ShapeDtypeStruct((rows, slices, LANES), F32),
        name="project",
    )(project, stepped)


def summed_lines(partial, axes):
    peers = lax.axis_size(axes)
    blocks = partial.reshape(peers, -1, partial.shape[-1])
    return jnp.sum(lax.all_to_all(blocks, axes, 0, 0, tiled=True), axis=0)


def whole_of(lines):
    copies = jnp.broadcast_to(lines, (lax.axis_size(EVERY), *lines.shape))
    return lax.all_to_all(copies, EVERY, 0, 0, tiled=True).reshape(-1, lines.shape[-1])


def neighbours(core):
    count = lax.axis_size(CUTS)
    head, tail = core[:, 0, :], core[:, -1, :]
    below = lax.ppermute(tail, CUTS, [(i, i + 1) for i in range(count - 1)])
    above = lax.ppermute(head, CUTS, [(i + 1, i) for i in range(count - 1)])
    return below, above


def shards(core_left, core_mid, core_right, sketch_mid, sketch_right, tail_sketch, stencil):
    row_count, slices, rank_width = core_left.shape
    sketch_width = tail_sketch.shape[1]
    quarters = rank_width // LANES
    ranks = lax.axis_size("rank")

    below, above = neighbours(core_mid)
    right_part = contract_back(core_right[None], tail_sketch, sketch_right)
    stepped = step_core(core_mid, below, above, stencil)
    right_sum = whole_of(summed_lines(right_part, CUTS))

    own_cols = lax.all_to_all(stepped, "rank", 0, 0, tiled=True)

    flat_left = core_left.reshape(row_count * slices, rank_width)
    local_gram = lax.dot_general(flat_left, flat_left, TN, precision=HIGH, preferred_element_type=F32)
    gram_left = whole_of(summed_lines(local_gram, EVERY))

    mid_sum = whole_of(summed_lines(contract_back(stepped, right_sum, sketch_mid), CUTS))

    scale = math.sqrt(rank_width * slices * lax.axis_size(CUTS))
    left, project = factored(mid_sum, gram_left, scale)

    product = projected(project, own_cols.reshape(rank_width, slices, LANES))
    blocks = product.reshape(ranks, sketch_width // ranks, slices, LANES)
    arrived = lax.all_to_all(blocks, "rank", 0, 0, tiled=True)
    next_core = jnp.moveaxis(arrived, 0, 2).reshape(sketch_width // ranks, slices, quarters * LANES)

    ortho_core = apply_right(flat_left, left).reshape(row_count, slices, sketch_width)
    return ortho_core, next_core


def solution(mesh):
    split = Mesh(
        mesh.devices.reshape(4, 4, 2, mesh.shape["rank"]), ("cuts_0", "cuts_1", "cuts_2", "rank")
    )
    in_specs = (
        P("rank", CUTS, None),
        P("rank", CUTS, None),
        P("rank", CUTS, None),
        P(None, CUTS, None),
        P(None, CUTS, None),
        P(),
        P(None, CUTS),
    )
    out_specs = (P("rank", CUTS, None), P("rank", CUTS, None))
    return jax.shard_map(
        shards, mesh=split, in_specs=in_specs, out_specs=out_specs, check_vma=False
    )
```

profile of v0, /device:TPU:0, one launch (start us, length us, event | category | flops | bytes accessed | tf_op | source)
XLA Modules:
  0.0 257.3 jit_solution(15491195304004393558)
XLA Ops:
  0.6 10.4 %contract.2 = f32[128,256]{1,0:T(8,128)} custom-call(f32[1,128,16,512]{3,2,1,0:T(8,128)} %bitcast.26, f32[512,256]{1,0:T(8,128)} %part_ref.1, f32[256,16,256]{2,1,0:T(8,128)} %refs_1_.2, f32[256,16,256]{2,1,0:T(8,128)} %refs_1_.2), custom_call_target="tpu_custom_call" | custom-call | tf_op jit(solution)/shard_map/contract/pallas_call | solution.py:77
  11.0 0.9 reshape.38
  12.0 16.1 %all_to_all.40 = f32[32,4,256]{2,1,0:T(4,128)S(1)} all-to-all(f32[32,4,256]{2,1,0:T(4,128)S(1)} %reshape.38), channel_id=1, replica_groups=mesh['cuts_0'=4,'cuts_1'=4,'cuts_2'=2,'rank'=4] {'cuts_0','cuts_1','cuts..., dimensions={0} | all-to-all | bytes 262144 | tf_op jit(solution)/shard_map/all_to_all | solution.py:254
  28.1 0.9 broadcast_in_dim.20
  28.9 6.3 %all-to-all-start.1 = ((f32[128,4,256]{2,1,0:T(4,128)}), f32[128,4,256]{2,1,0:T(4,128)S(1)}, u32[]{:S(2)}, u32[]{:S(2)}) async-start(f32[128,4,256]{2,1,0:T(4,128)} %broadcast_in_dim.20), calls=%async_computation.1 | async-start | bytes 1048576 | tf_op jit(solution)/shard_map/all_to_all | solution.py:259
  35.3 2.7 %fusion.2 = (f32[128,1,512]{2,1,0:T(1,128)S(1)}, f32[128,1,512]{2,1,0:T(1,128)S(1)}) fusion(f32[128,16,512]{2,1,0:T(8,128)} %core_ref.1), kind=kLoop, calls=%fused_computation.5 | loop fusion | bytes 1048576 | tf_op jit(solution)/shard_map/slice | solution.py:264
  38.1 1.4 collective-permute-start
  39.5 1.3 collective-permute-start.1
  40.8 5.4 %copy.20 = f32[512,2048]{1,0:T(8,128)} copy(f32[512,2048]{0,1:T(8,128)} %bitcast.22) | data formatting | bytes 8388608 | tf_op jit(solution)/shard_map/dot_general | solution.py:284
  46.2 0.0 copy-start.2
  46.2 5.2 %dot_general.8 = f32[128,4,2048]{2,1,0:T(4,128)} reshape(f32[512,2048]{1,0:T(8,128)} %copy.20) | data formatting | bytes 8388608 | tf_op jit(solution)/shard_map/dot_general | solution.py:284
  51.4 0.0 collective-permute-done.below_ref
  51.4 0.0 copy-start
  51.4 0.0 collective-permute-done.1.above_ref
  51.4 0.0 copy-done.2
  51.4 0.0 copy-start.1
  51.4 0.8 broadcast_in_dim.18.coef_ref
  52.2 0.0 copy-done
  52.2 0.0 copy-done.1
  52.2 7.5 %stencil.1.core_ref = f32[4,128,16,128]{3,2,1,0:T(8,128)} custom-call(f32[128,16,512]{2,1,0:T(8,128)} %core_ref.1, f32[128,512]{1,0:T(8,128)} %copy-done, f32[128,512]{1,0:T(8,128)} %copy-done.1, f32[3,16,128]{2,1,0:T(8,128)} %broadcast_in_dim.18.coef_ref), custom_call_target="tpu_custom_call" | custom-call | tf_op jit(solution)/shard_map/stencil/pallas_call | solution.py:112
  59.7 0.0 all-to-all-done.1
  59.7 1.0 reshape.39.part_ref
  60.7 10.4 %contract.3 = f32[128,256]{1,0:T(8,128)} custom-call(f32[4,128,16,128]{3,2,1,0:T(8,128)} %stencil.1.core_ref, f32[512,256]{1,0:T(8,128)} %reshape.39.part_ref, f32[256,16,256]{2,1,0:T(8,128)} %refs_1_.3, f32[256,16,256]{2,1,0:T(8,128)} %refs_1_.3), custom_call_target="tpu_custom_call" | custom-call | tf_op jit(solution)/shard_map/contract/pallas_call | solution.py:77
  71.1 1.6 reshape.40
  72.7 10.1 %all-to-all-start.2 = ((f32[32,4,256]{2,1,0:T(4,128)}), f32[32,4,256]{2,1,0:T(4,128)S(1)}, u32[]{:S(2)}, u32[]{:S(2)}) async-start(f32[32,4,256]{2,1,0:T(4,128)} %reshape.40), calls=%async_computation.2 | async-start | bytes 262144 | tf_op jit(solution)/shard_map/all_to_all | solution.py:254
  82.8 11.4 %fusion = f32[128,4,512]{2,0,1:T(8,128)S(1)} fusion(f32[2048,512,1]{1,0,2:T(8,128)} %bitcast.23, f32[128,4,2048]{2,1,0:T(4,128)} %dot_general.8), kind=kOutput, calls=%fused_computation | convolution fusion | flops 3221225472 | bytes 9437184 | tf_op jit(solution)/shard_map/dot_general | solution.py:284
  94.2 1.6 copy.22
  95.9 0.0 all-to-all-done.2
  95.9 9.9 %all-to-all-start.4 = ((f32[128,4,512]{2,1,0:T(4,128)}), f32[128,4,512]{2,1,0:T(4,128)S(1)}, u32[]{:S(2)}, u32[]{:S(2)}) async-start(f32[128,4,512]{2,1,0:T(4,128)} %copy.22), calls=%async_computation.4 | async-start | bytes 2097152 | tf_op jit(solution)/shard_map/all_to_all | solution.py:254
  105.8 19.3 %all-to-all-done.4 = f32[128,4,512]{2,1,0:T(4,128)S(1)} async-done(((f32[128,4,512]{2,1,0:T(4,128)}), f32[128,4,512]{2,1,0:T(4,128)S(1)}, u32[]{:S(2)}, u32[]{:S(2)}) %all-to-all-start.4) | async-done | bytes 1048608 | tf_op jit(solution)/shard_map/all_to_all | solution.py:254
  125.2 0.9 broadcast_in_dim.21
  126.0 4.6 %all-to-all-start.3 = ((f32[128,4,256]{2,1,0:T(4,128)}), f32[128,4,256]{2,1,0:T(4,128)S(1)}, u32[]{:S(2)}, u32[]{:S(2)}) async-start(f32[128,4,256]{2,1,0:T(4,128)} %broadcast_in_dim.21), calls=%async_computation.3 | async-start | bytes 1048576 | tf_op jit(solution)/shard_map/all_to_all | solution.py:259
  130.6 0.2 reduce_sum.29
  130.9 13.5 %all-to-all-done.3 = f32[128,4,256]{2,1,0:T(4,128)S(1)} async-done(((f32[128,4,256]{2,1,0:T(4,128)}), f32[128,4,256]{2,1,0:T(4,128)S(1)}, u32[]{:S(2)}, u32[]{:S(2)}) %all-to-all-start.3) | async-done | bytes 524320 | tf_op jit(solution)/shard_map/all_to_all | solution.py:259
  144.4 0.1 broadcast_in_dim.22
  144.5 23.7 %all_to_all.41 = f32[128,4,512]{2,1,0:T(4,128)S(1)} all-to-all(f32[128,4,512]{2,1,0:T(4,128)S(1)} %broadcast_in_dim.22), channel_id=1, replica_groups=mesh['cuts_0'=4,'cuts_1'=4,'cuts_2'=2,'rank'=4] {'rank','cuts_0','cuts_1..., dimensions={0} | all-to-all | bytes 2097152 | tf_op jit(solution)/shard_map/all_to_all | solution.py:259
  168.2 5.0 %all-to-all-start.6 = ((f32[4,128,16,128]{3,2,1,0:T(8,128)}), f32[4,128,16,128]{3,2,1,0:T(8,128)}, u32[]{:S(2)}, u32[]{:S(2)}) async-start(f32[4,128,16,128]{3,2,1,0:T(8,128)} %stencil.1.core_ref), calls=%async_computation.6 | async-start | bytes 8388608 | tf_op jit(solution)/shard_map/all_to_all | solution.py:281
  173.2 1.0 reshape.41.mid_ref
  174.2 1.3 reshape.42.gram_ref
  175.6 14.4 %factor.1 = (f32[512,256]{1,0:T(8,128)}, f32[256,512]{1,0:T(8,128)}) custom-call(f32[512,256]{1,0:T(8,128)} %reshape.41.mid_ref, f32[512,512]{1,0:T(8,128)} %reshape.42.gram_ref), custom_call_target="tpu_custom_call" | custom-call | tf_op jit(solution)/shard_map/factor/pallas_call | solution.py:196
  189.9 31.7 %all-to-all-done.6 = f32[4,128,16,128]{3,2,1,0:T(8,128)} async-done(((f32[4,128,16,128]{3,2,1,0:T(8,128)}), f32[4,128,16,128]{3,2,1,0:T(8,128)}, u32[]{:S(2)}, u32[]{:S(2)}) %all-to-all-start.6) | async-done | bytes 4194336 | tf_op jit(solution)/shard_map/all_to_all | solution.py:281
  221.6 5.2 %project.1 = f32[256,16,128]{2,1,0:T(8,128)} custom-call(f32[256,512]{1,0:T(8,128)} %get-tuple-element.5.project_ref, f32[512,16,128]{2,1,0:T(8,128)} %bitcast.7.stepped_ref), custom_call_target="tpu_custom_call" | custom-call | tf_op jit(solution)/shard_map/project/pallas_call | solution.py:241
  226.9 3.6 %all-to-all-start.7 = ((f32[4,64,16,128]{3,2,1,0:T(8,128)}), f32[4,64,16,128]{3,2,1,0:T(8,128)S(1)}, u32[]{:S(2)}, u32[]{:S(2)}) async-start(f32[4,64,16,128]{3,2,1,0:T(8,128)} %bitcast.25), calls=%async_computation.7 | async-start | bytes 4194304 | tf_op jit(solution)/shard_map/all_to_all | solution.py:294
  230.5 5.4 %ortho.1 = f32[2048,256]{1,0:T(8,128)} custom-call(f32[2048,512]{1,0:T(8,128)} %bitcast.24, f32[512,256]{1,0:T(8,128)} %get-tuple-element.4.right_ref), custom_call_target="tpu_custom_call" | custom-call | tf_op jit(solution)/shard_map/ortho/pallas_call | solution.py:215
  235.9 19.8 %all-to-all-done.7 = f32[4,64,16,128]{3,2,1,0:T(8,128)S(1)} async-done(((f32[4,64,16,128]{3,2,1,0:T(8,128)}), f32[4,64,16,128]{3,2,1,0:T(8,128)S(1)}, u32[]{:S(2)}, u32[]{:S(2)}) %all-to-all-start.7) | async-done | bytes 2097184 | tf_op jit(solution)/shard_map/all_to_all | solution.py:294
  255.6 1.6 copy_bitcast_fusion
  (4 shorter events, 0.1 us)
Async XLA Ops:
  28.9 30.8 %all-to-all-start.1 = ((f32[128,4,256]{2,1,0:T(4,128)}), f32[128,4,256]{2,1,0:T(4,128)S(1)}, u32[]{:S(2)}, u32[]{:S(2)}) async-start(f32[128,4,256]{2,1,0:T(4,128)} %broadcast_in_dim.20), calls=%async_computation.1 | async-start | bytes 1048576 | tf_op jit(solution)/shard_map/all_to_all | solution.py:259
  38.1 13.3 %collective-permute-start = (f32[128,512]{1,0:T(8,128)S(1)}, f32[128,512]{1,0:T(8,128)S(1)}, u32[]{:S(2)}, u32[]{:S(2)}) collective-permute-start(f32[128,512]{1,0:T(8,128)S(1)} %bitcast.28), channel_id=1, source_target_pairs={{0,4},{4,8},{8,12},{12,16},{16,20},{20,24},{24,28},{28,32},{32,36}... | collective-permute-start | bytes 786440 | tf_op jit(solution)/shard_map/ppermute | solution.py:265
  39.5 11.9 %collective-permute-start.1 = (f32[128,512]{1,0:T(8,128)S(1)}, f32[128,512]{1,0:T(8,128)S(1)}, u32[]{:S(2)}, u32[]{:S(2)}) collective-permute-start(f32[128,512]{1,0:T(8,128)S(1)} %bitcast.29), channel_id=1, source_target_pairs={{4,0},{8,4},{12,8},{16,12},{20,16},{24,20},{28,24},{32,28},{36,32}... | collective-permute-start | bytes 786440 | tf_op jit(solution)/shard_map/ppermute | solution.py:266
  46.2 5.2 %copy-start.2 = (f32[3,16]{1,0:T(4,128)S(1)}, f32[3,16]{1,0:T(4,128)}, u32[]{:S(2)}) copy-start(f32[3,16]{1,0:T(4,128)} %param.13) | copy-start | bytes 580
  51.4 0.8 copy-start
  51.4 0.8 copy-start.1
  72.7 23.2 %all-to-all-start.2 = ((f32[32,4,256]{2,1,0:T(4,128)}), f32[32,4,256]{2,1,0:T(4,128)S(1)}, u32[]{:S(2)}, u32[]{:S(2)}) async-start(f32[32,4,256]{2,1,0:T(4,128)} %reshape.40), calls=%async_computation.2 | async-start | bytes 262144 | tf_op jit(solution)/shard_map/all_to_all | solution.py:254
  95.9 29.3 %all-to-all-start.4 = ((f32[128,4,512]{2,1,0:T(4,128)}), f32[128,4,512]{2,1,0:T(4,128)S(1)}, u32[]{:S(2)}, u32[]{:S(2)}) async-start(f32[128,4,512]{2,1,0:T(4,128)} %copy.22), calls=%async_computation.4 | async-start | bytes 2097152 | tf_op jit(solution)/shard_map/all_to_all | solution.py:254
  126.0 18.4 %all-to-all-start.3 = ((f32[128,4,256]{2,1,0:T(4,128)}), f32[128,4,256]{2,1,0:T(4,128)S(1)}, u32[]{:S(2)}, u32[]{:S(2)}) async-start(f32[128,4,256]{2,1,0:T(4,128)} %broadcast_in_dim.21), calls=%async_computation.3 | async-start | bytes 1048576 | tf_op jit(solution)/shard_map/all_to_all | solution.py:259
  168.2 53.4 %all-to-all-start.6 = ((f32[4,128,16,128]{3,2,1,0:T(8,128)}), f32[4,128,16,128]{3,2,1,0:T(8,128)}, u32[]{:S(2)}, u32[]{:S(2)}) async-start(f32[4,128,16,128]{3,2,1,0:T(8,128)} %stencil.1.core_ref), calls=%async_computation.6 | async-start | bytes 8388608 | tf_op jit(solution)/shard_map/all_to_all | solution.py:281
  226.9 28.8 %all-to-all-start.7 = ((f32[4,64,16,128]{3,2,1,0:T(8,128)}), f32[4,64,16,128]{3,2,1,0:T(8,128)S(1)}, u32[]{:S(2)}, u32[]{:S(2)}) async-start(f32[4,64,16,128]{3,2,1,0:T(8,128)} %bitcast.25), calls=%async_computation.7 | async-start | bytes 4194304 | tf_op jit(solution)/shard_map/all_to_all | solution.py:294
where the time goes:
time: 258 us; the launch traced here: 257 us
  waiting for transfers between devices  84.3 us (33%)
  Pallas kernels  53.3 us (21%)
  starting transfers between devices  42.3 us (16%)
  blocking collectives  39.8 us (15%)
  local copies, waits for them, and re-layouts  25.1 us (10%)
  matrix products  11.4 us (4%)
    all_to_all x1, waiting for transfers between devices, shards(): own_cols = lax.all_to_all(stepped, 'rank', 0, 0, tiled=True)  31.7 us
    all_to_all x1, blocking collectives, whole_of(): lax.all_to_all(copies, EVERY, 0, 0, tiled=True).reshape(-1, lines.shape[-1])  23.7 us
    pallas_call x2, Pallas kernels, contract_back(): pl.pallas_call(contract_kernel, grid=(slices // TILE,), in_specs=[pl.Bloc...  20.8 us
    all_to_all x2, starting transfers between devices, summed_lines(): return jnp.sum(lax.all_to_all(blocks, axes, 0, 0, tiled=True), axis=0)  20.1 us
    all_to_all x1, waiting for transfers between devices, shards(): arrived = lax.all_to_all(blocks, 'rank', 0, 0, tiled=True)  19.8 us
    all_to_all x2, waiting for transfers between devices, summed_lines(): return jnp.sum(lax.all_to_all(blocks, axes, 0, 0, tiled=True), axis=0)  19.3 us
    all_to_all x1, blocking collectives, summed_lines(): return jnp.sum(lax.all_to_all(blocks, axes, 0, 0, tiled=True), axis=0)  16.1 us
    pallas_call x1, Pallas kernels, factored(): pl.pallas_call(functools.partial(factor_kernel, scale), out_shape=(jax.Sh...  14.4 us
  transfers between devices with their start and end apart: 8, of which 4 were waited for; matrix products, arithmetic and copies ran while one was open for 12% of the time, Pallas kernels for 11%

commit v1 on v0

--- a/solution.py
+++ b/solution.py
@@ -12,12 +12,12 @@
 CUTS = ("cuts_0", "cuts_1", "cuts_2")
 EVERY = ("rank", "cuts_0", "cuts_1", "cuts_2")
 HIGHEST = lax.Precision.HIGHEST
-HIGH = lax.Precision.HIGH
 F32 = jnp.float32
 BF16 = jnp.bfloat16
 LANES = 128
 TILE = 8
 BLOCK = 64
+PIECES = (1, 1, 2, 1)
 
 NN = (((1,), (0,)), ((), ()))
 NT = (((1,), (1,)), ((), ()))
@@ -43,13 +43,26 @@
     return pl.BlockSpec(shape, lambda *_: (0,) * len(shape))
 
 
-def contract_kernel(core_ref, part_ref, *refs):
-    *sketch_refs, out_ref, applied_ref = refs
-    quarters, rows, slices, width = core_ref.shape
-    part = halves(part_ref[...])
-    core = [core_ref[q].reshape(rows * slices, width) for q in range(quarters)]
-    core = core[0] if quarters == 1 else jnp.concatenate(core, axis=1)
-    applied = dot3(halves(core), part, NN)
+def own_block(rank_ref, distance, ranks):
+    return pl.multiple_of(lax.rem(rank_ref[0] + distance, ranks) * LANES, LANES)
+
+
+def contract_kernel(core_parts, rank_ref, part_ref, *refs):
+    count = sum(core_parts) if core_parts else 1
+    core_refs, (*sketch_refs, out_ref, applied_ref) = list(refs[:count]), refs[count:]
+    slices = core_refs[0].shape[1]
+    if not core_parts:
+        core = core_refs[0][...].reshape(-1, core_refs[0].shape[2])
+        part = part_ref[...]
+    else:
+        blocks, lines = [], []
+        for distance, pieces in enumerate(core_parts):
+            taken = [core_refs.pop(0)[...].reshape(-1, LANES) for _ in range(pieces)]
+            blocks.append(taken[0] if pieces == 1 else jnp.concatenate(taken, axis=0))
+            lines.append(part_ref[pl.ds(own_block(rank_ref, distance, len(core_parts)), LANES), :])
+        core, part = jnp.concatenate(blocks, axis=1), jnp.concatenate(lines, axis=0)
+    rows = core.shape[0] // slices
+    applied = dot3(halves(core), halves(part), NN)
     for h in range(len(sketch_refs)):
         applied_ref[h] = applied[:, h * LANES : (h + 1) * LANES]
     sketch_rows = sketch_refs[0].shape[0]
@@ -70,58 +83,83 @@
         out_ref[...] += total
 
 
-def contract_back(core, part, sketch):
-    quarters, rows, slices, width = core.shape
+SCALAR = pl.BlockSpec(memory_space=pltpu.SMEM)
+
+
+def contract_back(rank, cores, core_parts, part, sketch):
+    slices = cores[0].shape[1]
     sketch_rows, _, sketch_cols = sketch.shape
+    rows = sum(core.shape[0] for core in cores[: core_parts[0] if core_parts else 1])
     pieces = sketch_cols // LANES
     return pl.pallas_call(
-        contract_kernel,
+        functools.partial(contract_kernel, core_parts),
         grid=(slices // TILE,),
         in_specs=[
-            pl.BlockSpec((quarters, rows, TILE, width), lambda g: (0, 0, g, 0)),
+            SCALAR,
             whole_block(part.shape),
+            *[pl.BlockSpec((core.shape[0], TILE, core.shape[2]), lambda g: (0, g, 0)) for core in cores],
             *[pl.BlockSpec((sketch_rows, TILE, LANES), lambda g, h=h: (0, g, h)) for h in range(pieces)],
         ],
         out_specs=whole_block((rows, sketch_rows)),
         out_shape=jax.ShapeDtypeStruct((rows, sketch_rows), F32),
         scratch_shapes=[pltpu.VMEM((pieces, rows * TILE, LANES), F32)],
         name="contract",
-    )(core, part, *[sketch] * pieces)
-
-
-def stencil_kernel(core_ref, below_ref, above_ref, coef_ref, out_ref):
+    )(rank, part, *cores, *[sketch] * pieces)
+
+
+def stencil_kernel(pieces, rank_ref, core_ref, below_ref, above_ref, coef_ref, *out_refs):
     rows, slices, _ = core_ref.shape
+    out_refs = list(out_refs)
     place = lax.broadcasted_iota(jnp.int32, (rows * slices, LANES), 0) % slices
-    for q in range(out_ref.shape[0]):
-        cols = pl.ds(q * LANES, LANES)
+    coef = [jnp.broadcast_to(coef_ref[k][None], (rows, slices, LANES)).reshape(rows * slices, LANES) for k in range(3)]
+    for distance, count in enumerate(pieces):
+        cols = pl.ds(own_block(rank_ref, distance, len(pieces)), LANES)
         core = core_ref[:, :, cols].reshape(rows * slices, LANES)
         first = jnp.broadcast_to(below_ref[:, cols][:, None, :], (rows, slices, LANES)).reshape(rows * slices, LANES)
         last = jnp.broadcast_to(above_ref[:, cols][:, None, :], (rows, slices, LANES)).reshape(rows * slices, LANES)
         below = jnp.where(place == 0, first, pltpu.roll(core, 1, 0))
         above = jnp.where(place == slices - 1, last, pltpu.roll(core, rows * slices - 1, 0))
-        coef = [jnp.broadcast_to(coef_ref[k][None], (rows, slices, LANES)).reshape(rows * slices, LANES) for k in range(3)]
-        stepped = coef[0] * below + coef[1] * core + coef[2] * above
-        out_ref[q] = stepped.reshape(rows, slices, LANES)
-
-
-def step_core(core, below, above, stencil):
+        stepped = (coef[0] * below + coef[1] * core + coef[2] * above).reshape(rows, slices, LANES)
+        each = pl.num_programs(0) // count
+        for n in range(count):
+            out_ref = out_refs.pop(0)
+            if count == 1:
+                out_ref[...] = stepped
+                continue
+
+            @pl.when(pl.program_id(0) // each == n)
+            def _(out_ref=out_ref, stepped=stepped):
+                out_ref[...] = stepped
+
+
+def step_core(rank, core, below, above, stencil, pieces):
     rows, slices, width = core.shape
     group = 16
-    quarters = width // LANES
     coef = jnp.broadcast_to(stencil[:, :, None], (3, slices, LANES))
-    return pl.pallas_call(
-        stencil_kernel,
+    out_specs, out_shape = [], []
+    for count in pieces:
+        each = rows // group // count
+        for n in range(count):
+            out_specs.append(
+                pl.BlockSpec(
+                    (group, slices, LANES), lambda g, n=n, each=each: (jnp.clip(g - n * each, 0, each - 1), 0, 0)
+                )
+            )
+            out_shape.append(jax.ShapeDtypeStruct((rows // count, slices, LANES), F32))
+    return pl.pallas_call(
+        functools.partial(stencil_kernel, pieces),
         grid=(rows // group,),
         in_specs=[
+            SCALAR,
             pl.BlockSpec((group, slices, width), lambda g: (g, 0, 0)),
             pl.BlockSpec((group, width), lambda g: (g, 0)),
             pl.BlockSpec((group, width), lambda g: (g, 0)),
             whole_block(coef.shape),
         ],
-        out_specs=pl.BlockSpec((quarters, group, slices, LANES), lambda g: (0, g, 0, 0)),
-        out_shape=jax.ShapeDtypeStruct((quarters, rows, slices, LANES), F32),
+        out_specs=out_specs,
+        out_shape=out_shape,
         name="stencil",
-    )(core, below, above, coef)
+    )(rank, core, below, above, coef)
 
 
 def invert_factor(work_ref):
@@ -181,7 +219,17 @@
 
 def factor_kernel(scale, mid_ref, gram_ref, left_ref, project_ref, work_ref):
     mid = mid_ref[...]
-    cross = exact(gram_ref[...], mid, NN)
+    half = mid.shape[0] // 2
+    upper, lower = mid[:half], mid[half:]
+    side = gram_ref[:half, half:]
+    corner = jnp.concatenate([gram_ref[half:, :half], gram_ref[half:, half:]], axis=0)
+    cross = jnp.concatenate(
+        [
+            exact(gram_ref[:half, :half], upper, NN) + exact(side, lower, NN),
+            exact(side, upper, TN) + exact(corner, lower, NN),
+        ],
+        axis=0,
+    )
     work_ref[...] = exact(mid, cross, TN)
     invert_factor(work_ref)
     row = lax.broadcasted_iota(jnp.int32, work_ref.shape, 0)
@@ -204,6 +252,39 @@
     )(mid_sum, gram_left)
 
 
+def gram_kernel(rows_ref, out_ref):
+    half = rows_ref.shape[1] // 2
+    high, low = halves(rows_ref[...])
+    first = (high[:, :half], low[:, :half])
+    second = (high[:, half:], low[:, half:])
+    top = dot3(first, (high, low), TN)
+    corner = dot3(second, second, TN)
+    corner = jnp.concatenate([corner[: half // 2], corner[half // 2 :]], axis=1)
+    total = jnp.concatenate([top, corner], axis=0)
+
+    @pl.when(pl.program_id(0) == 0)
+    def _():
+        out_ref[...] = total
+
+    @pl.when(pl.program_id(0) > 0)
+    def _():
+        out_ref[...] += total
+
+
+def packed_gram(rows):
+    count, depth = rows.shape
+    group = 512
+    shape = (depth // 2 + depth // 4, depth)
+    return pl.pallas_call(
+        gram_kernel,
+        grid=(count // group,),
+        in_specs=[pl.BlockSpec((group, depth), lambda g: (g, 0))],
+        out_specs=whole_block(shape),
+        out_shape=jax.ShapeDtypeStruct(shape, F32),
+        name="gram",
+    )(rows)
+
+
 def apply_kernel(rows_ref, right_ref, out_ref):
     out_ref[...] = dot3(halves(rows_ref[...]), halves(right_ref[...]), NN)
 
@@ -222,30 +303,44 @@
     )(rows, right)
 
 
-def project_kernel(project_ref, stepped_ref, out_ref):
-    depth, slices, _ = stepped_ref.shape
+def project_kernel(pieces, rank_ref, project_ref, *refs):
+    *stepped_refs, out_ref = refs
+    slices = stepped_refs[0].shape[1]
     rows = project_ref.shape[0]
-    project = halves(project_ref[...])
-    stepped = stepped_ref.reshape(depth * slices, LANES)
+    ranks = len(pieces)
+    project = halves(
+        jnp.concatenate(
+            [project_ref[:, pl.ds(own_block(rank_ref, ranks - distance, ranks), LANES)] for distance in range(ranks)],
+            axis=1,
+        )
+    )
+    stepped = [(ref.reshape(-1, LANES), ref.shape[0]) for ref in stepped_refs]
     out = out_ref.reshape(rows * slices, LANES)
+
+    def slab(i):
+        return jnp.concatenate([ref[pl.ds(i, count, stride=slices), :] for ref, count in stepped], axis=0)
+
     for i in range(0, slices, 2):
-        pair = jnp.concatenate([stepped[pl.ds(i + d, depth, stride=slices), :] for d in range(2)], axis=1)
-        product = dot3(project, halves(pair), NN)
+        product = dot3(project, halves(jnp.concatenate([slab(i), slab(i + 1)], axis=1)), NN)
         for d in range(2):
             out[pl.ds(i + d, rows, stride=slices), :] = product[:, d * LANES : (d + 1) * LANES]
 
 
-def projected(project, stepped):
-    depth, slices, _ = stepped.shape
+def projected(rank, project, stepped, pieces):
+    slices = stepped[0].shape[1]
     rows = project.shape[0]
     return pl.pallas_call(
-        project_kernel,
+        functools.partial(project_kernel, pieces),
         grid=(slices // TILE,),
-        in_specs=[whole_block(project.shape), pl.BlockSpec((depth, TILE, LANES), lambda g: (0, g, 0))],
+        in_specs=[
+            SCALAR,
+            whole_block(project.shape),
+            *[pl.BlockSpec((block.shape[0], TILE, LANES), lambda g: (0, g, 0)) for block in stepped],
+        ],
         out_specs=pl.BlockSpec((rows, TILE, LANES), lambda g: (0, g, 0)),
         out_shape=jax.ShapeDtypeStruct((rows, slices, LANES), F32),
         name="project",
-    )(project, stepped)
+    )(rank, project, *stepped)
 
 
 def summed_lines(partial, axes):
@@ -254,9 +349,18 @@
     return jnp.sum(lax.all_to_all(blocks, axes, 0, 0, tiled=True), axis=0)
 
 
-def whole_of(lines):
-    copies = jnp.broadcast_to(lines, (lax.axis_size(EVERY), *lines.shape))
-    return lax.all_to_all(copies, EVERY, 0, 0, tiled=True).reshape(-1, lines.shape[-1])
+def copies_of(lines, axes):
+    copies = jnp.broadcast_to(lines, (lax.axis_size(axes), *lines.shape))
+    return lax.all_to_all(copies, axes, 0, 0, tiled=True)
+
+
+def whole_of(lines, axes):
+    return copies_of(lines, axes).reshape(-1, lines.shape[-1])
+
+
+def shifted(array, distance):
+    count = lax.axis_size("rank")
+    return lax.ppermute(array, "rank", [(i, (i + distance) % count) for i in range(count)])
 
 
 def neighbours(core):
@@ -267,33 +371,44 @@
     return below, above
 
 
-def shards(core_left, core_mid, core_right, sketch_mid, sketch_right, tail_sketch, stencil):
+def step(core_left, core_mid, core_right, sketch_mid, sketch_right, tail_sketch, stencil):
     row_count, slices, rank_width = core_left.shape
     sketch_width = tail_sketch.shape[1]
     quarters = rank_width // LANES
     ranks = lax.axis_size("rank")
+    flat_left = core_left.reshape(row_count * slices, rank_width)
+
+    rank = lax.axis_index("rank").astype(jnp.int32).reshape(1)
 
     below, above = neighbours(core_mid)
-    right_part = contract_back(core_right[None], tail_sketch, sketch_right)
-    stepped = step_core(core_mid, below, above, stencil)
-    right_sum = whole_of(summed_lines(right_part, CUTS))
-
-    own_cols = lax.all_to_all(stepped, "rank", 0, 0, tiled=True)
-
-    flat_left = core_left.reshape(row_count * slices, rank_width)
-    local_gram = lax.dot_general(flat_left, flat_left, TN, precision=HIGH, preferred_element_type=F32)
-    gram_left = whole_of(summed_lines(local_gram, EVERY))
-
-    mid_sum = whole_of(summed_lines(contract_back(stepped, right_sum, sketch_mid), CUTS))
+    stepped = step_core(rank, core_mid, below, above, stencil, PIECES)
+    own, up, far_up, far_down, down = stepped
+    up = shifted(up, 1)
+    down = shifted(down, -1)
+    far_up = shifted(far_up, 1)
+    far_down = shifted(far_down, -1)
+    far_up = shifted(far_up, 1)
+    far_down = shifted(far_down, -1)
+
+    gram_left = packed_gram(flat_left)
+    gram_left = summed_lines(gram_left, CUTS)
+    gram_left = sum([shifted(gram_left, d) for d in range(1, ranks)], gram_left)
+    gram_left = whole_of(gram_left, CUTS)
+
+    right_part = contract_back(rank, [core_right], (), tail_sketch, sketch_right)
+    right_sum = summed_lines(right_part, CUTS)
+    right_sum = whole_of(right_sum, EVERY)
+
+    mid_part = contract_back(rank, stepped, PIECES, right_sum, sketch_mid)
+    mid_sum = summed_lines(mid_part, CUTS)
+    mid_sum = whole_of(mid_sum, EVERY)
 
     scale = math.sqrt(rank_width * slices * lax.axis_size(CUTS))
     left, project = factored(mid_sum, gram_left, scale)
-
-    product = projected(project, own_cols.reshape(rank_width, slices, LANES))
+    product = projected(rank, project, [own, up, far_up, far_down, down], PIECES)
     blocks = product.reshape(ranks, sketch_width // ranks, slices, LANES)
     arrived = lax.all_to_all(blocks, "rank", 0, 0, tiled=True)
     next_core = jnp.moveaxis(arrived, 0, 2).reshape(sketch_width // ranks, slices, quarters * LANES)
-
     ortho_core = apply_right(flat_left, left).reshape(row_count, slices, sketch_width)
     return ortho_core, next_core
 
@@ -312,6 +427,4 @@
         P(None, CUTS),
     )
     out_specs = (P("rank", CUTS, None), P("rank", CUTS, None))
-    return jax.shard_map(
-        shards, mesh=split, in_specs=in_specs, out_specs=out_specs, check_vma=False
-    )
+    return jax.shard_map(step, mesh=split, in_specs=in_specs, out_specs=out_specs, check_vma=False)

time: 258 us -> 247 us (0.957)
  blocking collectives: 39.8 us -> 16.1 us
  starting transfers between devices: 42.3 us -> 62.6 us
  matrix products: 11.4 us -> 0 us
  local copies, waits for them, and re-layouts: 25.1 us -> 16.4 us
  waiting for transfers between devices: 84.3 us -> 90.1 us
  Pallas kernels: 53.3 us -> 59 us
    ppermute x0 -> x9, waiting for transfers between devices: none -> 35.8 us  [shifted(): lax.ppermute(array, 'rank', [(i, (i + distance) % count) for i in range(c...]
    all_to_all x4, waiting for transfers between devices: 64.9 us -> 34.2 us  [the longest x1 21.7 us: step(): arrived = lax.all_to_all(blocks, 'rank', 0, 0, tiled=True)]
    all_to_all x1 -> x0, blocking collectives: 23.7 us -> none  [whole_of(): lax.all_to_all(copies, EVERY, 0, 0, tiled=True).reshape(-1, lines.shape[-1])]
    ppermute x0 -> x9, starting transfers between devices: none -> 15.3 us  [shifted(): lax.ppermute(array, 'rank', [(i, (i + distance) % count) for i in range(c...]
    dot_general x3 -> x0, local copies, waits for them, and re-layouts: 12.3 us -> none  [shards(): lax.dot_general(flat_left, flat_left, TN, precision=HIGH, preferred_eleme...]
    dot_general x1 -> x0, matrix products: 11.4 us -> none  [shards(): lax.dot_general(flat_left, flat_left, TN, precision=HIGH, preferred_eleme...]
    pallas_call x4 -> x5, Pallas kernels: 33.5 us -> 40.1 us  [the longest x2 21 us: contract_back(): pl.pallas_call(functools.partial(contract_kernel, core_parts), grid=(slic...]
    all_to_all x4, starting transfers between devices: 19.6 us -> 24.3 us  [the longest x3 20.7 us: copies_of(): return lax.all_to_all(copies, axes, 0, 0, tiled=True)]
  transfers between devices with their start and end apart: 8 -> 17, of which waited for: 4 -> 6; matrix products, arithmetic and copies ran while one was open for 12% -> 4% of each run, Pallas kernels for 11% -> 13%
where the time goes in v1:
time: 247 us; the launch traced here: 245 us
  waiting for transfers between devices  90.1 us (36%)
  starting transfers between devices  62.6 us (25%)
  Pallas kernels  59 us (24%)
  local copies, waits for them, and re-layouts  16.4 us (7%)
  blocking collectives  16.1 us (7%)
    ppermute x9, waiting for transfers between devices, shifted(): lax.ppermute(array, 'rank', [(i, (i + distance) % count) for i in range(c...  35.8 us
    all_to_all x1, waiting for transfers between devices, step(): arrived = lax.all_to_all(blocks, 'rank', 0, 0, tiled=True)  21.7 us
    pallas_call x2, Pallas kernels, contract_back(): pl.pallas_call(functools.partial(contract_kernel, core_parts), grid=(slic...  21 us
    all_to_all x3, starting transfers between devices, copies_of(): return lax.all_to_all(copies, axes, 0, 0, tiled=True)  20.7 us
    all_to_all x2, starting transfers between devices, summed_lines(): return jnp.sum(lax.all_to_all(blocks, axes, 0, 0, tiled=True), axis=0)  20.4 us
    all_to_all x2, waiting for transfers between devices, summed_lines(): return jnp.sum(lax.all_to_all(blocks, axes, 0, 0, tiled=True), axis=0)  16.7 us
    all_to_all x1, blocking collectives, summed_lines(): return jnp.sum(lax.all_to_all(blocks, axes, 0, 0, tiled=True), axis=0)  16.1 us
    ppermute x9, starting transfers between devices, shifted(): lax.ppermute(array, 'rank', [(i, (i + distance) % count) for i in range(c...  15.3 us
  transfers between devices with their start and end apart: 17, of which 6 were waited for; matrix products, arithmetic and copies ran while one was open for 4% of the time, Pallas kernels for 13%

profile of v1, /device:TPU:0, one launch (start us, length us, event | category | flops | bytes accessed | tf_op | source)
XLA Modules:
  0.0 245.3 jit_solution(17114195449621637601)
XLA Ops:
  0.6 10.4 %contract.2 = f32[128,256]{1,0:T(8,128)} custom-call(s32[1]{0:T(128)} %bitcast.1.rank_ref, f32[512,256]{1,0:T(8,128)} %part_ref.1, f32[128,16,512]{2,1,0:T(8,128)} %refs_0_.1, f32[256,16,256]{2,1,0:T(8,128)} %refs_2_.1, f32[256,16,256]{2,1,0:T(8,128)} %refs_2_.1), custom_call_target="tpu_custom_call" | custom-call | tf_op jit(solution)/shard_map/contract/pallas_call | solution.py:94
  11.0 0.9 reshape.40
  12.0 0.0 copy-start.5
  12.0 16.1 %all_to_all.35 = f32[32,4,256]{2,1,0:T(4,128)S(1)} all-to-all(f32[32,4,256]{2,1,0:T(4,128)S(1)} %reshape.40), channel_id=1, replica_groups=mesh['cuts_0'=4,'cuts_1'=4,'cuts_2'=2,'rank'=4] {'cuts_0','cuts_1','cuts..., dimensions={0} | all-to-all | bytes 262144 | tf_op jit(solution)/shard_map/all_to_all | solution.py:349
  28.1 0.9 broadcast_in_dim.15
  29.0 6.3 %all-to-all-start.1 = ((f32[128,4,256]{2,1,0:T(4,128)}), f32[128,4,256]{2,1,0:T(4,128)S(1)}, u32[]{:S(2)}, u32[]{:S(2)}) async-start(f32[128,4,256]{2,1,0:T(4,128)} %broadcast_in_dim.15), calls=%async_computation.1 | async-start | bytes 1048576 | tf_op jit(solution)/shard_map/all_to_all | solution.py:354
  35.3 2.7 %fusion = (f32[128,1,512]{2,1,0:T(1,128)S(1)}, f32[128,1,512]{2,1,0:T(1,128)S(1)}) fusion(f32[128,16,512]{2,1,0:T(8,128)} %core_ref.1), kind=kLoop, calls=%fused_computation.4 | loop fusion | bytes 1048576 | tf_op jit(solution)/shard_map/slice | solution.py:368
  38.1 1.4 collective-permute-start
  39.5 1.3 collective-permute-start.1
  40.8 0.0 collective-permute-done.below_ref
  40.8 3.4 %collective-permute-done.1.above_ref = f32[128,512]{1,0:T(8,128)S(1)} collective-permute-done((f32[128,512]{1,0:T(8,128)S(1)}, f32[128,512]{1,0:T(8,128)S(1)}, u32[]{:S(2)}, u32[]{:S(2)}) %collective-permute-start.1) | collective-permute-done | bytes 262176 | tf_op jit(solution)/shard_map/ppermute | solution.py:370
  44.2 0.7 broadcast_in_dim.16.coef_ref
  44.9 7.3 %stencil.1 = (f32[128,16,128]{2,1,0:T(8,128)}, f32[128,16,128]{2,1,0:T(8,128)}, f32[64,16,128]{2,1,0:T(8,128)}, f32[64,16,128]{2,1,0:T(8,128)}, f32[128,16,128]{2,1,0:T(8,128)}) custom-call(s32[1]{0:T(128)} %bitcast.1.rank_ref, f32[128,16,512]{2,1,0:T(8,128)} %core_ref.1, f32[128,512]{1,0:T(8,128)} %copy-done.3, f32[128,512]{1,0:T(8,128)} %copy-done.4, ...), custom_call_target="tpu_custom_call" | custom-call | tf_op jit(solution)/shard_map/stencil/pallas_call | solution.py:149
  52.2 1.0 reshape.41.part_ref
  53.2 10.6 %contract.3 = f32[128,256]{1,0:T(8,128)} custom-call(s32[1]{0:T(128)} %bitcast.1.rank_ref, f32[512,256]{1,0:T(8,128)} %reshape.41.part_ref, f32[128,16,128]{2,1,0:T(8,128)} %get-tuple-element.9.refs_0_, f32[128,16,128]{2,1,0:T(8,128)} %get-tuple-element.10.refs_1_, f32[64,16,128]{2,1,0:T(8,128)} %get-tuple-element.11.refs_2_, ...), custom_call_target="tpu_custom_call" | custom-call | tf_op jit(solution)/shard_map/contract/pallas_call | solution.py:94
  63.8 1.6 reshape.42
  65.4 12.9 %all-to-all-start.2 = ((f32[32,4,256]{2,1,0:T(4,128)}), f32[32,4,256]{2,1,0:T(4,128)S(1)}, u32[]{:S(2)}, u32[]{:S(2)}) async-start(f32[32,4,256]{2,1,0:T(4,128)} %reshape.42), calls=%async_computation.2 | async-start | bytes 262144 | tf_op jit(solution)/shard_map/all_to_all | solution.py:349
  78.3 6.2 %gram.1 = f32[384,512]{1,0:T(8,128)} custom-call(f32[2048,512]{1,0:T(8,128)} %bitcast.16), custom_call_target="tpu_custom_call" | custom-call | tf_op jit(solution)/shard_map/gram/pallas_call | solution.py:278
  84.4 2.2 reshape.44
  86.7 7.5 %all-to-all-start.4 = ((f32[32,12,512]{2,1,0:T(8,128)}), f32[32,12,512]{2,1,0:T(8,128)S(1)}, u32[]{:S(2)}, u32[]{:S(2)}) async-start(f32[32,12,512]{2,1,0:T(8,128)} %reshape.44), calls=%async_computation.4 | async-start | bytes 2097152 | tf_op jit(solution)/shard_map/all_to_all | solution.py:349
  94.2 16.7 %all-to-all-done.4 = f32[32,12,512]{2,1,0:T(8,128)S(1)} async-done(((f32[32,12,512]{2,1,0:T(8,128)}), f32[32,12,512]{2,1,0:T(8,128)S(1)}, u32[]{:S(2)}, u32[]{:S(2)}) %all-to-all-start.4) | async-done | bytes 786464 | tf_op jit(solution)/shard_map/all_to_all | solution.py:349
  111.0 0.9 broadcast_in_dim.17
  111.8 6.8 %all-to-all-start.3 = ((f32[128,4,256]{2,1,0:T(4,128)}), f32[128,4,256]{2,1,0:T(4,128)S(1)}, u32[]{:S(2)}, u32[]{:S(2)}) async-start(f32[128,4,256]{2,1,0:T(4,128)} %broadcast_in_dim.17), calls=%async_computation.3 | async-start | bytes 1048576 | tf_op jit(solution)/shard_map/all_to_all | solution.py:354
  118.6 0.1 reduce_sum.29
  118.7 2.2 collective-permute-start.4
  120.9 0.0 collective-permute-start.6
  120.9 3.2 %collective-permute-start.8 = (f32[64,16,128]{2,1,0:T(8,128)S(1)}, f32[64,16,128]{2,1,0:T(8,128)}, u32[]{:S(2)}, u32[]{:S(2)}) collective-permute-start(f32[64,16,128]{2,1,0:T(8,128)S(1)} %copy-done.1), channel_id=1, source_target_pairs={{0,3},{1,0},{2,1},{3,2},{4,7},{5,4},{6,5},{7,6},{8,11},{9,8},{10,9... | collective-permute-start | bytes 1572872 | tf_op jit(solution)/shard_map/ppermute | solution.py:363
  124.1 0.0 collective-permute-start.5
  124.1 3.2 %collective-permute-start.10 = (f32[128,16,128]{2,1,0:T(8,128)S(1)}, f32[128,16,128]{2,1,0:T(8,128)}, u32[]{:S(2)}, u32[]{:S(2)}) collective-permute-start(f32[128,16,128]{2,1,0:T(8,128)S(1)} %copy-done), channel_id=1, source_target_pairs={{0,3},{1,0},{2,1},{3,2},{4,7},{5,4},{6,5},{7,6},{8,11},{9,8},{10,9... | collective-permute-start | bytes 3145736 | tf_op jit(solution)/shard_map/ppermute | solution.py:363
  127.4 2.0 collective-permute-start.3
  129.4 32.0 %collective-permute-done.3 = f32[12,512]{1,0:T(8,128)S(1)} collective-permute-done((f32[12,512]{1,0:T(8,128)S(1)}, f32[12,512]{1,0:T(8,128)S(1)}, u32[]{:S(2)}, u32[]{:S(2)}) %collective-permute-start.3) | collective-permute-done | bytes 24608 | tf_op jit(solution)/shard_map/ppermute | solution.py:363
  161.4 1.3 collective-permute-start.2
  162.6 3.9 %collective-permute-done.2 = f32[12,512]{1,0:T(8,128)S(1)} collective-permute-done((f32[12,512]{1,0:T(8,128)S(1)}, f32[12,512]{1,0:T(8,128)S(1)}, u32[]{:S(2)}, u32[]{:S(2)}) %collective-permute-start.2) | collective-permute-done | bytes 24608 | tf_op jit(solution)/shard_map/ppermute | solution.py:363
  166.5 0.0 all-to-all-done.3
  166.5 1.1 broadcast_in_dim.18
  167.6 7.6 %all-to-all-start.5 = ((f32[32,12,512]{2,1,0:T(8,128)}), f32[32,12,512]{2,1,0:T(8,128)S(1)}, u32[]{:S(2)}, u32[]{:S(2)}) async-start(f32[32,12,512]{2,1,0:T(8,128)} %broadcast_in_dim.18), calls=%async_computation.5 | async-start | bytes 2097152 | tf_op jit(solution)/shard_map/all_to_all | solution.py:354
  175.3 0.1 collective-permute-start.7
  175.4 3.2 %collective-permute-start.9 = (f32[64,16,128]{2,1,0:T(8,128)}, f32[64,16,128]{2,1,0:T(8,128)S(1)}, u32[]{:S(2)}, u32[]{:S(2)}) collective-permute-start(f32[64,16,128]{2,1,0:T(8,128)} %collective-permute-done.8), channel_id=1, source_target_pairs={{0,3},{1,0},{2,1},{3,2},{4,7},{5,4},{6,5},{7,6},{8,11},{9,8},{10,9... | collective-permute-start | bytes 1572872 | tf_op jit(solution)/shard_map/ppermute | solution.py:363
  178.6 1.0 reshape.43.mid_ref
  179.6 12.5 %all-to-all-done.5 = f32[32,12,512]{2,1,0:T(8,128)S(1)} async-done(((f32[32,12,512]{2,1,0:T(8,128)}), f32[32,12,512]{2,1,0:T(8,128)S(1)}, u32[]{:S(2)}, u32[]{:S(2)}) %all-to-all-start.5) | async-done | bytes 786464 | tf_op jit(solution)/shard_map/all_to_all | solution.py:354
  192.0 1.0 reshape.45.gram_ref
  193.0 13.6 %factor.1 = (f32[512,256]{1,0:T(8,128)}, f32[256,512]{1,0:T(8,128)}) custom-call(f32[512,256]{1,0:T(8,128)} %reshape.43.mid_ref, f32[384,512]{1,0:T(8,128)} %reshape.45.gram_ref), custom_call_target="tpu_custom_call" | custom-call | tf_op jit(solution)/shard_map/factor/pallas_call | solution.py:244
  206.6 0.8 copy-done.2
  207.4 5.6 %project.1 = f32[256,16,128]{2,1,0:T(8,128)} custom-call(s32[1]{0:T(128)} %bitcast.1.rank_ref, f32[256,512]{1,0:T(8,128)} %get-tuple-element.15.project_ref, f32[128,16,128]{2,1,0:T(8,128)} %get-tuple-element.9.refs_0_, f32[128,16,128]{2,1,0:T(8,128)} %collective-permute-done.5.refs_1_, f32[64,16,128]{2,1,0:T(8,128)} %collective-permute-done.7.refs_2_, ...), custom_call_target="tpu_custom_call" | custom-call | tf_op jit(solution)/shard_map/project/pallas_call | solution.py:332
  212.9 3.6 %all-to-all-start.6 = ((f32[4,64,16,128]{3,2,1,0:T(8,128)}), f32[4,64,16,128]{3,2,1,0:T(8,128)S(1)}, u32[]{:S(2)}, u32[]{:S(2)}) async-start(f32[4,64,16,128]{3,2,1,0:T(8,128)} %bitcast.18), calls=%async_computation.6 | async-start | bytes 4194304 | tf_op jit(solution)/shard_map/all_to_all | solution.py:410
  216.6 5.4 %ortho.1 = f32[2048,256]{1,0:T(8,128)} custom-call(f32[2048,512]{1,0:T(8,128)} %bitcast.17, f32[512,256]{1,0:T(8,128)} %get-tuple-element.14.right_ref), custom_call_target="tpu_custom_call" | custom-call | tf_op jit(solution)/shard_map/ortho/pallas_call | solution.py:296
  222.0 21.7 %all-to-all-done.6 = f32[4,64,16,128]{3,2,1,0:T(8,128)S(1)} async-done(((f32[4,64,16,128]{3,2,1,0:T(8,128)}), f32[4,64,16,128]{3,2,1,0:T(8,128)S(1)}, u32[]{:S(2)}, u32[]{:S(2)}) %all-to-all-start.6) | async-done | bytes 2097184 | tf_op jit(solution)/shard_map/all_to_all | solution.py:410
  243.7 1.6 copy_bitcast_fusion
  (24 shorter events, 0.2 us)
Async XLA Ops:
  12.0 32.2 %copy-start.5 = (f32[3,16]{1,0:T(4,128)S(1)}, f32[3,16]{1,0:T(4,128)}, u32[]{:S(2)}) copy-start(f32[3,16]{1,0:T(4,128)} %param.13) | copy-start | bytes 580
  29.0 23.2 %all-to-all-start.1 = ((f32[128,4,256]{2,1,0:T(4,128)}), f32[128,4,256]{2,1,0:T(4,128)S(1)}, u32[]{:S(2)}, u32[]{:S(2)}) async-start(f32[128,4,256]{2,1,0:T(4,128)} %broadcast_in_dim.15), calls=%async_computation.1 | async-start | bytes 1048576 | tf_op jit(solution)/shard_map/all_to_all | solution.py:354
  38.1 2.7 %collective-permute-start = (f32[128,512]{1,0:T(8,128)S(1)}, f32[128,512]{1,0:T(8,128)S(1)}, u32[]{:S(2)}, u32[]{:S(2)}) collective-permute-start(f32[128,512]{1,0:T(8,128)S(1)} %bitcast.20), channel_id=1, source_target_pairs={{0,4},{4,8},{8,12},{12,16},{16,20},{20,24},{24,28},{28,32},{32,36}... | collective-permute-start | bytes 786440 | tf_op jit(solution)/shard_map/ppermute | solution.py:369
  39.5 4.7 %collective-permute-start.1 = (f32[128,512]{1,0:T(8,128)S(1)}, f32[128,512]{1,0:T(8,128)S(1)}, u32[]{:S(2)}, u32[]{:S(2)}) collective-permute-start(f32[128,512]{1,0:T(8,128)S(1)} %bitcast.21), channel_id=1, source_target_pairs={{4,0},{8,4},{12,8},{16,12},{20,16},{24,20},{28,24},{32,28},{36,32}... | collective-permute-start | bytes 786440 | tf_op jit(solution)/shard_map/ppermute | solution.py:370
  40.8 4.1 %copy-start.3 = (f32[128,512]{1,0:T(8,128)}, f32[128,512]{1,0:T(8,128)S(1)}, u32[]{:S(2)}) copy-start(f32[128,512]{1,0:T(8,128)S(1)} %collective-permute-done.below_ref) | copy-start | bytes 786436
  44.2 0.7 copy-start.4
  65.4 21.2 %all-to-all-start.2 = ((f32[32,4,256]{2,1,0:T(4,128)}), f32[32,4,256]{2,1,0:T(4,128)S(1)}, u32[]{:S(2)}, u32[]{:S(2)}) async-start(f32[32,4,256]{2,1,0:T(4,128)} %reshape.42), calls=%async_computation.2 | async-start | bytes 262144 | tf_op jit(solution)/shard_map/all_to_all | solution.py:349
  86.6 34.3 %copy-start.1 = (f32[64,16,128]{2,1,0:T(8,128)S(1)}, f32[64,16,128]{2,1,0:T(8,128)}, u32[]{:S(2)}) copy-start(f32[64,16,128]{2,1,0:T(8,128)} %get-tuple-element.12.refs_3_) | copy-start | bytes 1572868
  86.6 37.5 %copy-start = (f32[128,16,128]{2,1,0:T(8,128)S(1)}, f32[128,16,128]{2,1,0:T(8,128)}, u32[]{:S(2)}) copy-start(f32[128,16,128]{2,1,0:T(8,128)} %get-tuple-element.13.refs_4_) | copy-start | bytes 3145732
  86.7 24.3 %all-to-all-start.4 = ((f32[32,12,512]{2,1,0:T(8,128)}), f32[32,12,512]{2,1,0:T(8,128)S(1)}, u32[]{:S(2)}, u32[]{:S(2)}) async-start(f32[32,12,512]{2,1,0:T(8,128)} %reshape.44), calls=%async_computation.4 | async-start | bytes 2097152 | tf_op jit(solution)/shard_map/all_to_all | solution.py:349
  111.8 54.7 %all-to-all-start.3 = ((f32[128,4,256]{2,1,0:T(4,128)}), f32[128,4,256]{2,1,0:T(4,128)S(1)}, u32[]{:S(2)}, u32[]{:S(2)}) async-start(f32[128,4,256]{2,1,0:T(4,128)} %broadcast_in_dim.17), calls=%async_computation.3 | async-start | bytes 1048576 | tf_op jit(solution)/shard_map/all_to_all | solution.py:354
  118.7 8.7 %collective-permute-start.4 = (f32[12,512]{1,0:T(8,128)S(1)}, f32[12,512]{1,0:T(8,128)S(1)}, u32[]{:S(2)}, u32[]{:S(2)}) collective-permute-start(f32[12,512]{1,0:T(8,128)S(1)} %reduce_sum.29), channel_id=1, source_target_pairs={{0,3},{1,0},{2,1},{3,2},{4,7},{5,4},{6,5},{7,6},{8,11},{9,8},{10,9... | collective-permute-start | bytes 73736 | tf_op jit(solution)/shard_map/ppermute | solution.py:363
  120.9 54.3 %collective-permute-start.6 = (f32[64,16,128]{2,1,0:T(8,128)}, f32[64,16,128]{2,1,0:T(8,128)}, u32[]{:S(2)}, u32[]{:S(2)}) collective-permute-start(f32[64,16,128]{2,1,0:T(8,128)} %get-tuple-element.11.refs_2_), channel_id=1, source_target_pairs={{0,1},{1,2},{2,3},{3,0},{4,5},{5,6},{6,7},{7,4},{8,9},{9,10},{10,1... | collective-permute-start | bytes 1572872 | tf_op jit(solution)/shard_map/ppermute | solution.py:363
  120.9 54.5 %collective-permute-start.8 = (f32[64,16,128]{2,1,0:T(8,128)S(1)}, f32[64,16,128]{2,1,0:T(8,128)}, u32[]{:S(2)}, u32[]{:S(2)}) collective-permute-start(f32[64,16,128]{2,1,0:T(8,128)S(1)} %copy-done.1), channel_id=1, source_target_pairs={{0,3},{1,0},{2,1},{3,2},{4,7},{5,4},{6,5},{7,6},{8,11},{9,8},{10,9... | collective-permute-start | bytes 1572872 | tf_op jit(solution)/shard_map/ppermute | solution.py:363
  124.1 82.4 %collective-permute-start.5 = (f32[128,16,128]{2,1,0:T(8,128)}, f32[128,16,128]{2,1,0:T(8,128)}, u32[]{:S(2)}, u32[]{:S(2)}) collective-permute-start(f32[128,16,128]{2,1,0:T(8,128)} %get-tuple-element.10.refs_1_), channel_id=1, source_target_pairs={{0,1},{1,2},{2,3},{3,0},{4,5},{5,6},{6,7},{7,4},{8,9},{9,10},{10,1... | collective-permute-start | bytes 3145736 | tf_op jit(solution)/shard_map/ppermute | solution.py:363
  124.1 82.4 %collective-permute-start.10 = (f32[128,16,128]{2,1,0:T(8,128)S(1)}, f32[128,16,128]{2,1,0:T(8,128)}, u32[]{:S(2)}, u32[]{:S(2)}) collective-permute-start(f32[128,16,128]{2,1,0:T(8,128)S(1)} %copy-done), channel_id=1, source_target_pairs={{0,3},{1,0},{2,1},{3,2},{4,7},{5,4},{6,5},{7,6},{8,11},{9,8},{10,9... | collective-permute-start | bytes 3145736 | tf_op jit(solution)/shard_map/ppermute | solution.py:363
  127.4 34.0 %collective-permute-start.3 = (f32[12,512]{1,0:T(8,128)S(1)}, f32[12,512]{1,0:T(8,128)S(1)}, u32[]{:S(2)}, u32[]{:S(2)}) collective-permute-start(f32[12,512]{1,0:T(8,128)S(1)} %reduce_sum.29), channel_id=1, source_target_pairs={{0,2},{1,3},{2,0},{3,1},{4,6},{5,7},{6,4},{7,5},{8,10},{9,11},{10,... | collective-permute-start | bytes 73736 | tf_op jit(solution)/shard_map/ppermute | solution.py:363
  161.4 5.1 %collective-permute-start.2 = (f32[12,512]{1,0:T(8,128)S(1)}, f32[12,512]{1,0:T(8,128)S(1)}, u32[]{:S(2)}, u32[]{:S(2)}) collective-permute-start(f32[12,512]{1,0:T(8,128)S(1)} %reduce_sum.29), channel_id=1, source_target_pairs={{0,1},{1,2},{2,3},{3,0},{4,5},{5,6},{6,7},{7,4},{8,9},{9,10},{10,1... | collective-permute-start | bytes 73736 | tf_op jit(solution)/shard_map/ppermute | solution.py:363
  167.6 24.4 %all-to-all-start.5 = ((f32[32,12,512]{2,1,0:T(8,128)}), f32[32,12,512]{2,1,0:T(8,128)S(1)}, u32[]{:S(2)}, u32[]{:S(2)}) async-start(f32[32,12,512]{2,1,0:T(8,128)} %broadcast_in_dim.18), calls=%async_computation.5 | async-start | bytes 2097152 | tf_op jit(solution)/shard_map/all_to_all | solution.py:354
  175.3 31.3 %collective-permute-start.7 = (f32[64,16,128]{2,1,0:T(8,128)}, f32[64,16,128]{2,1,0:T(8,128)}, u32[]{:S(2)}, u32[]{:S(2)}) collective-permute-start(f32[64,16,128]{2,1,0:T(8,128)} %collective-permute-done.6), channel_id=1, source_target_pairs={{0,1},{1,2},{2,3},{3,0},{4,5},{5,6},{6,7},{7,4},{8,9},{9,10},{10,1... | collective-permute-start | bytes 1572872 | tf_op jit(solution)/shard_map/ppermute | solution.py:363
  175.4 31.2 %collective-permute-start.9 = (f32[64,16,128]{2,1,0:T(8,128)}, f32[64,16,128]{2,1,0:T(8,128)S(1)}, u32[]{:S(2)}, u32[]{:S(2)}) collective-permute-start(f32[64,16,128]{2,1,0:T(8,128)} %collective-permute-done.8), channel_id=1, source_target_pairs={{0,3},{1,0},{2,1},{3,2},{4,7},{5,4},{6,5},{7,6},{8,11},{9,8},{10,9... | collective-permute-start | bytes 1572872 | tf_op jit(solution)/shard_map/ppermute | solution.py:363
  206.6 0.8 copy-start.2
  212.9 30.7 %all-to-all-start.6 = ((f32[4,64,16,128]{3,2,1,0:T(8,128)}), f32[4,64,16,128]{3,2,1,0:T(8,128)S(1)}, u32[]{:S(2)}, u32[]{:S(2)}) async-start(f32[4,64,16,128]{3,2,1,0:T(8,128)} %bitcast.18), calls=%async_computation.6 | async-start | bytes 4194304 | tf_op jit(solution)/shard_map/all_to_all | solution.py:410

commit v2 on v1

--- a/solution.py
+++ b/solution.py
@@ -47,9 +47,35 @@
     return pl.multiple_of(lax.rem(rank_ref[0] + distance, ranks) * LANES, LANES)
 
 
+def spread(out_ref, total):
+    peers, height, _ = out_ref.shape
+    out = out_ref.reshape(peers * height, LANES)
+    lines = total.shape[0] // peers
+    for h in range(total.shape[1] // LANES):
+        for j in range(lines):
+            block = total[j * peers : (j + 1) * peers, h * LANES : (h + 1) * LANES]
+            out[pl.ds(h * lines + j, peers, stride=height), :] = block
+
+
+def gathered(ref, peers, lines, first=0):
+    count, height, _ = ref.shape
+    flat = ref.reshape(count * height, LANES)
+    return jnp.concatenate(
+        [
+            jnp.concatenate(
+                [flat[pl.ds(first * height + h * lines + j, peers, stride=height), :] for h in range(height // lines)],
+                axis=1,
+            )
+            for j in range(lines)
+        ],
+        axis=0,
+    )
+
+
 def contract_kernel(core_parts, rank_ref, part_ref, *refs):
     count = sum(core_parts) if core_parts else 1
-    core_refs, (*sketch_refs, out_ref, applied_ref) = list(refs[:count]), refs[count:]
+    core_refs, (*sketch_refs, out_ref, applied_ref, sum_ref) = list(refs[:count]), refs[count:]
+    peers = out_ref.shape[0]
     slices = core_refs[0].shape[1]
     if not core_parts:
         core = core_refs[0][...].reshape(-1, core_refs[0].shape[2])
@@ -59,7 +85,8 @@
         for distance, pieces in enumerate(core_parts):
             taken = [core_refs.pop(0)[...].reshape(-1, LANES) for _ in range(pieces)]
             blocks.append(taken[0] if pieces == 1 else jnp.concatenate(taken, axis=0))
-            lines.append(part_ref[pl.ds(own_block(rank_ref, distance, len(core_parts)), LANES), :])
+            block = lax.rem(rank_ref[0] + distance, len(core_parts))
+            lines.append(gathered(part_ref, peers, LANES // peers, block * peers))
         core, part = jnp.concatenate(blocks, axis=1), jnp.concatenate(lines, axis=0)
     rows = core.shape[0] // slices
     applied = dot3(halves(core), halves(part), NN)
@@ -74,13 +101,19 @@
         term = dot3(halves(jnp.concatenate(left, axis=1)), halves(jnp.concatenate(right, axis=1)), NT)
         total = term if total is None else total + term
 
+    last = pl.num_programs(0) - 1
+
     @pl.when(pl.program_id(0) == 0)
     def _():
-        out_ref[...] = total
-
-    @pl.when(pl.program_id(0) > 0)
-    def _():
-        out_ref[...] += total
+        sum_ref[...] = total
+
+    @pl.when((pl.program_id(0) > 0) & (pl.program_id(0) < last))
+    def _():
+        sum_ref[...] += total
+
+    @pl.when(pl.program_id(0) == last)
+    def _():
+        spread(out_ref, sum_ref[...] + total)
 
 
 SCALAR = pl.BlockSpec(memory_space=pltpu.SMEM)
@@ -91,6 +124,8 @@
     sketch_rows, _, sketch_cols = sketch.shape
     rows = sum(core.shape[0] for core in cores[: core_parts[0] if core_parts else 1])
     pieces = sketch_cols // LANES
+    peers = lax.axis_size(CUTS)
+    shape = (peers, rows * sketch_rows // LANES // peers, LANES)
     return pl.pallas_call(
         functools.partial(contract_kernel, core_parts),
         grid=(slices // TILE,),
@@ -100,9 +135,9 @@
             *[pl.BlockSpec((core.shape[0], TILE, core.shape[2]), lambda g: (0, g, 0)) for core in cores],
             *[pl.BlockSpec((sketch_rows, TILE, LANES), lambda g, h=h: (0, g, h)) for h in range(pieces)],
         ],
-        out_specs=whole_block((rows, sketch_rows)),
-        out_shape=jax.ShapeDtypeStruct((rows, sketch_rows), F32),
-        scratch_shapes=[pltpu.VMEM((pieces, rows * TILE, LANES), F32)],
+        out_specs=whole_block(shape),
+        out_shape=jax.ShapeDtypeStruct(shape, F32),
+        scratch_shapes=[pltpu.VMEM((pieces, rows * TILE, LANES), F32), pltpu.VMEM((rows, sketch_rows), F32)],
         name="contract",
     )(rank, part, *cores, *[sketch] * pieces)
 
@@ -218,7 +253,12 @@
 
 
 def factor_kernel(scale, mid_ref, gram_ref, left_ref, project_ref, work_ref):
-    mid = mid_ref[...]
+    peers, height, _ = gram_ref.shape
+    rank_width = left_ref.shape[0]
+    ranks = mid_ref.shape[0] // peers
+    lines = rank_width // ranks // peers
+    mid = jnp.concatenate([gathered(mid_ref, peers, lines, r * peers) for r in range(ranks)], axis=0)
+    gram_ref = gathered(gram_ref, peers, height * LANES // rank_width)
     half = mid.shape[0] // 2
     upper, lower = mid[:half], mid[half:]
     side = gram_ref[:half, half:]
@@ -239,8 +279,8 @@
     project_ref[...] = exact(inverse, cross, NT)
 
 
-def factored(mid_sum, gram_left, scale):
-    rank_width, sketch_width = mid_sum.shape
+def factored(mid_sum, gram_left, scale, rank_width):
+    sketch_width = mid_sum.size // rank_width
     return pl.pallas_call(
         functools.partial(factor_kernel, scale),
         out_shape=(
@@ -252,7 +292,7 @@
     )(mid_sum, gram_left)
 
 
-def gram_kernel(rows_ref, out_ref):
+def gram_kernel(rows_ref, out_ref, sum_ref):
     half = rows_ref.shape[1] // 2
     high, low = halves(rows_ref[...])
     first = (high[:, :half], low[:, :half])
@@ -261,26 +301,34 @@
     corner = dot3(second, second, TN)
     corner = jnp.concatenate([corner[: half // 2], corner[half // 2 :]], axis=1)
     total = jnp.concatenate([top, corner], axis=0)
+    last = pl.num_programs(0) - 1
 
     @pl.when(pl.program_id(0) == 0)
     def _():
-        out_ref[...] = total
-
-    @pl.when(pl.program_id(0) > 0)
-    def _():
-        out_ref[...] += total
+        sum_ref[...] = total
+
+    @pl.when((pl.program_id(0) > 0) & (pl.program_id(0) < last))
+    def _():
+        sum_ref[...] += total
+
+    @pl.when(pl.program_id(0) == last)
+    def _():
+        spread(out_ref, sum_ref[...] + total)
 
 
 def packed_gram(rows):
     count, depth = rows.shape
     group = 512
-    shape = (depth // 2 + depth // 4, depth)
+    sums = (depth // 2 + depth // 4, depth)
+    peers = lax.axis_size(CUTS)
+    shape = (peers, sums[0] * sums[1] // LANES // peers, LANES)
     return pl.pallas_call(
         gram_kernel,
         grid=(count // group,),
         in_specs=[pl.BlockSpec((group, depth), lambda g: (g, 0))],
         out_specs=whole_block(shape),
         out_shape=jax.ShapeDtypeStruct(shape, F32),
+        scratch_shapes=[pltpu.VMEM(sums, F32)],
         name="gram",
     )(rows)
 
@@ -343,19 +391,13 @@
     )(rank, project, *stepped)
 
 
-def summed_lines(partial, axes):
-    peers = lax.axis_size(axes)
-    blocks = partial.reshape(peers, -1, partial.shape[-1])
-    return jnp.sum(lax.all_to_all(blocks, axes, 0, 0, tiled=True), axis=0)
-
-
-def copies_of(lines, axes):
-    copies = jnp.broadcast_to(lines, (lax.axis_size(axes), *lines.shape))
+def summed(pieces, axes):
+    return jnp.sum(lax.all_to_all(pieces, axes, 0, 0, tiled=True), axis=0)
+
+
+def copies_of(piece, axes):
+    copies = jnp.broadcast_to(piece, (lax.axis_size(axes), *piece.shape))
     return lax.all_to_all(copies, axes, 0, 0, tiled=True)
-
-
-def whole_of(lines, axes):
-    return copies_of(lines, axes).reshape(-1, lines.shape[-1])
 
 
 def shifted(array, distance):
@@ -391,20 +433,20 @@
     far_down = shifted(far_down, -1)
 
     gram_left = packed_gram(flat_left)
-    gram_left = summed_lines(gram_left, CUTS)
+    gram_left = summed(gram_left, CUTS)
     gram_left = sum([shifted(gram_left, d) for d in range(1, ranks)], gram_left)
-    gram_left = whole_of(gram_left, CUTS)
+    gram_left = copies_of(gram_left, CUTS)
 
     right_part = contract_back(rank, [core_right], (), tail_sketch, sketch_right)
-    right_sum = summed_lines(right_part, CUTS)
-    right_sum = whole_of(right_sum, EVERY)
+    right_sum = summed(right_part, CUTS)
+    right_sum = copies_of(right_sum, EVERY)
 
     mid_part = contract_back(rank, stepped, PIECES, right_sum, sketch_mid)
-    mid_sum = summed_lines(mid_part, CUTS)
-    mid_sum = whole_of(mid_sum, EVERY)
+    mid_sum = summed(mid_part, CUTS)
+    mid_sum = copies_of(mid_sum, EVERY)
 
     scale = math.sqrt(rank_width * slices * lax.axis_size(CUTS))
-    left, project = factored(mid_sum, gram_left, scale)
+    left, project = factored(mid_sum, gram_left, scale, rank_width)
     product = projected(rank, project, [own, up, far_up, far_down, down], PIECES)
     blocks = product.reshape(ranks, sketch_width // ranks, slices, LANES)
     arrived = lax.all_to_all(blocks, "rank", 0, 0, tiled=True)

time: 247 us -> 236 us (0.955)
  local copies, waits for them, and re-layouts: 16.4 us -> 9.46 us
  waiting for transfers between devices: 90.1 us -> 87 us
    reshape x6 -> x0, local copies, waits for them, and re-layouts: 7.7 us -> none  [the longest x3 4.75 us: summed_lines(): blocks = partial.reshape(peers, -1, partial.shape[-1])]
  transfers between devices with their start and end apart: 17 -> 17, of which waited for: 6 -> 7; matrix products, arithmetic and copies ran while one was open for 4% -> 2% of each run, Pallas kernels for 13% -> 14%
where the time goes in v2:
time: 236 us; the launch traced here: 234 us
  waiting for transfers between devices  87 us (37%)
  starting transfers between devices  61 us (26%)
  Pallas kernels  59.6 us (25%)
  blocking collectives  16.4 us (7%)
  local copies, waits for them, and re-layouts  9.46 us (4%)
    ppermute x9, waiting for transfers between devices, shifted(): lax.ppermute(array, 'rank', [(i, (i + distance) % count) for i in range(c...  35.9 us
    all_to_all x1, waiting for transfers between devices, step(): arrived = lax.all_to_all(blocks, 'rank', 0, 0, tiled=True)  21.9 us
    pallas_call x2, Pallas kernels, contract_back(): pl.pallas_call(functools.partial(contract_kernel, core_parts), grid=(slic...  21.1 us
    all_to_all x3, starting transfers between devices, copies_of(): return lax.all_to_all(copies, axes, 0, 0, tiled=True)  20.8 us
    all_to_all x2, starting transfers between devices, summed(): return jnp.sum(lax.all_to_all(pieces, axes, 0, 0, tiled=True), axis=0)  19 us
    all_to_all x1, blocking collectives, summed(): return jnp.sum(lax.all_to_all(pieces, axes, 0, 0, tiled=True), axis=0)  16.4 us
    all_to_all x2, waiting for transfers between devices, summed(): return jnp.sum(lax.all_to_all(pieces, axes, 0, 0, tiled=True), axis=0)  15.2 us
    ppermute x9, starting transfers between devices, shifted(): lax.ppermute(array, 'rank', [(i, (i + distance) % count) for i in range(c...  15 us
  transfers between devices with their start and end apart: 17, of which 7 were waited for; matrix products, arithmetic and copies ran while one was open for 2% of the time, Pallas kernels for 14%

profile of v2, /device:TPU:0, one launch (start us, length us, event | category | flops | bytes accessed | tf_op | source)
XLA Modules:
  0.0 234.5 jit_solution(16918422089896641786)
XLA Ops:
  0.6 10.4 %contract.2 = f32[32,8,128]{2,1,0:T(8,128)} custom-call(s32[1]{0:T(128)} %bitcast.1.rank_ref, f32[512,256]{1,0:T(8,128)} %part_ref.1, f32[128,16,512]{2,1,0:T(8,128)} %refs_0_.1, f32[256,16,256]{2,1,0:T(8,128)} %refs_2_.1, f32[256,16,256]{2,1,0:T(8,128)} %refs_2_.1), custom_call_target="tpu_custom_call" | custom-call | tf_op jit(solution)/shard_map/contract/pallas_call | solution.py:129
  11.0 16.4 %all_to_all.35 = f32[32,8,128]{2,1,0:T(8,128)S(1)} all-to-all(f32[32,8,128]{2,1,0:T(8,128)} %contract.2), channel_id=1, replica_groups=mesh['cuts_0'=4,'cuts_1'=4,'cuts_2'=2,'rank'=4] {'cuts_0','cuts_1','cuts..., dimensions={0} | all-to-all | bytes 262144 | tf_op jit(solution)/shard_map/all_to_all | solution.py:395
  27.5 0.8 broadcast_in_dim.15
  28.3 6.3 %all-to-all-start.1 = ((f32[128,8,128]{2,1,0:T(8,128)}), f32[128,8,128]{2,1,0:T(8,128)S(1)}, u32[]{:S(2)}, u32[]{:S(2)}) async-start(f32[128,8,128]{2,1,0:T(8,128)} %broadcast_in_dim.15), calls=%async_computation.1 | async-start | bytes 1048576 | tf_op jit(solution)/shard_map/all_to_all | solution.py:400
  34.7 2.7 %fusion = (f32[128,1,512]{2,1,0:T(1,128)S(1)}, f32[128,1,512]{2,1,0:T(1,128)S(1)}) fusion(f32[128,16,512]{2,1,0:T(8,128)} %core_ref.1), kind=kLoop, calls=%fused_computation.4 | loop fusion | bytes 1048576 | tf_op jit(solution)/shard_map/slice | solution.py:410
  37.4 1.4 collective-permute-start
  38.8 1.3 collective-permute-start.1
  40.1 0.0 collective-permute-done.below_ref
  40.2 3.4 %collective-permute-done.1.above_ref = f32[128,512]{1,0:T(8,128)S(1)} collective-permute-done((f32[128,512]{1,0:T(8,128)S(1)}, f32[128,512]{1,0:T(8,128)S(1)}, u32[]{:S(2)}, u32[]{:S(2)}) %collective-permute-start.1) | collective-permute-done | bytes 262176 | tf_op jit(solution)/shard_map/ppermute | solution.py:412
  43.5 0.7 broadcast_in_dim.16.coef_ref
  44.2 7.3 %stencil.1 = (f32[128,16,128]{2,1,0:T(8,128)}, f32[128,16,128]{2,1,0:T(8,128)}, f32[64,16,128]{2,1,0:T(8,128)}, f32[64,16,128]{2,1,0:T(8,128)}, f32[128,16,128]{2,1,0:T(8,128)}) custom-call(s32[1]{0:T(128)} %bitcast.1.rank_ref, f32[128,16,512]{2,1,0:T(8,128)} %core_ref.1, f32[128,512]{1,0:T(8,128)} %copy-done.5, f32[128,512]{1,0:T(8,128)} %copy-done.6, ...), custom_call_target="tpu_custom_call" | custom-call | tf_op jit(solution)/shard_map/stencil/pallas_call | solution.py:184
  51.5 0.0 all-to-all-done.1.part_ref
  51.5 0.8 copy-done.1
  52.3 10.7 %contract.3 = f32[32,8,128]{2,1,0:T(8,128)} custom-call(s32[1]{0:T(128)} %bitcast.1.rank_ref, f32[128,8,128]{2,1,0:T(8,128)} %copy-done.1, f32[128,16,128]{2,1,0:T(8,128)} %get-tuple-element.9.refs_0_, f32[128,16,128]{2,1,0:T(8,128)} %get-tuple-element.10.refs_1_, f32[64,16,128]{2,1,0:T(8,128)} %get-tuple-element.11.refs_2_, ...), custom_call_target="tpu_custom_call" | custom-call | tf_op jit(solution)/shard_map/contract/pallas_call | solution.py:129
  63.0 12.9 %all-to-all-start.2 = ((f32[32,8,128]{2,1,0:T(8,128)}), f32[32,8,128]{2,1,0:T(8,128)S(1)}, u32[]{:S(2)}, u32[]{:S(2)}) async-start(f32[32,8,128]{2,1,0:T(8,128)} %contract.3), calls=%async_computation.2 | async-start | bytes 262144 | tf_op jit(solution)/shard_map/all_to_all | solution.py:395
  75.9 6.5 %gram.1 = f32[32,48,128]{2,1,0:T(8,128)} custom-call(f32[2048,512]{1,0:T(8,128)} %bitcast.16), custom_call_target="tpu_custom_call" | custom-call | tf_op jit(solution)/shard_map/gram/pallas_call | solution.py:325
  82.4 1.4 all-to-all-done.2
  83.7 6.2 %all-to-all-start.4 = ((f32[32,48,128]{2,1,0:T(8,128)}), f32[32,48,128]{2,1,0:T(8,128)S(1)}, u32[]{:S(2)}, u32[]{:S(2)}) async-start(f32[32,48,128]{2,1,0:T(8,128)} %gram.1), calls=%async_computation.4 | async-start | bytes 1572864 | tf_op jit(solution)/shard_map/all_to_all | solution.py:395
  89.9 13.9 %all-to-all-done.4 = f32[32,48,128]{2,1,0:T(8,128)S(1)} async-done(((f32[32,48,128]{2,1,0:T(8,128)}), f32[32,48,128]{2,1,0:T(8,128)S(1)}, u32[]{:S(2)}, u32[]{:S(2)}) %all-to-all-start.4) | async-done | bytes 786464 | tf_op jit(solution)/shard_map/all_to_all | solution.py:395
  103.8 0.8 broadcast_in_dim.17
  104.7 6.8 %all-to-all-start.3 = ((f32[128,8,128]{2,1,0:T(8,128)}), f32[128,8,128]{2,1,0:T(8,128)S(1)}, u32[]{:S(2)}, u32[]{:S(2)}) async-start(f32[128,8,128]{2,1,0:T(8,128)} %broadcast_in_dim.17), calls=%async_computation.3 | async-start | bytes 1048576 | tf_op jit(solution)/shard_map/all_to_all | solution.py:400
  111.5 0.1 reduce_sum.29
  111.5 2.2 collective-permute-start.4
  113.8 0.0 collective-permute-start.6
  113.8 3.2 %collective-permute-start.8 = (f32[64,16,128]{2,1,0:T(8,128)}, f32[64,16,128]{2,1,0:T(8,128)}, u32[]{:S(2)}, u32[]{:S(2)}) collective-permute-start(f32[64,16,128]{2,1,0:T(8,128)} %get-tuple-element.12.refs_3_), channel_id=1, source_target_pairs={{0,3},{1,0},{2,1},{3,2},{4,7},{5,4},{6,5},{7,6},{8,11},{9,8},{10,9... | collective-permute-start | bytes 1572872 | tf_op jit(solution)/shard_map/ppermute | solution.py:405
  117.0 0.0 collective-permute-start.5
  117.0 3.2 %collective-permute-start.10 = (f32[128,16,128]{2,1,0:T(8,128)S(1)}, f32[128,16,128]{2,1,0:T(8,128)}, u32[]{:S(2)}, u32[]{:S(2)}) collective-permute-start(f32[128,16,128]{2,1,0:T(8,128)S(1)} %copy-done.3), channel_id=1, source_target_pairs={{0,3},{1,0},{2,1},{3,2},{4,7},{5,4},{6,5},{7,6},{8,11},{9,8},{10,9... | collective-permute-start | bytes 3145736 | tf_op jit(solution)/shard_map/ppermute | solution.py:405
  120.3 0.0 collective-permute-done.4
  120.3 1.9 collective-permute-start.3
  122.1 32.0 %collective-permute-done.3 = f32[48,128]{1,0:T(8,128)S(1)} collective-permute-done((f32[48,128]{1,0:T(8,128)S(1)}, f32[48,128]{1,0:T(8,128)S(1)}, u32[]{:S(2)}, u32[]{:S(2)}) %collective-permute-start.3) | collective-permute-done | bytes 24608 | tf_op jit(solution)/shard_map/ppermute | solution.py:405
  154.1 1.1 collective-permute-start.2
  155.2 3.9 %collective-permute-done.2 = f32[48,128]{1,0:T(8,128)S(1)} collective-permute-done((f32[48,128]{1,0:T(8,128)S(1)}, f32[48,128]{1,0:T(8,128)S(1)}, u32[]{:S(2)}, u32[]{:S(2)}) %collective-permute-start.2) | collective-permute-done | bytes 24608 | tf_op jit(solution)/shard_map/ppermute | solution.py:405
  159.1 0.0 all-to-all-done.3.mid_ref
  159.2 1.0 broadcast_in_dim.18
  160.1 7.6 %all-to-all-start.5 = ((f32[32,48,128]{2,1,0:T(8,128)}), f32[32,48,128]{2,1,0:T(8,128)S(1)}, u32[]{:S(2)}, u32[]{:S(2)}) async-start(f32[32,48,128]{2,1,0:T(8,128)} %broadcast_in_dim.18), calls=%async_computation.5 | async-start | bytes 1572864 | tf_op jit(solution)/shard_map/all_to_all | solution.py:400
  167.8 0.0 collective-permute-done.6
  167.8 0.1 collective-permute-start.7
  167.9 3.2 %collective-permute-start.9 = (f32[64,16,128]{2,1,0:T(8,128)}, f32[64,16,128]{2,1,0:T(8,128)}, u32[]{:S(2)}, u32[]{:S(2)}) collective-permute-start(f32[64,16,128]{2,1,0:T(8,128)} %collective-permute-done.8), channel_id=1, source_target_pairs={{0,3},{1,0},{2,1},{3,2},{4,7},{5,4},{6,5},{7,6},{8,11},{9,8},{10,9... | collective-permute-start | bytes 1572872 | tf_op jit(solution)/shard_map/ppermute | solution.py:405
  171.1 10.6 %all-to-all-done.5.gram_ref = f32[32,48,128]{2,1,0:T(8,128)S(1)} async-done(((f32[32,48,128]{2,1,0:T(8,128)}), f32[32,48,128]{2,1,0:T(8,128)S(1)}, u32[]{:S(2)}, u32[]{:S(2)}) %all-to-all-start.5) | async-done | bytes 786464 | tf_op jit(solution)/shard_map/all_to_all | solution.py:400
  181.7 0.9 copy-done
  182.6 13.7 %factor.1 = (f32[512,256]{1,0:T(8,128)}, f32[256,512]{1,0:T(8,128)}) custom-call(f32[128,8,128]{2,1,0:T(8,128)} %copy-done.2, f32[32,48,128]{2,1,0:T(8,128)} %copy-done), custom_call_target="tpu_custom_call" | custom-call | tf_op jit(solution)/shard_map/factor/pallas_call | solution.py:284
  196.3 0.0 collective-permute-done.5.refs_1_
  196.3 0.0 collective-permute-done.10.refs_4_
  196.3 5.6 %project.1 = f32[256,16,128]{2,1,0:T(8,128)} custom-call(s32[1]{0:T(128)} %bitcast.1.rank_ref, f32[256,512]{1,0:T(8,128)} %get-tuple-element.15.project_ref, f32[128,16,128]{2,1,0:T(8,128)} %get-tuple-element.9.refs_0_, f32[128,16,128]{2,1,0:T(8,128)} %collective-permute-done.5.refs_1_, f32[64,16,128]{2,1,0:T(8,128)} %collective-permute-done.7.refs_2_, ...), custom_call_target="tpu_custom_call" | custom-call | tf_op jit(solution)/shard_map/project/pallas_call | solution.py:380
  201.9 3.6 %all-to-all-start.6 = ((f32[4,64,16,128]{3,2,1,0:T(8,128)}), f32[4,64,16,128]{3,2,1,0:T(8,128)S(1)}, u32[]{:S(2)}, u32[]{:S(2)}) async-start(f32[4,64,16,128]{3,2,1,0:T(8,128)} %bitcast.18), calls=%async_computation.6 | async-start | bytes 4194304 | tf_op jit(solution)/shard_map/all_to_all | solution.py:452
  205.5 5.4 %ortho.1 = f32[2048,256]{1,0:T(8,128)} custom-call(f32[2048,512]{1,0:T(8,128)} %bitcast.17, f32[512,256]{1,0:T(8,128)} %get-tuple-element.14.right_ref), custom_call_target="tpu_custom_call" | custom-call | tf_op jit(solution)/shard_map/ortho/pallas_call | solution.py:344
  211.0 21.9 %all-to-all-done.6 = f32[4,64,16,128]{3,2,1,0:T(8,128)S(1)} async-done(((f32[4,64,16,128]{3,2,1,0:T(8,128)}), f32[4,64,16,128]{3,2,1,0:T(8,128)S(1)}, u32[]{:S(2)}, u32[]{:S(2)}) %all-to-all-start.6) | async-done | bytes 2097184 | tf_op jit(solution)/shard_map/all_to_all | solution.py:452
  232.9 1.6 copy_bitcast_fusion
  (22 shorter events, 0.2 us)
Async XLA Ops:
  11.0 32.5 %copy-start.7 = (f32[3,16]{1,0:T(4,128)S(1)}, f32[3,16]{1,0:T(4,128)}, u32[]{:S(2)}) copy-start(f32[3,16]{1,0:T(4,128)} %param.13) | copy-start | bytes 580
  28.3 23.2 %all-to-all-start.1 = ((f32[128,8,128]{2,1,0:T(8,128)}), f32[128,8,128]{2,1,0:T(8,128)S(1)}, u32[]{:S(2)}, u32[]{:S(2)}) async-start(f32[128,8,128]{2,1,0:T(8,128)} %broadcast_in_dim.15), calls=%async_computation.1 | async-start | bytes 1048576 | tf_op jit(solution)/shard_map/all_to_all | solution.py:400
  37.4 2.7 %collective-permute-start = (f32[128,512]{1,0:T(8,128)S(1)}, f32[128,512]{1,0:T(8,128)S(1)}, u32[]{:S(2)}, u32[]{:S(2)}) collective-permute-start(f32[128,512]{1,0:T(8,128)S(1)} %bitcast.20), channel_id=1, source_target_pairs={{0,4},{4,8},{8,12},{12,16},{16,20},{20,24},{24,28},{28,32},{32,36}... | collective-permute-start | bytes 786440 | tf_op jit(solution)/shard_map/ppermute | solution.py:411
  38.8 4.7 %collective-permute-start.1 = (f32[128,512]{1,0:T(8,128)S(1)}, f32[128,512]{1,0:T(8,128)S(1)}, u32[]{:S(2)}, u32[]{:S(2)}) collective-permute-start(f32[128,512]{1,0:T(8,128)S(1)} %bitcast.21), channel_id=1, source_target_pairs={{4,0},{8,4},{12,8},{16,12},{20,16},{24,20},{28,24},{32,28},{36,32}... | collective-permute-start | bytes 786440 | tf_op jit(solution)/shard_map/ppermute | solution.py:412
  40.2 4.1 %copy-start.5 = (f32[128,512]{1,0:T(8,128)}, f32[128,512]{1,0:T(8,128)S(1)}, u32[]{:S(2)}) copy-start(f32[128,512]{1,0:T(8,128)S(1)} %collective-permute-done.below_ref) | copy-start | bytes 786436
  43.5 0.7 copy-start.6
  51.5 0.8 copy-start.1
  63.0 20.7 %all-to-all-start.2 = ((f32[32,8,128]{2,1,0:T(8,128)}), f32[32,8,128]{2,1,0:T(8,128)S(1)}, u32[]{:S(2)}, u32[]{:S(2)}) async-start(f32[32,8,128]{2,1,0:T(8,128)} %contract.3), calls=%async_computation.2 | async-start | bytes 262144 | tf_op jit(solution)/shard_map/all_to_all | solution.py:395
  82.4 34.7 %copy-start.4 = (f32[128,16,128]{2,1,0:T(8,128)S(1)}, f32[128,16,128]{2,1,0:T(8,128)}, u32[]{:S(2)}) copy-start(f32[128,16,128]{2,1,0:T(8,128)} %get-tuple-element.10.refs_1_) | copy-start | bytes 3145732
  82.4 34.7 %copy-start.3 = (f32[128,16,128]{2,1,0:T(8,128)S(1)}, f32[128,16,128]{2,1,0:T(8,128)}, u32[]{:S(2)}) copy-start(f32[128,16,128]{2,1,0:T(8,128)} %get-tuple-element.13.refs_4_) | copy-start | bytes 3145732
  83.7 20.1 %all-to-all-start.4 = ((f32[32,48,128]{2,1,0:T(8,128)}), f32[32,48,128]{2,1,0:T(8,128)S(1)}, u32[]{:S(2)}, u32[]{:S(2)}) async-start(f32[32,48,128]{2,1,0:T(8,128)} %gram.1), calls=%async_computation.4 | async-start | bytes 1572864 | tf_op jit(solution)/shard_map/all_to_all | solution.py:395
  104.7 54.5 %all-to-all-start.3 = ((f32[128,8,128]{2,1,0:T(8,128)}), f32[128,8,128]{2,1,0:T(8,128)S(1)}, u32[]{:S(2)}, u32[]{:S(2)}) async-start(f32[128,8,128]{2,1,0:T(8,128)} %broadcast_in_dim.17), calls=%async_computation.3 | async-start | bytes 1048576 | tf_op jit(solution)/shard_map/all_to_all | solution.py:400
  111.5 8.7 %collective-permute-start.4 = (f32[48,128]{1,0:T(8,128)S(1)}, f32[48,128]{1,0:T(8,128)S(1)}, u32[]{:S(2)}, u32[]{:S(2)}) collective-permute-start(f32[48,128]{1,0:T(8,128)S(1)} %reduce_sum.29), channel_id=1, source_target_pairs={{0,3},{1,0},{2,1},{3,2},{4,7},{5,4},{6,5},{7,6},{8,11},{9,8},{10,9... | collective-permute-start | bytes 73736 | tf_op jit(solution)/shard_map/ppermute | solution.py:405
  113.8 54.0 %collective-permute-start.6 = (f32[64,16,128]{2,1,0:T(8,128)}, f32[64,16,128]{2,1,0:T(8,128)}, u32[]{:S(2)}, u32[]{:S(2)}) collective-permute-start(f32[64,16,128]{2,1,0:T(8,128)} %get-tuple-element.11.refs_2_), channel_id=1, source_target_pairs={{0,1},{1,2},{2,3},{3,0},{4,5},{5,6},{6,7},{7,4},{8,9},{9,10},{10,1... | collective-permute-start | bytes 1572872 | tf_op jit(solution)/shard_map/ppermute | solution.py:405
  113.8 54.1 %collective-permute-start.8 = (f32[64,16,128]{2,1,0:T(8,128)}, f32[64,16,128]{2,1,0:T(8,128)}, u32[]{:S(2)}, u32[]{:S(2)}) collective-permute-start(f32[64,16,128]{2,1,0:T(8,128)} %get-tuple-element.12.refs_3_), channel_id=1, source_target_pairs={{0,3},{1,0},{2,1},{3,2},{4,7},{5,4},{6,5},{7,6},{8,11},{9,8},{10,9... | collective-permute-start | bytes 1572872 | tf_op jit(solution)/shard_map/ppermute | solution.py:405
  117.0 79.3 %collective-permute-start.5 = (f32[128,16,128]{2,1,0:T(8,128)S(1)}, f32[128,16,128]{2,1,0:T(8,128)}, u32[]{:S(2)}, u32[]{:S(2)}) collective-permute-start(f32[128,16,128]{2,1,0:T(8,128)S(1)} %copy-done.4), channel_id=1, source_target_pairs={{0,1},{1,2},{2,3},{3,0},{4,5},{5,6},{6,7},{7,4},{8,9},{9,10},{10,1... | collective-permute-start | bytes 3145736 | tf_op jit(solution)/shard_map/ppermute | solution.py:405
  117.0 79.3 %collective-permute-start.10 = (f32[128,16,128]{2,1,0:T(8,128)S(1)}, f32[128,16,128]{2,1,0:T(8,128)}, u32[]{:S(2)}, u32[]{:S(2)}) collective-permute-start(f32[128,16,128]{2,1,0:T(8,128)S(1)} %copy-done.3), channel_id=1, source_target_pairs={{0,3},{1,0},{2,1},{3,2},{4,7},{5,4},{6,5},{7,6},{8,11},{9,8},{10,9... | collective-permute-start | bytes 3145736 | tf_op jit(solution)/shard_map/ppermute | solution.py:405
  120.3 33.8 %collective-permute-start.3 = (f32[48,128]{1,0:T(8,128)S(1)}, f32[48,128]{1,0:T(8,128)S(1)}, u32[]{:S(2)}, u32[]{:S(2)}) collective-permute-start(f32[48,128]{1,0:T(8,128)S(1)} %reduce_sum.29), channel_id=1, source_target_pairs={{0,2},{1,3},{2,0},{3,1},{4,6},{5,7},{6,4},{7,5},{8,10},{9,11},{10,... | collective-permute-start | bytes 73736 | tf_op jit(solution)/shard_map/ppermute | solution.py:405
  154.1 5.0 %collective-permute-start.2 = (f32[48,128]{1,0:T(8,128)S(1)}, f32[48,128]{1,0:T(8,128)S(1)}, u32[]{:S(2)}, u32[]{:S(2)}) collective-permute-start(f32[48,128]{1,0:T(8,128)S(1)} %reduce_sum.29), channel_id=1, source_target_pairs={{0,1},{1,2},{2,3},{3,0},{4,5},{5,6},{6,7},{7,4},{8,9},{9,10},{10,1... | collective-permute-start | bytes 73736 | tf_op jit(solution)/shard_map/ppermute | solution.py:405
  159.2 22.5 %copy-start.2 = (f32[128,8,128]{2,1,0:T(8,128)}, f32[128,8,128]{2,1,0:T(8,128)S(1)}, u32[]{:S(2)}) copy-start(f32[128,8,128]{2,1,0:T(8,128)S(1)} %all-to-all-done.3.mid_ref) | copy-start | bytes 1572868
  160.1 21.5 %all-to-all-start.5 = ((f32[32,48,128]{2,1,0:T(8,128)}), f32[32,48,128]{2,1,0:T(8,128)S(1)}, u32[]{:S(2)}, u32[]{:S(2)}) async-start(f32[32,48,128]{2,1,0:T(8,128)} %broadcast_in_dim.18), calls=%async_computation.5 | async-start | bytes 1572864 | tf_op jit(solution)/shard_map/all_to_all | solution.py:400
  167.8 28.5 %collective-permute-start.7 = (f32[64,16,128]{2,1,0:T(8,128)}, f32[64,16,128]{2,1,0:T(8,128)}, u32[]{:S(2)}, u32[]{:S(2)}) collective-permute-start(f32[64,16,128]{2,1,0:T(8,128)} %collective-permute-done.6), channel_id=1, source_target_pairs={{0,1},{1,2},{2,3},{3,0},{4,5},{5,6},{6,7},{7,4},{8,9},{9,10},{10,1... | collective-permute-start | bytes 1572872 | tf_op jit(solution)/shard_map/ppermute | solution.py:405
  167.9 28.4 %collective-permute-start.9 = (f32[64,16,128]{2,1,0:T(8,128)}, f32[64,16,128]{2,1,0:T(8,128)}, u32[]{:S(2)}, u32[]{:S(2)}) collective-permute-start(f32[64,16,128]{2,1,0:T(8,128)} %collective-permute-done.8), channel_id=1, source_target_pairs={{0,3},{1,0},{2,1},{3,2},{4,7},{5,4},{6,5},{7,6},{8,11},{9,8},{10,9... | collective-permute-start | bytes 1572872 | tf_op jit(solution)/shard_map/ppermute | solution.py:405
  181.7 0.9 copy-start
  201.9 31.0 %all-to-all-start.6 = ((f32[4,64,16,128]{3,2,1,0:T(8,128)}), f32[4,64,16,128]{3,2,1,0:T(8,128)S(1)}, u32[]{:S(2)}, u32[]{:S(2)}) async-start(f32[4,64,16,128]{3,2,1,0:T(8,128)} %bitcast.18), calls=%async_computation.6 | async-start | bytes 4194304 | tf_op jit(solution)/shard_map/all_to_all | solution.py:452

commit v3 on v2

--- a/solution.py
+++ b/solution.py
@@ -18,6 +18,9 @@
 TILE = 8
 BLOCK = 64
 PIECES = (1, 1, 2, 1)
+STEPS = 4
+SKETCH_STEPS = 2
+GROUP = 16
 
 NN = (((1,), (0,)), ((), ()))
 NT = (((1,), (1,)), ((), ()))
@@ -72,127 +75,149 @@
     )
 
 
+def started(source, target, sem):
+    copy = pltpu.make_async_copy(source, target, sem)
+    copy.start()
+    return copy
+
+
 def contract_kernel(core_parts, rank_ref, part_ref, *refs):
     count = sum(core_parts) if core_parts else 1
-    core_refs, (*sketch_refs, out_ref, applied_ref, sum_ref) = list(refs[:count]), refs[count:]
+    core_hbm, sketch_hbm, out_ref, *refs = refs[:count], refs[count], refs[count + 1], *refs[count + 2 :]
+    core_refs, (sketch_ref, applied_ref, core_sems, sketch_sems) = refs[:count], refs[count:]
     peers = out_ref.shape[0]
     slices = core_refs[0].shape[1]
-    if not core_parts:
-        core = core_refs[0][...].reshape(-1, core_refs[0].shape[2])
+    rows = core_refs[0].shape[0]
+    pieces, sketch_rows = sketch_ref.shape[:2]
+    step = rows // STEPS
+
+    plan = []
+    for k in range(STEPS):
+        at = 0
+        for split in core_parts or (1,):
+            n, begin = divmod(k * step, rows // split)
+            plan.append((k, at + n, pl.ds(begin, step)))
+            at += split
+    arriving = [
+        (k, index, lines, started(core_hbm[index].at[lines], core_refs[index].at[lines], core_sems.at[n]))
+        for n, (k, index, lines) in enumerate(plan)
+    ]
+    sketch_part = sketch_rows // SKETCH_STEPS
+    sketches_arriving = []
+    for c in range(SKETCH_STEPS):
+        lines = pl.ds(c * sketch_part, sketch_part)
+        for h in range(pieces):
+            source = sketch_hbm.at[lines, :, pl.ds(h * LANES, LANES)]
+            sketches_arriving.append(started(source, sketch_ref.at[h, lines], sketch_sems.at[c * pieces + h]))
+
+    if core_parts:
+        blocks = [lax.rem(rank_ref[0] + distance, len(core_parts)) for distance in range(len(core_parts))]
+        part = jnp.concatenate([gathered(part_ref, peers, LANES // peers, block * peers) for block in blocks], axis=0)
+    else:
         part = part_ref[...]
-    else:
-        blocks, lines = [], []
-        for distance, pieces in enumerate(core_parts):
-            taken = [core_refs.pop(0)[...].reshape(-1, LANES) for _ in range(pieces)]
-            blocks.append(taken[0] if pieces == 1 else jnp.concatenate(taken, axis=0))
-            block = lax.rem(rank_ref[0] + distance, len(core_parts))
-            lines.append(gathered(part_ref, peers, LANES // peers, block * peers))
-        core, part = jnp.concatenate(blocks, axis=1), jnp.concatenate(lines, axis=0)
-    rows = core.shape[0] // slices
-    applied = dot3(halves(core), halves(part), NN)
-    for h in range(len(sketch_refs)):
-        applied_ref[h] = applied[:, h * LANES : (h + 1) * LANES]
-    sketch_rows = sketch_refs[0].shape[0]
-    sketches = [ref.reshape(sketch_rows * slices, LANES) for ref in sketch_refs]
-    total = None
-    for i in range(slices):
-        left = [applied_ref.at[h][pl.ds(i, rows, stride=slices), :] for h in range(len(sketches))]
-        right = [ref[pl.ds(i, sketch_rows, stride=slices), :] for ref in sketches]
-        term = dot3(halves(jnp.concatenate(left, axis=1)), halves(jnp.concatenate(right, axis=1)), NT)
-        total = term if total is None else total + term
-
-    last = pl.num_programs(0) - 1
-
-    @pl.when(pl.program_id(0) == 0)
-    def _():
-        sum_ref[...] = total
-
-    @pl.when((pl.program_id(0) > 0) & (pl.program_id(0) < last))
-    def _():
-        sum_ref[...] += total
-
-    @pl.when(pl.program_id(0) == last)
-    def _():
-        spread(out_ref, sum_ref[...] + total)
+    part = halves(part)
+    for k in range(STEPS):
+        taken = []
+        for chunk, index, lines, copy in arriving:
+            if chunk == k:
+                copy.wait()
+                taken.append(core_refs[index][lines].reshape(step * slices, -1))
+        core = taken[0] if len(taken) == 1 else jnp.concatenate(taken, axis=1)
+        applied = dot3(halves(core), part, NN)
+        for h in range(pieces):
+            applied_ref[h, pl.ds(k * step * slices, step * slices), :] = applied[:, h * LANES : (h + 1) * LANES]
+    for copy in sketches_arriving:
+        copy.wait()
+    sketches = [sketch_ref.at[h].reshape(sketch_rows * slices, LANES) for h in range(pieces)]
+
+    def run(g, total):
+        for i in range(TILE):
+            at = g * TILE + i
+            left = [applied_ref.at[h][pl.ds(at, rows, stride=slices), :] for h in range(pieces)]
+            right = [ref[pl.ds(at, sketch_rows, stride=slices), :] for ref in sketches]
+            total += dot3(halves(jnp.concatenate(left, axis=1)), halves(jnp.concatenate(right, axis=1)), NT)
+        return total
+
+    total = lax.fori_loop(0, slices // TILE, run, jnp.zeros((rows, sketch_rows), F32))
+    spread(out_ref, total)
 
 
 SCALAR = pl.BlockSpec(memory_space=pltpu.SMEM)
+IN_VMEM = pl.BlockSpec(memory_space=pltpu.VMEM)
+IN_HBM = pl.BlockSpec(memory_space=pltpu.HBM)
 
 
 def contract_back(rank, cores, core_parts, part, sketch):
-    slices = cores[0].shape[1]
+    rows, slices = cores[0].shape[:2]
     sketch_rows, _, sketch_cols = sketch.shape
-    rows = sum(core.shape[0] for core in cores[: core_parts[0] if core_parts else 1])
     pieces = sketch_cols // LANES
     peers = lax.axis_size(CUTS)
     shape = (peers, rows * sketch_rows // LANES // peers, LANES)
     return pl.pallas_call(
         functools.partial(contract_kernel, core_parts),
-        grid=(slices // TILE,),
-        in_specs=[
-            SCALAR,
-            whole_block(part.shape),
-            *[pl.BlockSpec((core.shape[0], TILE, core.shape[2]), lambda g: (0, g, 0)) for core in cores],
-            *[pl.BlockSpec((sketch_rows, TILE, LANES), lambda g, h=h: (0, g, h)) for h in range(pieces)],
+        in_specs=[SCALAR, IN_VMEM, *[IN_HBM] * (len(cores) + 1)],
+        out_specs=IN_VMEM,
+        out_shape=jax.ShapeDtypeStruct(shape, F32),
+        scratch_shapes=[
+            *[pltpu.VMEM(core.shape, F32) for core in cores],
+            pltpu.VMEM((pieces, sketch_rows, slices, LANES), F32),
+            pltpu.VMEM((pieces, rows * slices, LANES), F32),
+            pltpu.SemaphoreType.DMA((STEPS * max(1, len(core_parts)),)),
+            pltpu.SemaphoreType.DMA((SKETCH_STEPS * pieces,)),
         ],
-        out_specs=whole_block(shape),
-        out_shape=jax.ShapeDtypeStruct(shape, F32),
-        scratch_shapes=[pltpu.VMEM((pieces, rows * TILE, LANES), F32), pltpu.VMEM((rows, sketch_rows), F32)],
         name="contract",
-    )(rank, part, *cores, *[sketch] * pieces)
-
-
-def stencil_kernel(pieces, rank_ref, core_ref, below_ref, above_ref, coef_ref, *out_refs):
-    rows, slices, _ = core_ref.shape
-    out_refs = list(out_refs)
+    )(rank, part, *cores, sketch)
+
+
+def stencil_kernel(pieces, rank_ref, core_hbm, below_ref, above_ref, coef_ref, *refs):
+    count = sum(pieces)
+    outs_hbm, core_all, step_refs, (in_sems, out_sems) = refs[:count], refs[count], refs[count + 1 : -2], refs[-2:]
+    total, slices, _ = core_all.shape
+    rows = GROUP
+    groups = total // rows
+    lines = [pl.ds(g * rows, rows) for g in range(groups)]
+    arriving = [started(core_hbm.at[lines[g]], core_all.at[lines[g]], in_sems.at[g]) for g in range(groups)]
     place = lax.broadcasted_iota(jnp.int32, (rows * slices, LANES), 0) % slices
     coef = [jnp.broadcast_to(coef_ref[k][None], (rows, slices, LANES)).reshape(rows * slices, LANES) for k in range(3)]
-    for distance, count in enumerate(pieces):
-        cols = pl.ds(own_block(rank_ref, distance, len(pieces)), LANES)
-        core = core_ref[:, :, cols].reshape(rows * slices, LANES)
-        first = jnp.broadcast_to(below_ref[:, cols][:, None, :], (rows, slices, LANES)).reshape(rows * slices, LANES)
-        last = jnp.broadcast_to(above_ref[:, cols][:, None, :], (rows, slices, LANES)).reshape(rows * slices, LANES)
-        below = jnp.where(place == 0, first, pltpu.roll(core, 1, 0))
-        above = jnp.where(place == slices - 1, last, pltpu.roll(core, rows * slices - 1, 0))
-        stepped = (coef[0] * below + coef[1] * core + coef[2] * above).reshape(rows, slices, LANES)
-        each = pl.num_programs(0) // count
-        for n in range(count):
-            out_ref = out_refs.pop(0)
-            if count == 1:
-                out_ref[...] = stepped
-                continue
-
-            @pl.when(pl.program_id(0) // each == n)
-            def _(out_ref=out_ref, stepped=stepped):
-                out_ref[...] = stepped
+    leaving = []
+    for g in range(groups):
+        arriving[g].wait()
+        at = 0
+        for distance, split in enumerate(pieces):
+            cols = pl.ds(own_block(rank_ref, distance, len(pieces)), LANES)
+            core = core_all[lines[g], :, cols].reshape(rows * slices, LANES)
+            first = jnp.broadcast_to(below_ref[lines[g], cols][:, None, :], (rows, slices, LANES))
+            last = jnp.broadcast_to(above_ref[lines[g], cols][:, None, :], (rows, slices, LANES))
+            below = jnp.where(place == 0, first.reshape(rows * slices, LANES), pltpu.roll(core, 1, 0))
+            above = jnp.where(
+                place == slices - 1, last.reshape(rows * slices, LANES), pltpu.roll(core, rows * slices - 1, 0)
+            )
+            stepped = (coef[0] * below + coef[1] * core + coef[2] * above).reshape(rows, slices, LANES)
+            n, begin = divmod(g * rows, total // split)
+            target = pl.ds(begin, rows)
+            step_refs[at + n][target] = stepped
+            sem = out_sems.at[g * len(pieces) + distance]
+            leaving.append(started(step_refs[at + n].at[target], outs_hbm[at + n].at[target], sem))
+            at += split
+    for copy in leaving:
+        copy.wait()
 
 
 def step_core(rank, core, below, above, stencil, pieces):
-    rows, slices, width = core.shape
-    group = 16
+    rows, slices, _ = core.shape
     coef = jnp.broadcast_to(stencil[:, :, None], (3, slices, LANES))
-    out_specs, out_shape = [], []
-    for count in pieces:
-        each = rows // group // count
-        for n in range(count):
-            out_specs.append(
-                pl.BlockSpec(
-                    (group, slices, LANES), lambda g, n=n, each=each: (jnp.clip(g - n * each, 0, each - 1), 0, 0)
-                )
-            )
-            out_shape.append(jax.ShapeDtypeStruct((rows // count, slices, LANES), F32))
+    shapes = [(rows // split, slices, LANES) for split in pieces for _ in range(split)]
     return pl.pallas_call(
         functools.partial(stencil_kernel, pieces),
-        grid=(rows // group,),
-        in_specs=[
-            SCALAR,
-            pl.BlockSpec((group, slices, width), lambda g: (g, 0, 0)),
-            pl.BlockSpec((group, width), lambda g: (g, 0)),
-            pl.BlockSpec((group, width), lambda g: (g, 0)),
-            whole_block(coef.shape),
+        in_specs=[SCALAR, IN_HBM, IN_VMEM, IN_VMEM, IN_VMEM],
+        out_specs=[IN_HBM] * len(shapes),
+        out_shape=[jax.ShapeDtypeStruct(shape, F32) for shape in shapes],
+        scratch_shapes=[
+            pltpu.VMEM(core.shape, F32),
+            *[pltpu.VMEM(shape, F32) for shape in shapes],
+            pltpu.SemaphoreType.DMA((rows // GROUP,)),
+            pltpu.SemaphoreType.DMA((rows // GROUP * len(pieces),)),
         ],
-        out_specs=out_specs,
-        out_shape=out_shape,
         name="stencil",
     )(rank, core, below, above, coef)
 
@@ -292,43 +317,46 @@
     )(mid_sum, gram_left)
 
 
-def gram_kernel(rows_ref, out_ref, sum_ref):
-    half = rows_ref.shape[1] // 2
-    high, low = halves(rows_ref[...])
-    first = (high[:, :half], low[:, :half])
-    second = (high[:, half:], low[:, half:])
-    top = dot3(first, (high, low), TN)
-    corner = dot3(second, second, TN)
-    corner = jnp.concatenate([corner[: half // 2], corner[half // 2 :]], axis=1)
-    total = jnp.concatenate([top, corner], axis=0)
-    last = pl.num_programs(0) - 1
-
-    @pl.when(pl.program_id(0) == 0)
-    def _():
-        sum_ref[...] = total
-
-    @pl.when((pl.program_id(0) > 0) & (pl.program_id(0) < last))
-    def _():
-        sum_ref[...] += total
-
-    @pl.when(pl.program_id(0) == last)
-    def _():
-        spread(out_ref, sum_ref[...] + total)
+def gram_kernel(rows_hbm, out_ref, rows_ref, sum_ref, sems):
+    count, depth = rows_ref.shape
+    half = depth // 2
+    part = count // STEPS
+
+    def copy_of(k):
+        lines = pl.ds(pl.multiple_of(k * part, part), part)
+        return lines, pltpu.make_async_copy(rows_hbm.at[lines], rows_ref.at[lines], sems.at[k])
+
+    for k in range(STEPS):
+        copy_of(k)[1].start()
+    sum_ref[...] = jnp.zeros_like(sum_ref)
+
+    def run(k, carry):
+        lines, copy = copy_of(k)
+        copy.wait()
+        high, low = halves(rows_ref[lines, :])
+        first = (high[:, :half], low[:, :half])
+        second = (high[:, half:], low[:, half:])
+        sum_ref[:half, :] += dot3(first, (high, low), TN)
+        corner = dot3(second, second, TN)
+        sum_ref[half:, :half] += corner[: half // 2]
+        sum_ref[half:, half:] += corner[half // 2 :]
+        return carry
+
+    lax.fori_loop(0, STEPS, run, 0)
+    spread(out_ref, sum_ref[...])
 
 
 def packed_gram(rows):
-    count, depth = rows.shape
-    group = 512
+    depth = rows.shape[1]
     sums = (depth // 2 + depth // 4, depth)
     peers = lax.axis_size(CUTS)
     shape = (peers, sums[0] * sums[1] // LANES // peers, LANES)
     return pl.pallas_call(
         gram_kernel,
-        grid=(count // group,),
-        in_specs=[pl.BlockSpec((group, depth), lambda g: (g, 0))],
-        out_specs=whole_block(shape),
+        in_specs=[IN_HBM],
+        out_specs=IN_VMEM,
         out_shape=jax.ShapeDtypeStruct(shape, F32),
-        scratch_shapes=[pltpu.VMEM(sums, F32)],
+        scratch_shapes=[pltpu.VMEM(rows.shape, F32), pltpu.VMEM(sums, F32), pltpu.SemaphoreType.DMA((STEPS,))],
         name="gram",
     )(rows)
 
@@ -352,41 +380,57 @@
 
 
 def project_kernel(pieces, rank_ref, project_ref, *refs):
-    *stepped_refs, out_ref = refs
-    slices = stepped_refs[0].shape[1]
+    count = sum(pieces)
+    blocks_hbm, out_hbm, block_refs, (out_ref, in_sems, out_sems) = refs[:count], refs[count], refs[count + 1 : -3], refs[-3:]
+    slices = blocks_hbm[0].shape[1]
     rows = project_ref.shape[0]
     ranks = len(pieces)
+    groups = slices // TILE
+    slabs = [pl.ds(g * TILE, TILE) for g in range(groups)]
+    arriving = [
+        [started(hbm.at[:, slabs[g]], ref.at[g], in_sems.at[g * count + n]) for n, (hbm, ref) in enumerate(zip(blocks_hbm, block_refs))]
+        for g in range(groups)
+    ]
     project = halves(
         jnp.concatenate(
             [project_ref[:, pl.ds(own_block(rank_ref, ranks - distance, ranks), LANES)] for distance in range(ranks)],
             axis=1,
         )
     )
-    stepped = [(ref.reshape(-1, LANES), ref.shape[0]) for ref in stepped_refs]
-    out = out_ref.reshape(rows * slices, LANES)
-
-    def slab(i):
-        return jnp.concatenate([ref[pl.ds(i, count, stride=slices), :] for ref, count in stepped], axis=0)
-
-    for i in range(0, slices, 2):
-        product = dot3(project, halves(jnp.concatenate([slab(i), slab(i + 1)], axis=1)), NN)
-        for d in range(2):
-            out[pl.ds(i + d, rows, stride=slices), :] = product[:, d * LANES : (d + 1) * LANES]
+    leaving = []
+    for g in range(groups):
+        for copy in arriving[g]:
+            copy.wait()
+        stepped = [(ref.at[g].reshape(-1, LANES), ref.shape[1]) for ref in block_refs]
+        out = out_ref.at[g].reshape(rows * TILE, LANES)
+
+        def slab(i, stepped=stepped):
+            return jnp.concatenate([ref[pl.ds(i, length, stride=TILE), :] for ref, length in stepped], axis=0)
+
+        for i in range(0, TILE, 2):
+            product = dot3(project, halves(jnp.concatenate([slab(i), slab(i + 1)], axis=1)), NN)
+            for d in range(2):
+                out[pl.ds(i + d, rows, stride=TILE), :] = product[:, d * LANES : (d + 1) * LANES]
+        leaving.append(started(out_ref.at[g], out_hbm.at[:, slabs[g]], out_sems.at[g]))
+    for copy in leaving:
+        copy.wait()
 
 
 def projected(rank, project, stepped, pieces):
     slices = stepped[0].shape[1]
     rows = project.shape[0]
+    groups = slices // TILE
     return pl.pallas_call(
         functools.partial(project_kernel, pieces),
-        grid=(slices // TILE,),
-        in_specs=[
-            SCALAR,
-            whole_block(project.shape),
-            *[pl.BlockSpec((block.shape[0], TILE, LANES), lambda g: (0, g, 0)) for block in stepped],
+        in_specs=[SCALAR, IN_VMEM, *[IN_HBM] * len(stepped)],
+        out_specs=IN_HBM,
+        out_shape=jax.ShapeDtypeStruct((rows, slices, LANES), F32),
+        scratch_shapes=[
+            *[pltpu.VMEM((groups, block.shape[0], TILE, LANES), F32) for block in stepped],
+            pltpu.VMEM((groups, rows, TILE, LANES), F32),
+            pltpu.SemaphoreType.DMA((groups * len(stepped),)),
+            pltpu.SemaphoreType.DMA((groups,)),
         ],
-        out_specs=pl.BlockSpec((rows, TILE, LANES), lambda g: (0, g, 0)),
-        out_shape=jax.ShapeDtypeStruct((rows, slices, LANES), F32),
         name="project",
     )(rank, project, *stepped)
 

time: 236 us -> 233 us (0.987)
  Pallas kernels: 59.6 us -> 56.6 us
    pallas_call x5, Pallas kernels: 40.4 us -> 37.5 us  [the longest x2 20.4 us: contract_back(): pl.pallas_call(functools.partial(contract_kernel, core_parts), in_specs=[...]
  transfers between devices with their start and end apart: 17 -> 17, of which waited for: 7 -> 7; matrix products, arithmetic and copies ran while one was open for 2% -> 2% of each run, Pallas kernels for 14% -> 13%
where the time goes in v3:
time: 233 us; the launch traced here: 231 us
  waiting for transfers between devices  87.5 us (38%)
  starting transfers between devices  60.5 us (26%)
  Pallas kernels  56.6 us (24%)
  blocking collectives  16.3 us (7%)
  local copies, waits for them, and re-layouts  9.47 us (4%)
    ppermute x9, waiting for transfers between devices, shifted(): lax.ppermute(array, 'rank', [(i, (i + distance) % count) for i in range(c...  35.9 us
    all_to_all x1, waiting for transfers between devices, step(): arrived = lax.all_to_all(blocks, 'rank', 0, 0, tiled=True)  21.9 us
    all_to_all x3, starting transfers between devices, copies_of(): return lax.all_to_all(copies, axes, 0, 0, tiled=True)  20.8 us
    pallas_call x2, Pallas kernels, contract_back(): pl.pallas_call(functools.partial(contract_kernel, core_parts), in_specs=[...  20.4 us
    all_to_all x2, starting transfers between devices, summed(): return jnp.sum(lax.all_to_all(pieces, axes, 0, 0, tiled=True), axis=0)  18.5 us
    all_to_all x1, blocking collectives, summed(): return jnp.sum(lax.all_to_all(pieces, axes, 0, 0, tiled=True), axis=0)  16.3 us
    all_to_all x2, waiting for transfers between devices, summed(): return jnp.sum(lax.all_to_all(pieces, axes, 0, 0, tiled=True), axis=0)  15.8 us
    ppermute x9, starting transfers between devices, shifted(): lax.ppermute(array, 'rank', [(i, (i + distance) % count) for i in range(c...  15 us
  transfers between devices with their start and end apart: 17, of which 7 were waited for; matrix products, arithmetic and copies ran while one was open for 2% of the time, Pallas kernels for 13%

profile of v3, /device:TPU:0, one launch (start us, length us, event | category | flops | bytes accessed | tf_op | source)
XLA Modules:
  0.0 231.5 jit_solution(13049771060795482795)
XLA Ops:
  0.6 10.1 %contract.2 = f32[32,8,128]{2,1,0:T(8,128)} custom-call(s32[1]{0:T(128)} %bitcast.1.rank_ref, f32[512,256]{1,0:T(8,128)} %part_ref.1, f32[128,16,512]{2,1,0:T(8,128)} %refs_0_.1, f32[256,16,256]{2,1,0:T(8,128)} %refs_1_.1), custom_call_target="tpu_custom_call" | custom-call | tf_op jit(solution)/shard_map/contract/pallas_call | solution.py:156
  10.7 0.0 copy-start.7
  10.7 16.3 %all_to_all.35 = f32[32,8,128]{2,1,0:T(8,128)S(1)} all-to-all(f32[32,8,128]{2,1,0:T(8,128)} %contract.2), channel_id=1, replica_groups=mesh['cuts_0'=4,'cuts_1'=4,'cuts_2'=2,'rank'=4] {'cuts_0','cuts_1','cuts..., dimensions={0} | all-to-all | bytes 262144 | tf_op jit(solution)/shard_map/all_to_all | solution.py:439
  27.1 0.8 broadcast_in_dim.15
  27.9 6.3 %all-to-all-start.1 = ((f32[128,8,128]{2,1,0:T(8,128)}), f32[128,8,128]{2,1,0:T(8,128)S(1)}, u32[]{:S(2)}, u32[]{:S(2)}) async-start(f32[128,8,128]{2,1,0:T(8,128)} %broadcast_in_dim.15), calls=%async_computation.1 | async-start | bytes 1048576 | tf_op jit(solution)/shard_map/all_to_all | solution.py:444
  34.2 2.7 %fusion = (f32[128,1,512]{2,1,0:T(1,128)S(1)}, f32[128,1,512]{2,1,0:T(1,128)S(1)}) fusion(f32[128,16,512]{2,1,0:T(8,128)} %core_hbm.1), kind=kLoop, calls=%fused_computation.4 | loop fusion | bytes 1048576 | tf_op jit(solution)/shard_map/slice | solution.py:454
  37.0 1.4 collective-permute-start
  38.4 1.3 collective-permute-start.1
  39.7 3.4 %collective-permute-done.1.above_ref = f32[128,512]{1,0:T(8,128)S(1)} collective-permute-done((f32[128,512]{1,0:T(8,128)S(1)}, f32[128,512]{1,0:T(8,128)S(1)}, u32[]{:S(2)}, u32[]{:S(2)}) %collective-permute-start.1) | collective-permute-done | bytes 262176 | tf_op jit(solution)/shard_map/ppermute | solution.py:456
  43.1 0.7 broadcast_in_dim.16.coef_ref
  43.8 4.9 %stencil.1 = (f32[128,16,128]{2,1,0:T(8,128)}, f32[128,16,128]{2,1,0:T(8,128)}, f32[64,16,128]{2,1,0:T(8,128)}, f32[64,16,128]{2,1,0:T(8,128)}, f32[128,16,128]{2,1,0:T(8,128)}) custom-call(s32[1]{0:T(128)} %bitcast.1.rank_ref, f32[128,16,512]{2,1,0:T(8,128)} %core_hbm.1, f32[128,512]{1,0:T(8,128)} %copy-done.5, f32[128,512]{1,0:T(8,128)} %copy-done.6, ...), custom_call_target="tpu_custom_call" | custom-call | tf_op jit(solution)/shard_map/stencil/pallas_call | solution.py:210
  48.7 0.0 all-to-all-done.1.part_ref
  48.8 0.8 copy-done.1
  49.6 10.3 %contract.3 = f32[32,8,128]{2,1,0:T(8,128)} custom-call(s32[1]{0:T(128)} %bitcast.1.rank_ref, f32[128,8,128]{2,1,0:T(8,128)} %copy-done.1, f32[128,16,128]{2,1,0:T(8,128)} %get-tuple-element.9.refs_0_, f32[128,16,128]{2,1,0:T(8,128)} %get-tuple-element.10.refs_1_, f32[64,16,128]{2,1,0:T(8,128)} %get-tuple-element.11.refs_2_, ...), custom_call_target="tpu_custom_call" | custom-call | tf_op jit(solution)/shard_map/contract/pallas_call | solution.py:156
  59.9 12.9 %all-to-all-start.2 = ((f32[32,8,128]{2,1,0:T(8,128)}), f32[32,8,128]{2,1,0:T(8,128)S(1)}, u32[]{:S(2)}, u32[]{:S(2)}) async-start(f32[32,8,128]{2,1,0:T(8,128)} %contract.3), calls=%async_computation.2 | async-start | bytes 262144 | tf_op jit(solution)/shard_map/all_to_all | solution.py:439
  72.7 5.9 %gram.1 = f32[32,48,128]{2,1,0:T(8,128)} custom-call(f32[2048,512]{1,0:T(8,128)} %bitcast.16), custom_call_target="tpu_custom_call" | custom-call | tf_op jit(solution)/shard_map/gram/pallas_call | solution.py:354
  78.6 0.0 copy-start.4
  78.7 1.9 all-to-all-done.2
  80.6 5.6 %all-to-all-start.4 = ((f32[32,48,128]{2,1,0:T(8,128)}), f32[32,48,128]{2,1,0:T(8,128)S(1)}, u32[]{:S(2)}, u32[]{:S(2)}) async-start(f32[32,48,128]{2,1,0:T(8,128)} %gram.1), calls=%async_computation.4 | async-start | bytes 1572864 | tf_op jit(solution)/shard_map/all_to_all | solution.py:439
  86.2 13.9 %all-to-all-done.4 = f32[32,48,128]{2,1,0:T(8,128)S(1)} async-done(((f32[32,48,128]{2,1,0:T(8,128)}), f32[32,48,128]{2,1,0:T(8,128)S(1)}, u32[]{:S(2)}, u32[]{:S(2)}) %all-to-all-start.4) | async-done | bytes 786464 | tf_op jit(solution)/shard_map/all_to_all | solution.py:439
  100.1 0.8 broadcast_in_dim.17
  101.0 6.8 %all-to-all-start.3 = ((f32[128,8,128]{2,1,0:T(8,128)}), f32[128,8,128]{2,1,0:T(8,128)S(1)}, u32[]{:S(2)}, u32[]{:S(2)}) async-start(f32[128,8,128]{2,1,0:T(8,128)} %broadcast_in_dim.17), calls=%async_computation.3 | async-start | bytes 1048576 | tf_op jit(solution)/shard_map/all_to_all | solution.py:444
  107.8 0.1 reduce_sum.29
  107.8 2.2 collective-permute-start.4
  110.1 0.0 collective-permute-start.6
  110.1 3.2 %collective-permute-start.8 = (f32[64,16,128]{2,1,0:T(8,128)}, f32[64,16,128]{2,1,0:T(8,128)}, u32[]{:S(2)}, u32[]{:S(2)}) collective-permute-start(f32[64,16,128]{2,1,0:T(8,128)} %get-tuple-element.12.refs_3_), channel_id=1, source_target_pairs={{0,3},{1,0},{2,1},{3,2},{4,7},{5,4},{6,5},{7,6},{8,11},{9,8},{10,9... | collective-permute-start | bytes 1572872 | tf_op jit(solution)/shard_map/ppermute | solution.py:449
  113.3 0.0 collective-permute-start.5
  113.3 3.2 %collective-permute-start.10 = (f32[128,16,128]{2,1,0:T(8,128)S(1)}, f32[128,16,128]{2,1,0:T(8,128)}, u32[]{:S(2)}, u32[]{:S(2)}) collective-permute-start(f32[128,16,128]{2,1,0:T(8,128)S(1)} %copy-done.3), channel_id=1, source_target_pairs={{0,3},{1,0},{2,1},{3,2},{4,7},{5,4},{6,5},{7,6},{8,11},{9,8},{10,9... | collective-permute-start | bytes 3145736 | tf_op jit(solution)/shard_map/ppermute | solution.py:449
  116.6 0.0 collective-permute-done.4
  116.6 1.9 collective-permute-start.3
  118.4 32.0 %collective-permute-done.3 = f32[48,128]{1,0:T(8,128)S(1)} collective-permute-done((f32[48,128]{1,0:T(8,128)S(1)}, f32[48,128]{1,0:T(8,128)S(1)}, u32[]{:S(2)}, u32[]{:S(2)}) %collective-permute-start.3) | collective-permute-done | bytes 24608 | tf_op jit(solution)/shard_map/ppermute | solution.py:449
  150.4 1.1 collective-permute-start.2
  151.5 3.9 %collective-permute-done.2 = f32[48,128]{1,0:T(8,128)S(1)} collective-permute-done((f32[48,128]{1,0:T(8,128)S(1)}, f32[48,128]{1,0:T(8,128)S(1)}, u32[]{:S(2)}, u32[]{:S(2)}) %collective-permute-start.2) | collective-permute-done | bytes 24608 | tf_op jit(solution)/shard_map/ppermute | solution.py:449
  155.5 1.0 broadcast_in_dim.18
  156.4 7.6 %all-to-all-start.5 = ((f32[32,48,128]{2,1,0:T(8,128)}), f32[32,48,128]{2,1,0:T(8,128)S(1)}, u32[]{:S(2)}, u32[]{:S(2)}) async-start(f32[32,48,128]{2,1,0:T(8,128)} %broadcast_in_dim.18), calls=%async_computation.5 | async-start | bytes 1572864 | tf_op jit(solution)/shard_map/all_to_all | solution.py:444
  164.1 0.0 collective-permute-done.6
  164.1 0.1 collective-permute-start.7
  164.2 0.0 collective-permute-done.8
  164.2 3.2 %collective-permute-start.9 = (f32[64,16,128]{2,1,0:T(8,128)}, f32[64,16,128]{2,1,0:T(8,128)}, u32[]{:S(2)}, u32[]{:S(2)}) collective-permute-start(f32[64,16,128]{2,1,0:T(8,128)} %collective-permute-done.8), channel_id=1, source_target_pairs={{0,3},{1,0},{2,1},{3,2},{4,7},{5,4},{6,5},{7,6},{8,11},{9,8},{10,9... | collective-permute-start | bytes 1572872 | tf_op jit(solution)/shard_map/ppermute | solution.py:449
  167.4 10.6 %all-to-all-done.5.gram_ref = f32[32,48,128]{2,1,0:T(8,128)S(1)} async-done(((f32[32,48,128]{2,1,0:T(8,128)}), f32[32,48,128]{2,1,0:T(8,128)S(1)}, u32[]{:S(2)}, u32[]{:S(2)}) %all-to-all-start.5) | async-done | bytes 786464 | tf_op jit(solution)/shard_map/all_to_all | solution.py:444
  178.0 0.9 copy-done
  178.9 13.7 %factor.1 = (f32[512,256]{1,0:T(8,128)}, f32[256,512]{1,0:T(8,128)}) custom-call(f32[128,8,128]{2,1,0:T(8,128)} %copy-done.2, f32[32,48,128]{2,1,0:T(8,128)} %copy-done), custom_call_target="tpu_custom_call" | custom-call | tf_op jit(solution)/shard_map/factor/pallas_call | solution.py:309
  192.6 0.0 collective-permute-done.7.refs_2_
  192.6 6.3 %project.1 = f32[256,16,128]{2,1,0:T(8,128)} custom-call(s32[1]{0:T(128)} %bitcast.1.rank_ref, f32[256,512]{1,0:T(8,128)} %get-tuple-element.15.project_ref, f32[128,16,128]{2,1,0:T(8,128)} %get-tuple-element.9.refs_0_, f32[128,16,128]{2,1,0:T(8,128)} %collective-permute-done.5.refs_1_, f32[64,16,128]{2,1,0:T(8,128)} %collective-permute-done.7.refs_2_, ...), custom_call_target="tpu_custom_call" | custom-call | tf_op jit(solution)/shard_map/project/pallas_call | solution.py:423
  198.9 3.6 %all-to-all-start.6 = ((f32[4,64,16,128]{3,2,1,0:T(8,128)}), f32[4,64,16,128]{3,2,1,0:T(8,128)S(1)}, u32[]{:S(2)}, u32[]{:S(2)}) async-start(f32[4,64,16,128]{3,2,1,0:T(8,128)} %bitcast.18), calls=%async_computation.6 | async-start | bytes 4194304 | tf_op jit(solution)/shard_map/all_to_all | solution.py:496
  202.5 5.4 %ortho.1 = f32[2048,256]{1,0:T(8,128)} custom-call(f32[2048,512]{1,0:T(8,128)} %bitcast.17, f32[512,256]{1,0:T(8,128)} %get-tuple-element.14.right_ref), custom_call_target="tpu_custom_call" | custom-call | tf_op jit(solution)/shard_map/ortho/pallas_call | solution.py:372
  207.9 21.9 %all-to-all-done.6 = f32[4,64,16,128]{3,2,1,0:T(8,128)S(1)} async-done(((f32[4,64,16,128]{3,2,1,0:T(8,128)}), f32[4,64,16,128]{3,2,1,0:T(8,128)S(1)}, u32[]{:S(2)}, u32[]{:S(2)}) %all-to-all-start.6) | async-done | bytes 2097184 | tf_op jit(solution)/shard_map/all_to_all | solution.py:496
  229.8 1.6 copy_bitcast_fusion
  (22 shorter events, 0.2 us)
Async XLA Ops:
  10.7 32.4 %copy-start.7 = (f32[3,16]{1,0:T(4,128)S(1)}, f32[3,16]{1,0:T(4,128)}, u32[]{:S(2)}) copy-start(f32[3,16]{1,0:T(4,128)} %param.13) | copy-start | bytes 580
  27.9 20.8 %all-to-all-start.1 = ((f32[128,8,128]{2,1,0:T(8,128)}), f32[128,8,128]{2,1,0:T(8,128)S(1)}, u32[]{:S(2)}, u32[]{:S(2)}) async-start(f32[128,8,128]{2,1,0:T(8,128)} %broadcast_in_dim.15), calls=%async_computation.1 | async-start | bytes 1048576 | tf_op jit(solution)/shard_map/all_to_all | solution.py:444
  37.0 2.7 %collective-permute-start = (f32[128,512]{1,0:T(8,128)S(1)}, f32[128,512]{1,0:T(8,128)S(1)}, u32[]{:S(2)}, u32[]{:S(2)}) collective-permute-start(f32[128,512]{1,0:T(8,128)S(1)} %bitcast.20), channel_id=1, source_target_pairs={{0,4},{4,8},{8,12},{12,16},{16,20},{20,24},{24,28},{28,32},{32,36}... | collective-permute-start | bytes 786440 | tf_op jit(solution)/shard_map/ppermute | solution.py:455
  38.4 4.7 %collective-permute-start.1 = (f32[128,512]{1,0:T(8,128)S(1)}, f32[128,512]{1,0:T(8,128)S(1)}, u32[]{:S(2)}, u32[]{:S(2)}) collective-permute-start(f32[128,512]{1,0:T(8,128)S(1)} %bitcast.21), channel_id=1, source_target_pairs={{4,0},{8,4},{12,8},{16,12},{20,16},{24,20},{28,24},{32,28},{36,32}... | collective-permute-start | bytes 786440 | tf_op jit(solution)/shard_map/ppermute | solution.py:456
  39.7 4.1 %copy-start.5 = (f32[128,512]{1,0:T(8,128)}, f32[128,512]{1,0:T(8,128)S(1)}, u32[]{:S(2)}) copy-start(f32[128,512]{1,0:T(8,128)S(1)} %collective-permute-done.below_ref) | copy-start | bytes 786436
  43.1 0.7 copy-start.6
  48.8 0.8 copy-start.1
  59.9 20.7 %all-to-all-start.2 = ((f32[32,8,128]{2,1,0:T(8,128)}), f32[32,8,128]{2,1,0:T(8,128)S(1)}, u32[]{:S(2)}, u32[]{:S(2)}) async-start(f32[32,8,128]{2,1,0:T(8,128)} %contract.3), calls=%async_computation.2 | async-start | bytes 262144 | tf_op jit(solution)/shard_map/all_to_all | solution.py:439
  78.6 34.7 %copy-start.4 = (f32[128,16,128]{2,1,0:T(8,128)S(1)}, f32[128,16,128]{2,1,0:T(8,128)}, u32[]{:S(2)}) copy-start(f32[128,16,128]{2,1,0:T(8,128)} %get-tuple-element.10.refs_1_) | copy-start | bytes 3145732
  78.7 34.7 %copy-start.3 = (f32[128,16,128]{2,1,0:T(8,128)S(1)}, f32[128,16,128]{2,1,0:T(8,128)}, u32[]{:S(2)}) copy-start(f32[128,16,128]{2,1,0:T(8,128)} %get-tuple-element.13.refs_4_) | copy-start | bytes 3145732
  80.6 19.6 %all-to-all-start.4 = ((f32[32,48,128]{2,1,0:T(8,128)}), f32[32,48,128]{2,1,0:T(8,128)S(1)}, u32[]{:S(2)}, u32[]{:S(2)}) async-start(f32[32,48,128]{2,1,0:T(8,128)} %gram.1), calls=%async_computation.4 | async-start | bytes 1572864 | tf_op jit(solution)/shard_map/all_to_all | solution.py:439
  101.0 54.5 %all-to-all-start.3 = ((f32[128,8,128]{2,1,0:T(8,128)}), f32[128,8,128]{2,1,0:T(8,128)S(1)}, u32[]{:S(2)}, u32[]{:S(2)}) async-start(f32[128,8,128]{2,1,0:T(8,128)} %broadcast_in_dim.17), calls=%async_computation.3 | async-start | bytes 1048576 | tf_op jit(solution)/shard_map/all_to_all | solution.py:444
  107.8 8.7 %collective-permute-start.4 = (f32[48,128]{1,0:T(8,128)S(1)}, f32[48,128]{1,0:T(8,128)S(1)}, u32[]{:S(2)}, u32[]{:S(2)}) collective-permute-start(f32[48,128]{1,0:T(8,128)S(1)} %reduce_sum.29), channel_id=1, source_target_pairs={{0,3},{1,0},{2,1},{3,2},{4,7},{5,4},{6,5},{7,6},{8,11},{9,8},{10,9... | collective-permute-start | bytes 73736 | tf_op jit(solution)/shard_map/ppermute | solution.py:449
  110.1 54.0 %collective-permute-start.6 = (f32[64,16,128]{2,1,0:T(8,128)}, f32[64,16,128]{2,1,0:T(8,128)}, u32[]{:S(2)}, u32[]{:S(2)}) collective-permute-start(f32[64,16,128]{2,1,0:T(8,128)} %get-tuple-element.11.refs_2_), channel_id=1, source_target_pairs={{0,1},{1,2},{2,3},{3,0},{4,5},{5,6},{6,7},{7,4},{8,9},{9,10},{10,1... | collective-permute-start | bytes 1572872 | tf_op jit(solution)/shard_map/ppermute | solution.py:449
  110.1 54.1 %collective-permute-start.8 = (f32[64,16,128]{2,1,0:T(8,128)}, f32[64,16,128]{2,1,0:T(8,128)}, u32[]{:S(2)}, u32[]{:S(2)}) collective-permute-start(f32[64,16,128]{2,1,0:T(8,128)} %get-tuple-element.12.refs_3_), channel_id=1, source_target_pairs={{0,3},{1,0},{2,1},{3,2},{4,7},{5,4},{6,5},{7,6},{8,11},{9,8},{10,9... | collective-permute-start | bytes 1572872 | tf_op jit(solution)/shard_map/ppermute | solution.py:449
  113.3 79.3 %collective-permute-start.5 = (f32[128,16,128]{2,1,0:T(8,128)S(1)}, f32[128,16,128]{2,1,0:T(8,128)}, u32[]{:S(2)}, u32[]{:S(2)}) collective-permute-start(f32[128,16,128]{2,1,0:T(8,128)S(1)} %copy-done.4), channel_id=1, source_target_pairs={{0,1},{1,2},{2,3},{3,0},{4,5},{5,6},{6,7},{7,4},{8,9},{9,10},{10,1... | collective-permute-start | bytes 3145736 | tf_op jit(solution)/shard_map/ppermute | solution.py:449
  113.3 79.3 %collective-permute-start.10 = (f32[128,16,128]{2,1,0:T(8,128)S(1)}, f32[128,16,128]{2,1,0:T(8,128)}, u32[]{:S(2)}, u32[]{:S(2)}) collective-permute-start(f32[128,16,128]{2,1,0:T(8,128)S(1)} %copy-done.3), channel_id=1, source_target_pairs={{0,3},{1,0},{2,1},{3,2},{4,7},{5,4},{6,5},{7,6},{8,11},{9,8},{10,9... | collective-permute-start | bytes 3145736 | tf_op jit(solution)/shard_map/ppermute | solution.py:449
  116.6 33.8 %collective-permute-start.3 = (f32[48,128]{1,0:T(8,128)S(1)}, f32[48,128]{1,0:T(8,128)S(1)}, u32[]{:S(2)}, u32[]{:S(2)}) collective-permute-start(f32[48,128]{1,0:T(8,128)S(1)} %reduce_sum.29), channel_id=1, source_target_pairs={{0,2},{1,3},{2,0},{3,1},{4,6},{5,7},{6,4},{7,5},{8,10},{9,11},{10,... | collective-permute-start | bytes 73736 | tf_op jit(solution)/shard_map/ppermute | solution.py:449
  150.4 5.0 %collective-permute-start.2 = (f32[48,128]{1,0:T(8,128)S(1)}, f32[48,128]{1,0:T(8,128)S(1)}, u32[]{:S(2)}, u32[]{:S(2)}) collective-permute-start(f32[48,128]{1,0:T(8,128)S(1)} %reduce_sum.29), channel_id=1, source_target_pairs={{0,1},{1,2},{2,3},{3,0},{4,5},{5,6},{6,7},{7,4},{8,9},{9,10},{10,1... | collective-permute-start | bytes 73736 | tf_op jit(solution)/shard_map/ppermute | solution.py:449
  155.5 22.5 %copy-start.2 = (f32[128,8,128]{2,1,0:T(8,128)}, f32[128,8,128]{2,1,0:T(8,128)S(1)}, u32[]{:S(2)}) copy-start(f32[128,8,128]{2,1,0:T(8,128)S(1)} %all-to-all-done.3.mid_ref) | copy-start | bytes 1572868
  156.4 21.5 %all-to-all-start.5 = ((f32[32,48,128]{2,1,0:T(8,128)}), f32[32,48,128]{2,1,0:T(8,128)S(1)}, u32[]{:S(2)}, u32[]{:S(2)}) async-start(f32[32,48,128]{2,1,0:T(8,128)} %broadcast_in_dim.18), calls=%async_computation.5 | async-start | bytes 1572864 | tf_op jit(solution)/shard_map/all_to_all | solution.py:444
  164.1 28.5 %collective-permute-start.7 = (f32[64,16,128]{2,1,0:T(8,128)}, f32[64,16,128]{2,1,0:T(8,128)}, u32[]{:S(2)}, u32[]{:S(2)}) collective-permute-start(f32[64,16,128]{2,1,0:T(8,128)} %collective-permute-done.6), channel_id=1, source_target_pairs={{0,1},{1,2},{2,3},{3,0},{4,5},{5,6},{6,7},{7,4},{8,9},{9,10},{10,1... | collective-permute-start | bytes 1572872 | tf_op jit(solution)/shard_map/ppermute | solution.py:449
  164.2 28.4 %collective-permute-start.9 = (f32[64,16,128]{2,1,0:T(8,128)}, f32[64,16,128]{2,1,0:T(8,128)}, u32[]{:S(2)}, u32[]{:S(2)}) collective-permute-start(f32[64,16,128]{2,1,0:T(8,128)} %collective-permute-done.8), channel_id=1, source_target_pairs={{0,3},{1,0},{2,1},{3,2},{4,7},{5,4},{6,5},{7,6},{8,11},{9,8},{10,9... | collective-permute-start | bytes 1572872 | tf_op jit(solution)/shard_map/ppermute | solution.py:449
  178.0 0.9 copy-start
  198.9 31.0 %all-to-all-start.6 = ((f32[4,64,16,128]{3,2,1,0:T(8,128)}), f32[4,64,16,128]{3,2,1,0:T(8,128)S(1)}, u32[]{:S(2)}, u32[]{:S(2)}) async-start(f32[4,64,16,128]{3,2,1,0:T(8,128)} %bitcast.18), calls=%async_computation.6 | async-start | bytes 4194304 | tf_op jit(solution)/shard_map/all_to_all | solution.py:496

commit v4 on v3

--- a/solution.py
+++ b/solution.py
@@ -19,8 +19,6 @@
 BLOCK = 64
 PIECES = (1, 1, 2, 1)
 STEPS = 4
-SKETCH_STEPS = 2
-GROUP = 16
 
 NN = (((1,), (0,)), ((), ()))
 NT = (((1,), (1,)), ((), ()))
@@ -86,29 +84,25 @@
     core_hbm, sketch_hbm, out_ref, *refs = refs[:count], refs[count], refs[count + 1], *refs[count + 2 :]
     core_refs, (sketch_ref, applied_ref, core_sems, sketch_sems) = refs[:count], refs[count:]
     peers = out_ref.shape[0]
-    slices = core_refs[0].shape[1]
-    rows = core_refs[0].shape[0]
-    pieces, sketch_rows = sketch_ref.shape[:2]
-    step = rows // STEPS
-
-    plan = []
+    pieces, groups, sketch_rows = sketch_ref.shape[:3]
+    slices = groups * TILE
+    rows = applied_ref.shape[1] // slices
+    step = core_refs[0].shape[0] // STEPS
+
+    arriving = []
     for k in range(STEPS):
-        at = 0
-        for split in core_parts or (1,):
-            n, begin = divmod(k * step, rows // split)
-            plan.append((k, at + n, pl.ds(begin, step)))
-            at += split
-    arriving = [
-        (k, index, lines, started(core_hbm[index].at[lines], core_refs[index].at[lines], core_sems.at[n]))
-        for n, (k, index, lines) in enumerate(plan)
+        lines = pl.ds(k * step, step)
+        for n, (hbm, ref) in enumerate(zip(core_hbm, core_refs)):
+            arriving.append((k, started(hbm.at[lines], ref.at[lines], core_sems.at[k * count + n])))
+    sketches_arriving = [
+        started(
+            sketch_hbm.at[:, pl.ds(g * TILE, TILE), pl.ds(h * LANES, LANES)],
+            sketch_ref.at[h, g],
+            sketch_sems.at[g * pieces + h],
+        )
+        for g in range(groups)
+        for h in range(pieces)
     ]
-    sketch_part = sketch_rows // SKETCH_STEPS
-    sketches_arriving = []
-    for c in range(SKETCH_STEPS):
-        lines = pl.ds(c * sketch_part, sketch_part)
-        for h in range(pieces):
-            source = sketch_hbm.at[lines, :, pl.ds(h * LANES, LANES)]
-            sketches_arriving.append(started(source, sketch_ref.at[h, lines], sketch_sems.at[c * pieces + h]))
 
     if core_parts:
         blocks = [lax.rem(rank_ref[0] + distance, len(core_parts)) for distance in range(len(core_parts))]
@@ -117,29 +111,48 @@
         part = part_ref[...]
     part = halves(part)
     for k in range(STEPS):
-        taken = []
-        for chunk, index, lines, copy in arriving:
+        for chunk, copy in arriving:
             if chunk == k:
                 copy.wait()
-                taken.append(core_refs[index][lines].reshape(step * slices, -1))
-        core = taken[0] if len(taken) == 1 else jnp.concatenate(taken, axis=1)
+        if core_parts:
+            slabs = []
+            for i in range(k * step, (k + 1) * step):
+                taken, blocks = list(core_refs), []
+                for split in core_parts:
+                    block = [taken.pop(0)[i] for _ in range(split)]
+                    blocks.append(block[0] if split == 1 else jnp.concatenate(block, axis=0))
+                slabs.append(jnp.concatenate(blocks, axis=1))
+            core = jnp.concatenate(slabs, axis=0)
+        else:
+            core = core_refs[0][pl.ds(k * step, step)].reshape(step * slices, -1)
         applied = dot3(halves(core), part, NN)
         for h in range(pieces):
-            applied_ref[h, pl.ds(k * step * slices, step * slices), :] = applied[:, h * LANES : (h + 1) * LANES]
+            own = applied[:, h * LANES : (h + 1) * LANES]
+            if core_parts:
+                applied_ref[h, pl.ds(k * step * rows, step * rows), :] = own
+                continue
+            own = own.reshape(step, groups, TILE, LANES)
+            for g in range(groups):
+                begin = (g * rows + k * step) * TILE
+                applied_ref[h, pl.ds(begin, step * TILE), :] = own[:, g].reshape(step * TILE, LANES)
     for copy in sketches_arriving:
         copy.wait()
-    sketches = [sketch_ref.at[h].reshape(sketch_rows * slices, LANES) for h in range(pieces)]
 
     def run(g, total):
         for i in range(TILE):
-            at = g * TILE + i
-            left = [applied_ref.at[h][pl.ds(at, rows, stride=slices), :] for h in range(pieces)]
-            right = [ref[pl.ds(at, sketch_rows, stride=slices), :] for ref in sketches]
+            if core_parts:
+                lines = pl.ds(pl.multiple_of((g * TILE + i) * rows, rows), rows)
+            else:
+                lines = pl.ds(g * rows * TILE + i, rows, stride=TILE)
+            left = [applied_ref.at[h][lines, :] for h in range(pieces)]
+            right = [
+                sketch_ref.at[h, g].reshape(sketch_rows * TILE, LANES)[pl.ds(i, sketch_rows, stride=TILE), :]
+                for h in range(pieces)
+            ]
             total += dot3(halves(jnp.concatenate(left, axis=1)), halves(jnp.concatenate(right, axis=1)), NT)
         return total
 
-    total = lax.fori_loop(0, slices // TILE, run, jnp.zeros((rows, sketch_rows), F32))
-    spread(out_ref, total)
+    spread(out_ref, lax.fori_loop(0, groups, run, jnp.zeros((rows, sketch_rows), F32)))
 
 
 SCALAR = pl.BlockSpec(memory_space=pltpu.SMEM)
@@ -148,8 +161,8 @@
 
 
 def contract_back(rank, cores, core_parts, part, sketch):
-    rows, slices = cores[0].shape[:2]
-    sketch_rows, _, sketch_cols = sketch.shape
+    sketch_rows, slices, sketch_cols = sketch.shape
+    rows = cores[0].shape[1 if core_parts else 0]
     pieces = sketch_cols // LANES
     peers = lax.axis_size(CUTS)
     shape = (peers, rows * sketch_rows // LANES // peers, LANES)
@@ -160,66 +173,77 @@
         out_shape=jax.ShapeDtypeStruct(shape, F32),
         scratch_shapes=[
             *[pltpu.VMEM(core.shape, F32) for core in cores],
-            pltpu.VMEM((pieces, sketch_rows, slices, LANES), F32),
+            pltpu.VMEM((pieces, slices // TILE, sketch_rows, TILE, LANES), F32),
             pltpu.VMEM((pieces, rows * slices, LANES), F32),
-            pltpu.SemaphoreType.DMA((STEPS * max(1, len(core_parts)),)),
-            pltpu.SemaphoreType.DMA((SKETCH_STEPS * pieces,)),
+            pltpu.SemaphoreType.DMA((STEPS * len(cores),)),
+            pltpu.SemaphoreType.DMA((pieces * slices // TILE,)),
         ],
         name="contract",
     )(rank, part, *cores, sketch)
 
 
-def stencil_kernel(pieces, rank_ref, core_hbm, below_ref, above_ref, coef_ref, *refs):
+def stencil_kernel(pieces, rank_ref, coef_ref, core_hbm, below_ref, above_ref, *refs):
     count = sum(pieces)
-    outs_hbm, core_all, step_refs, (in_sems, out_sems) = refs[:count], refs[count], refs[count + 1 : -2], refs[-2:]
-    total, slices, _ = core_all.shape
-    rows = GROUP
-    groups = total // rows
-    lines = [pl.ds(g * rows, rows) for g in range(groups)]
-    arriving = [started(core_hbm.at[lines[g]], core_all.at[lines[g]], in_sems.at[g]) for g in range(groups)]
-    place = lax.broadcasted_iota(jnp.int32, (rows * slices, LANES), 0) % slices
-    coef = [jnp.broadcast_to(coef_ref[k][None], (rows, slices, LANES)).reshape(rows * slices, LANES) for k in range(3)]
-    leaving = []
-    for g in range(groups):
-        arriving[g].wait()
-        at = 0
-        for distance, split in enumerate(pieces):
-            cols = pl.ds(own_block(rank_ref, distance, len(pieces)), LANES)
-            core = core_all[lines[g], :, cols].reshape(rows * slices, LANES)
-            first = jnp.broadcast_to(below_ref[lines[g], cols][:, None, :], (rows, slices, LANES))
-            last = jnp.broadcast_to(above_ref[lines[g], cols][:, None, :], (rows, slices, LANES))
-            below = jnp.where(place == 0, first.reshape(rows * slices, LANES), pltpu.roll(core, 1, 0))
-            above = jnp.where(
-                place == slices - 1, last.reshape(rows * slices, LANES), pltpu.roll(core, rows * slices - 1, 0)
+    outs_hbm, core_ref, step_refs, (in_sems, out_sems) = refs[:count], refs[count], refs[count + 1 : -2], refs[-2:]
+    groups, blocks, rows, _, _ = core_ref.shape
+    slices = groups * TILE
+    arriving = [
+        [
+            started(
+                core_hbm.at[:, pl.ds(g * TILE, TILE), pl.ds(own_block(rank_ref, distance, blocks), LANES)],
+                core_ref.at[g, distance],
+                in_sems.at[g * blocks + distance],
             )
-            stepped = (coef[0] * below + coef[1] * core + coef[2] * above).reshape(rows, slices, LANES)
-            n, begin = divmod(g * rows, total // split)
-            target = pl.ds(begin, rows)
-            step_refs[at + n][target] = stepped
-            sem = out_sems.at[g * len(pieces) + distance]
-            leaving.append(started(step_refs[at + n].at[target], outs_hbm[at + n].at[target], sem))
-            at += split
+            for g in range(groups)
+        ]
+        for distance in range(blocks)
+    ]
+    leaving, at = [], 0
+    for distance, split in enumerate(pieces):
+        for copy in arriving[distance]:
+            copy.wait()
+        cols = pl.ds(own_block(rank_ref, distance, blocks), LANES)
+
+        def slab(i, distance=distance, cols=cols):
+            if i < 0:
+                return below_ref[:, cols]
+            if i == slices:
+                return above_ref[:, cols]
+            flat = core_ref.at[i // TILE, distance].reshape(rows * TILE, LANES)
+            return flat[pl.ds(i % TILE, rows, stride=TILE), :]
+
+        below, core = slab(-1), slab(0)
+        part = rows // split
+        for i in range(slices):
+            above = slab(i + 1)
+            stepped = coef_ref[0, i] * below + coef_ref[1, i] * core + coef_ref[2, i] * above
+            for n in range(split):
+                step_refs[at + n][i] = stepped[n * part : (n + 1) * part]
+            below, core = core, above
+        for n in range(split):
+            leaving.append(started(step_refs[at + n], outs_hbm[at + n], out_sems.at[at + n]))
+        at += split
     for copy in leaving:
         copy.wait()
 
 
 def step_core(rank, core, below, above, stencil, pieces):
     rows, slices, _ = core.shape
-    coef = jnp.broadcast_to(stencil[:, :, None], (3, slices, LANES))
-    shapes = [(rows // split, slices, LANES) for split in pieces for _ in range(split)]
+    groups, blocks = slices // TILE, len(pieces)
+    shapes = [(slices, rows // split, LANES) for split in pieces for _ in range(split)]
     return pl.pallas_call(
         functools.partial(stencil_kernel, pieces),
-        in_specs=[SCALAR, IN_HBM, IN_VMEM, IN_VMEM, IN_VMEM],
+        in_specs=[SCALAR, SCALAR, IN_HBM, IN_VMEM, IN_VMEM],
         out_specs=[IN_HBM] * len(shapes),
         out_shape=[jax.ShapeDtypeStruct(shape, F32) for shape in shapes],
         scratch_shapes=[
-            pltpu.VMEM(core.shape, F32),
+            pltpu.VMEM((groups, blocks, rows, TILE, LANES), F32),
             *[pltpu.VMEM(shape, F32) for shape in shapes],
-            pltpu.SemaphoreType.DMA((rows // GROUP,)),
-            pltpu.SemaphoreType.DMA((rows // GROUP * len(pieces),)),
+            pltpu.SemaphoreType.DMA((groups * blocks,)),
+            pltpu.SemaphoreType.DMA((len(shapes),)),
         ],
         name="stencil",
-    )(rank, core, below, above, coef)
+    )(rank, stencil, core, below, above)
 
 
 def invert_factor(work_ref):
@@ -382,13 +406,16 @@
 def project_kernel(pieces, rank_ref, project_ref, *refs):
     count = sum(pieces)
     blocks_hbm, out_hbm, block_refs, (out_ref, in_sems, out_sems) = refs[:count], refs[count], refs[count + 1 : -3], refs[-3:]
-    slices = blocks_hbm[0].shape[1]
+    slices = blocks_hbm[0].shape[0]
     rows = project_ref.shape[0]
     ranks = len(pieces)
     groups = slices // TILE
     slabs = [pl.ds(g * TILE, TILE) for g in range(groups)]
     arriving = [
-        [started(hbm.at[:, slabs[g]], ref.at[g], in_sems.at[g * count + n]) for n, (hbm, ref) in enumerate(zip(blocks_hbm, block_refs))]
+        [
+            started(hbm.at[slabs[g]], ref.at[slabs[g]], in_sems.at[g * count + n])
+            for n, (hbm, ref) in enumerate(zip(blocks_hbm, block_refs))
+        ]
         for g in range(groups)
     ]
     project = halves(
@@ -401,14 +428,10 @@
     for g in range(groups):
         for copy in arriving[g]:
             copy.wait()
-        stepped = [(ref.at[g].reshape(-1, LANES), ref.shape[1]) for ref in block_refs]
         out = out_ref.at[g].reshape(rows * TILE, LANES)
-
-        def slab(i, stepped=stepped):
-            return jnp.concatenate([ref[pl.ds(i, length, stride=TILE), :] for ref, length in stepped], axis=0)
-
         for i in range(0, TILE, 2):
-            product = dot3(project, halves(jnp.concatenate([slab(i), slab(i + 1)], axis=1)), NN)
+            pair = [jnp.concatenate([ref[g * TILE + i + d] for ref in block_refs], axis=0) for d in range(2)]
+            product = dot3(project, halves(jnp.concatenate(pair, axis=1)), NN)
             for d in range(2):
                 out[pl.ds(i + d, rows, stride=TILE), :] = product[:, d * LANES : (d + 1) * LANES]
         leaving.append(started(out_ref.at[g], out_hbm.at[:, slabs[g]], out_sems.at[g]))
@@ -417,7 +440,7 @@
 
 
 def projected(rank, project, stepped, pieces):
-    slices = stepped[0].shape[1]
+    slices = stepped[0].shape[0]
     rows = project.shape[0]
     groups = slices // TILE
     return pl.pallas_call(
@@ -426,7 +449,7 @@
         out_specs=IN_HBM,
         out_shape=jax.ShapeDtypeStruct((rows, slices, LANES), F32),
         scratch_shapes=[
-            *[pltpu.VMEM((groups, block.shape[0], TILE, LANES), F32) for block in stepped],
+            *[pltpu.VMEM(block.shape, F32) for block in stepped],
             pltpu.VMEM((groups, rows, TILE, LANES), F32),
             pltpu.SemaphoreType.DMA((groups * len(stepped),)),
             pltpu.SemaphoreType.DMA((groups,)),

time: 233 us -> 231 us (level)
  no operation moved by 1% of the time
where the time goes in v4:
time: 231 us; the launch traced here: 229 us
  waiting for transfers between devices  87.5 us (38%)
  starting transfers between devices  60.5 us (26%)
  Pallas kernels  54.6 us (24%)
  blocking collectives  16.3 us (7%)
  local copies, waits for them, and re-layouts  9.42 us (4%)
    ppermute x9, waiting for transfers between devices, shifted(): lax.ppermute(array, 'rank', [(i, (i + distance) % count) for i in range(c...  35.9 us
    all_to_all x1, waiting for transfers between devices, step(): arrived = lax.all_to_all(blocks, 'rank', 0, 0, tiled=True)  21.9 us
    all_to_all x3, starting transfers between devices, copies_of(): return lax.all_to_all(copies, axes, 0, 0, tiled=True)  20.7 us
    pallas_call x2, Pallas kernels, contract_back(): pl.pallas_call(functools.partial(contract_kernel, core_parts), in_specs=[...  19.1 us
    all_to_all x2, starting transfers between devices, summed(): return jnp.sum(lax.all_to_all(pieces, axes, 0, 0, tiled=True), axis=0)  18.5 us
    all_to_all x1, blocking collectives, summed(): return jnp.sum(lax.all_to_all(pieces, axes, 0, 0, tiled=True), axis=0)  16.3 us
    all_to_all x2, waiting for transfers between devices, summed(): return jnp.sum(lax.all_to_all(pieces, axes, 0, 0, tiled=True), axis=0)  15.8 us
    ppermute x9, starting transfers between devices, shifted(): lax.ppermute(array, 'rank', [(i, (i + distance) % count) for i in range(c...  15 us
  transfers between devices with their start and end apart: 17, of which 7 were waited for; matrix products, arithmetic and copies ran while one was open for 2% of the time, Pallas kernels for 13%

profile of v4, /device:TPU:0, one launch (start us, length us, event | category | flops | bytes accessed | tf_op | source)
XLA Modules:
  0.0 229.4 jit_solution(8431350298472421384)
XLA Ops:
  0.6 9.6 %contract.2 = f32[32,8,128]{2,1,0:T(8,128)} custom-call(s32[1]{0:T(128)} %bitcast.1.rank_ref, f32[512,256]{1,0:T(8,128)} %part_ref.1, f32[128,16,512]{2,1,0:T(8,128)} %refs_0_.1, f32[256,16,256]{2,1,0:T(8,128)} %refs_1_.1), custom_call_target="tpu_custom_call" | custom-call | tf_op jit(solution)/shard_map/contract/pallas_call | solution.py:169
  10.2 16.3 %all_to_all.35 = f32[32,8,128]{2,1,0:T(8,128)S(1)} all-to-all(f32[32,8,128]{2,1,0:T(8,128)} %contract.2), channel_id=1, replica_groups=mesh['cuts_0'=4,'cuts_1'=4,'cuts_2'=2,'rank'=4] {'cuts_0','cuts_1','cuts..., dimensions={0} | all-to-all | bytes 262144 | tf_op jit(solution)/shard_map/all_to_all | solution.py:462
  26.6 0.8 broadcast_in_dim.9
  27.4 6.3 %all-to-all-start.1 = ((f32[128,8,128]{2,1,0:T(8,128)}), f32[128,8,128]{2,1,0:T(8,128)S(1)}, u32[]{:S(2)}, u32[]{:S(2)}) async-start(f32[128,8,128]{2,1,0:T(8,128)} %broadcast_in_dim.9), calls=%async_computation.1 | async-start | bytes 1048576 | tf_op jit(solution)/shard_map/all_to_all | solution.py:467
  33.7 2.7 %fusion = (f32[128,1,512]{2,1,0:T(1,128)S(1)}, f32[128,1,512]{2,1,0:T(1,128)S(1)}) fusion(f32[128,16,512]{2,1,0:T(8,128)} %core_hbm.1), kind=kLoop, calls=%fused_computation.4 | loop fusion | bytes 1048576 | tf_op jit(solution)/shard_map/slice | solution.py:477
  36.5 1.4 collective-permute-start
  37.9 1.3 collective-permute-start.1
  39.2 0.0 collective-permute-done.below_ref
  39.2 3.4 %collective-permute-done.1.above_ref = f32[128,512]{1,0:T(8,128)S(1)} collective-permute-done((f32[128,512]{1,0:T(8,128)S(1)}, f32[128,512]{1,0:T(8,128)S(1)}, u32[]{:S(2)}, u32[]{:S(2)}) %collective-permute-start.1) | collective-permute-done | bytes 262176 | tf_op jit(solution)/shard_map/ppermute | solution.py:479
  42.6 0.7 copy-done.6
  43.3 4.6 %stencil.1 = (f32[16,128,128]{2,1,0:T(8,128)}, f32[16,128,128]{2,1,0:T(8,128)}, f32[16,64,128]{2,1,0:T(8,128)}, f32[16,64,128]{2,1,0:T(8,128)}, f32[16,128,128]{2,1,0:T(8,128)}) custom-call(s32[1]{0:T(128)} %bitcast.1.rank_ref, f32[3,16]{1,0:T(4,128)} %coef_ref.1, f32[128,16,512]{2,1,0:T(8,128)} %core_hbm.1, f32[128,512]{1,0:T(8,128)} %copy-done.5, ...), custom_call_target="tpu_custom_call" | custom-call | tf_op jit(solution)/shard_map/stencil/pallas_call | solution.py:234
  47.9 0.0 all-to-all-done.1.part_ref
  47.9 0.8 copy-done.1
  48.7 9.6 %contract.3 = f32[32,8,128]{2,1,0:T(8,128)} custom-call(s32[1]{0:T(128)} %bitcast.1.rank_ref, f32[128,8,128]{2,1,0:T(8,128)} %copy-done.1, f32[16,128,128]{2,1,0:T(8,128)} %get-tuple-element.9.refs_0_, f32[16,128,128]{2,1,0:T(8,128)} %get-tuple-element.10.refs_1_, f32[16,64,128]{2,1,0:T(8,128)} %get-tuple-element.11.refs_2_, ...), custom_call_target="tpu_custom_call" | custom-call | tf_op jit(solution)/shard_map/contract/pallas_call | solution.py:169
  58.3 12.9 %all-to-all-start.2 = ((f32[32,8,128]{2,1,0:T(8,128)}), f32[32,8,128]{2,1,0:T(8,128)S(1)}, u32[]{:S(2)}, u32[]{:S(2)}) async-start(f32[32,8,128]{2,1,0:T(8,128)} %contract.3), calls=%async_computation.2 | async-start | bytes 262144 | tf_op jit(solution)/shard_map/all_to_all | solution.py:462
  71.2 5.9 %gram.1 = f32[32,48,128]{2,1,0:T(8,128)} custom-call(f32[2048,512]{1,0:T(8,128)} %bitcast.16), custom_call_target="tpu_custom_call" | custom-call | tf_op jit(solution)/shard_map/gram/pallas_call | solution.py:378
  77.1 0.0 copy-start.4
  77.1 1.9 all-to-all-done.2
  79.0 5.6 %all-to-all-start.4 = ((f32[32,48,128]{2,1,0:T(8,128)}), f32[32,48,128]{2,1,0:T(8,128)S(1)}, u32[]{:S(2)}, u32[]{:S(2)}) async-start(f32[32,48,128]{2,1,0:T(8,128)} %gram.1), calls=%async_computation.4 | async-start | bytes 1572864 | tf_op jit(solution)/shard_map/all_to_all | solution.py:462
  84.7 13.9 %all-to-all-done.4 = f32[32,48,128]{2,1,0:T(8,128)S(1)} async-done(((f32[32,48,128]{2,1,0:T(8,128)}), f32[32,48,128]{2,1,0:T(8,128)S(1)}, u32[]{:S(2)}, u32[]{:S(2)}) %all-to-all-start.4) | async-done | bytes 786464 | tf_op jit(solution)/shard_map/all_to_all | solution.py:462
  98.6 0.8 broadcast_in_dim.10
  99.4 6.8 %all-to-all-start.3 = ((f32[128,8,128]{2,1,0:T(8,128)}), f32[128,8,128]{2,1,0:T(8,128)S(1)}, u32[]{:S(2)}, u32[]{:S(2)}) async-start(f32[128,8,128]{2,1,0:T(8,128)} %broadcast_in_dim.10), calls=%async_computation.3 | async-start | bytes 1048576 | tf_op jit(solution)/shard_map/all_to_all | solution.py:467
  106.2 0.1 reduce_sum.29
  106.3 2.2 collective-permute-start.4
  108.5 0.0 collective-permute-start.6
  108.5 3.2 %collective-permute-start.8 = (f32[16,64,128]{2,1,0:T(8,128)}, f32[16,64,128]{2,1,0:T(8,128)}, u32[]{:S(2)}, u32[]{:S(2)}) collective-permute-start(f32[16,64,128]{2,1,0:T(8,128)} %get-tuple-element.12.refs_3_), channel_id=1, source_target_pairs={{0,3},{1,0},{2,1},{3,2},{4,7},{5,4},{6,5},{7,6},{8,11},{9,8},{10,9... | collective-permute-start | bytes 1572872 | tf_op jit(solution)/shard_map/ppermute | solution.py:472
  111.8 0.0 collective-permute-start.5
  111.8 3.2 %collective-permute-start.10 = (f32[16,128,128]{2,1,0:T(8,128)S(1)}, f32[16,128,128]{2,1,0:T(8,128)}, u32[]{:S(2)}, u32[]{:S(2)}) collective-permute-start(f32[16,128,128]{2,1,0:T(8,128)S(1)} %copy-done.3), channel_id=1, source_target_pairs={{0,3},{1,0},{2,1},{3,2},{4,7},{5,4},{6,5},{7,6},{8,11},{9,8},{10,9... | collective-permute-start | bytes 3145736 | tf_op jit(solution)/shard_map/ppermute | solution.py:472
  115.0 0.0 collective-permute-done.4
  115.0 1.9 collective-permute-start.3
  116.9 32.0 %collective-permute-done.3 = f32[48,128]{1,0:T(8,128)S(1)} collective-permute-done((f32[48,128]{1,0:T(8,128)S(1)}, f32[48,128]{1,0:T(8,128)S(1)}, u32[]{:S(2)}, u32[]{:S(2)}) %collective-permute-start.3) | collective-permute-done | bytes 24608 | tf_op jit(solution)/shard_map/ppermute | solution.py:472
  148.8 1.1 collective-permute-start.2
  149.9 3.9 %collective-permute-done.2 = f32[48,128]{1,0:T(8,128)S(1)} collective-permute-done((f32[48,128]{1,0:T(8,128)S(1)}, f32[48,128]{1,0:T(8,128)S(1)}, u32[]{:S(2)}, u32[]{:S(2)}) %collective-permute-start.2) | collective-permute-done | bytes 24608 | tf_op jit(solution)/shard_map/ppermute | solution.py:472
  153.9 1.0 broadcast_in_dim.11
  154.9 7.6 %all-to-all-start.5 = ((f32[32,48,128]{2,1,0:T(8,128)}), f32[32,48,128]{2,1,0:T(8,128)S(1)}, u32[]{:S(2)}, u32[]{:S(2)}) async-start(f32[32,48,128]{2,1,0:T(8,128)} %broadcast_in_dim.11), calls=%async_computation.5 | async-start | bytes 1572864 | tf_op jit(solution)/shard_map/all_to_all | solution.py:467
  162.5 0.0 collective-permute-done.6
  162.5 0.1 collective-permute-start.7
  162.6 3.2 %collective-permute-start.9 = (f32[16,64,128]{2,1,0:T(8,128)}, f32[16,64,128]{2,1,0:T(8,128)}, u32[]{:S(2)}, u32[]{:S(2)}) collective-permute-start(f32[16,64,128]{2,1,0:T(8,128)} %collective-permute-done.8), channel_id=1, source_target_pairs={{0,3},{1,0},{2,1},{3,2},{4,7},{5,4},{6,5},{7,6},{8,11},{9,8},{10,9... | collective-permute-start | bytes 1572872 | tf_op jit(solution)/shard_map/ppermute | solution.py:472
  165.8 10.6 %all-to-all-done.5.gram_ref = f32[32,48,128]{2,1,0:T(8,128)S(1)} async-done(((f32[32,48,128]{2,1,0:T(8,128)}), f32[32,48,128]{2,1,0:T(8,128)S(1)}, u32[]{:S(2)}, u32[]{:S(2)}) %all-to-all-start.5) | async-done | bytes 786464 | tf_op jit(solution)/shard_map/all_to_all | solution.py:467
  176.4 0.9 copy-done
  177.3 13.7 %factor.1 = (f32[512,256]{1,0:T(8,128)}, f32[256,512]{1,0:T(8,128)}) custom-call(f32[128,8,128]{2,1,0:T(8,128)} %copy-done.2, f32[32,48,128]{2,1,0:T(8,128)} %copy-done), custom_call_target="tpu_custom_call" | custom-call | tf_op jit(solution)/shard_map/factor/pallas_call | solution.py:333
  191.0 0.0 collective-permute-done.7.refs_2_
  191.0 0.0 collective-permute-done.9.refs_3_
  191.1 5.8 %project.1 = f32[256,16,128]{2,1,0:T(8,128)} custom-call(s32[1]{0:T(128)} %bitcast.1.rank_ref, f32[256,512]{1,0:T(8,128)} %get-tuple-element.15.project_ref, f32[16,128,128]{2,1,0:T(8,128)} %get-tuple-element.9.refs_0_, f32[16,128,128]{2,1,0:T(8,128)} %collective-permute-done.5.refs_1_, f32[16,64,128]{2,1,0:T(8,128)} %collective-permute-done.7.refs_2_, ...), custom_call_target="tpu_custom_call" | custom-call | tf_op jit(solution)/shard_map/project/pallas_call | solution.py:446
  196.8 3.6 %all-to-all-start.6 = ((f32[4,64,16,128]{3,2,1,0:T(8,128)}), f32[4,64,16,128]{3,2,1,0:T(8,128)S(1)}, u32[]{:S(2)}, u32[]{:S(2)}) async-start(f32[4,64,16,128]{3,2,1,0:T(8,128)} %bitcast.18), calls=%async_computation.6 | async-start | bytes 4194304 | tf_op jit(solution)/shard_map/all_to_all | solution.py:519
  200.5 5.4 %ortho.1 = f32[2048,256]{1,0:T(8,128)} custom-call(f32[2048,512]{1,0:T(8,128)} %bitcast.17, f32[512,256]{1,0:T(8,128)} %get-tuple-element.14.right_ref), custom_call_target="tpu_custom_call" | custom-call | tf_op jit(solution)/shard_map/ortho/pallas_call | solution.py:396
  205.9 21.9 %all-to-all-done.6 = f32[4,64,16,128]{3,2,1,0:T(8,128)S(1)} async-done(((f32[4,64,16,128]{3,2,1,0:T(8,128)}), f32[4,64,16,128]{3,2,1,0:T(8,128)S(1)}, u32[]{:S(2)}, u32[]{:S(2)}) %all-to-all-start.6) | async-done | bytes 2097184 | tf_op jit(solution)/shard_map/all_to_all | solution.py:519
  227.8 1.6 copy_bitcast_fusion
  (19 shorter events, 0.1 us)
Async XLA Ops:
  27.4 20.5 %all-to-all-start.1 = ((f32[128,8,128]{2,1,0:T(8,128)}), f32[128,8,128]{2,1,0:T(8,128)S(1)}, u32[]{:S(2)}, u32[]{:S(2)}) async-start(f32[128,8,128]{2,1,0:T(8,128)} %broadcast_in_dim.9), calls=%async_computation.1 | async-start | bytes 1048576 | tf_op jit(solution)/shard_map/all_to_all | solution.py:467
  36.5 2.7 %collective-permute-start = (f32[128,512]{1,0:T(8,128)S(1)}, f32[128,512]{1,0:T(8,128)S(1)}, u32[]{:S(2)}, u32[]{:S(2)}) collective-permute-start(f32[128,512]{1,0:T(8,128)S(1)} %bitcast.20), channel_id=1, source_target_pairs={{0,4},{4,8},{8,12},{12,16},{16,20},{20,24},{24,28},{28,32},{32,36}... | collective-permute-start | bytes 786440 | tf_op jit(solution)/shard_map/ppermute | solution.py:478
  37.9 4.7 %collective-permute-start.1 = (f32[128,512]{1,0:T(8,128)S(1)}, f32[128,512]{1,0:T(8,128)S(1)}, u32[]{:S(2)}, u32[]{:S(2)}) collective-permute-start(f32[128,512]{1,0:T(8,128)S(1)} %bitcast.21), channel_id=1, source_target_pairs={{4,0},{8,4},{12,8},{16,12},{20,16},{24,20},{28,24},{32,28},{36,32}... | collective-permute-start | bytes 786440 | tf_op jit(solution)/shard_map/ppermute | solution.py:479
  39.2 3.4 %copy-start.5 = (f32[128,512]{1,0:T(8,128)}, f32[128,512]{1,0:T(8,128)S(1)}, u32[]{:S(2)}) copy-start(f32[128,512]{1,0:T(8,128)S(1)} %collective-permute-done.below_ref) | copy-start | bytes 786436
  42.6 0.7 copy-start.6
  47.9 0.8 copy-start.1
  58.3 20.7 %all-to-all-start.2 = ((f32[32,8,128]{2,1,0:T(8,128)}), f32[32,8,128]{2,1,0:T(8,128)S(1)}, u32[]{:S(2)}, u32[]{:S(2)}) async-start(f32[32,8,128]{2,1,0:T(8,128)} %contract.3), calls=%async_computation.2 | async-start | bytes 262144 | tf_op jit(solution)/shard_map/all_to_all | solution.py:462
  77.1 34.7 %copy-start.4 = (f32[16,128,128]{2,1,0:T(8,128)S(1)}, f32[16,128,128]{2,1,0:T(8,128)}, u32[]{:S(2)}) copy-start(f32[16,128,128]{2,1,0:T(8,128)} %get-tuple-element.10.refs_1_) | copy-start | bytes 3145732
  77.1 34.7 %copy-start.3 = (f32[16,128,128]{2,1,0:T(8,128)S(1)}, f32[16,128,128]{2,1,0:T(8,128)}, u32[]{:S(2)}) copy-start(f32[16,128,128]{2,1,0:T(8,128)} %get-tuple-element.13.refs_4_) | copy-start | bytes 3145732
  79.0 19.6 %all-to-all-start.4 = ((f32[32,48,128]{2,1,0:T(8,128)}), f32[32,48,128]{2,1,0:T(8,128)S(1)}, u32[]{:S(2)}, u32[]{:S(2)}) async-start(f32[32,48,128]{2,1,0:T(8,128)} %gram.1), calls=%async_computation.4 | async-start | bytes 1572864 | tf_op jit(solution)/shard_map/all_to_all | solution.py:462
  99.4 54.5 %all-to-all-start.3 = ((f32[128,8,128]{2,1,0:T(8,128)}), f32[128,8,128]{2,1,0:T(8,128)S(1)}, u32[]{:S(2)}, u32[]{:S(2)}) async-start(f32[128,8,128]{2,1,0:T(8,128)} %broadcast_in_dim.10), calls=%async_computation.3 | async-start | bytes 1048576 | tf_op jit(solution)/shard_map/all_to_all | solution.py:467
  106.3 8.7 %collective-permute-start.4 = (f32[48,128]{1,0:T(8,128)S(1)}, f32[48,128]{1,0:T(8,128)S(1)}, u32[]{:S(2)}, u32[]{:S(2)}) collective-permute-start(f32[48,128]{1,0:T(8,128)S(1)} %reduce_sum.29), channel_id=1, source_target_pairs={{0,3},{1,0},{2,1},{3,2},{4,7},{5,4},{6,5},{7,6},{8,11},{9,8},{10,9... | collective-permute-start | bytes 73736 | tf_op jit(solution)/shard_map/ppermute | solution.py:472
  108.5 54.0 %collective-permute-start.6 = (f32[16,64,128]{2,1,0:T(8,128)}, f32[16,64,128]{2,1,0:T(8,128)}, u32[]{:S(2)}, u32[]{:S(2)}) collective-permute-start(f32[16,64,128]{2,1,0:T(8,128)} %get-tuple-element.11.refs_2_), channel_id=1, source_target_pairs={{0,1},{1,2},{2,3},{3,0},{4,5},{5,6},{6,7},{7,4},{8,9},{9,10},{10,1... | collective-permute-start | bytes 1572872 | tf_op jit(solution)/shard_map/ppermute | solution.py:472
  108.5 54.1 %collective-permute-start.8 = (f32[16,64,128]{2,1,0:T(8,128)}, f32[16,64,128]{2,1,0:T(8,128)}, u32[]{:S(2)}, u32[]{:S(2)}) collective-permute-start(f32[16,64,128]{2,1,0:T(8,128)} %get-tuple-element.12.refs_3_), channel_id=1, source_target_pairs={{0,3},{1,0},{2,1},{3,2},{4,7},{5,4},{6,5},{7,6},{8,11},{9,8},{10,9... | collective-permute-start | bytes 1572872 | tf_op jit(solution)/shard_map/ppermute | solution.py:472
  111.8 79.3 %collective-permute-start.5 = (f32[16,128,128]{2,1,0:T(8,128)S(1)}, f32[16,128,128]{2,1,0:T(8,128)}, u32[]{:S(2)}, u32[]{:S(2)}) collective-permute-start(f32[16,128,128]{2,1,0:T(8,128)S(1)} %copy-done.4), channel_id=1, source_target_pairs={{0,1},{1,2},{2,3},{3,0},{4,5},{5,6},{6,7},{7,4},{8,9},{9,10},{10,1... | collective-permute-start | bytes 3145736 | tf_op jit(solution)/shard_map/ppermute | solution.py:472
  111.8 79.3 %collective-permute-start.10 = (f32[16,128,128]{2,1,0:T(8,128)S(1)}, f32[16,128,128]{2,1,0:T(8,128)}, u32[]{:S(2)}, u32[]{:S(2)}) collective-permute-start(f32[16,128,128]{2,1,0:T(8,128)S(1)} %copy-done.3), channel_id=1, source_target_pairs={{0,3},{1,0},{2,1},{3,2},{4,7},{5,4},{6,5},{7,6},{8,11},{9,8},{10,9... | collective-permute-start | bytes 3145736 | tf_op jit(solution)/shard_map/ppermute | solution.py:472
  115.0 33.8 %collective-permute-start.3 = (f32[48,128]{1,0:T(8,128)S(1)}, f32[48,128]{1,0:T(8,128)S(1)}, u32[]{:S(2)}, u32[]{:S(2)}) collective-permute-start(f32[48,128]{1,0:T(8,128)S(1)} %reduce_sum.29), channel_id=1, source_target_pairs={{0,2},{1,3},{2,0},{3,1},{4,6},{5,7},{6,4},{7,5},{8,10},{9,11},{10,... | collective-permute-start | bytes 73736 | tf_op jit(solution)/shard_map/ppermute | solution.py:472
  148.8 5.0 %collective-permute-start.2 = (f32[48,128]{1,0:T(8,128)S(1)}, f32[48,128]{1,0:T(8,128)S(1)}, u32[]{:S(2)}, u32[]{:S(2)}) collective-permute-start(f32[48,128]{1,0:T(8,128)S(1)} %reduce_sum.29), channel_id=1, source_target_pairs={{0,1},{1,2},{2,3},{3,0},{4,5},{5,6},{6,7},{7,4},{8,9},{9,10},{10,1... | collective-permute-start | bytes 73736 | tf_op jit(solution)/shard_map/ppermute | solution.py:472
  153.9 22.5 %copy-start.2 = (f32[128,8,128]{2,1,0:T(8,128)}, f32[128,8,128]{2,1,0:T(8,128)S(1)}, u32[]{:S(2)}) copy-start(f32[128,8,128]{2,1,0:T(8,128)S(1)} %all-to-all-done.3.mid_ref) | copy-start | bytes 1572868
  154.9 21.5 %all-to-all-start.5 = ((f32[32,48,128]{2,1,0:T(8,128)}), f32[32,48,128]{2,1,0:T(8,128)S(1)}, u32[]{:S(2)}, u32[]{:S(2)}) async-start(f32[32,48,128]{2,1,0:T(8,128)} %broadcast_in_dim.11), calls=%async_computation.5 | async-start | bytes 1572864 | tf_op jit(solution)/shard_map/all_to_all | solution.py:467
  162.5 28.5 %collective-permute-start.7 = (f32[16,64,128]{2,1,0:T(8,128)}, f32[16,64,128]{2,1,0:T(8,128)}, u32[]{:S(2)}, u32[]{:S(2)}) collective-permute-start(f32[16,64,128]{2,1,0:T(8,128)} %collective-permute-done.6), channel_id=1, source_target_pairs={{0,1},{1,2},{2,3},{3,0},{4,5},{5,6},{6,7},{7,4},{8,9},{9,10},{10,1... | collective-permute-start | bytes 1572872 | tf_op jit(solution)/shard_map/ppermute | solution.py:472
  162.6 28.4 %collective-permute-start.9 = (f32[16,64,128]{2,1,0:T(8,128)}, f32[16,64,128]{2,1,0:T(8,128)}, u32[]{:S(2)}, u32[]{:S(2)}) collective-permute-start(f32[16,64,128]{2,1,0:T(8,128)} %collective-permute-done.8), channel_id=1, source_target_pairs={{0,3},{1,0},{2,1},{3,2},{4,7},{5,4},{6,5},{7,6},{8,11},{9,8},{10,9... | collective-permute-start | bytes 1572872 | tf_op jit(solution)/shard_map/ppermute | solution.py:472
  176.4 0.9 copy-start
  196.8 31.0 %all-to-all-start.6 = ((f32[4,64,16,128]{3,2,1,0:T(8,128)}), f32[4,64,16,128]{3,2,1,0:T(8,128)S(1)}, u32[]{:S(2)}, u32[]{:S(2)}) async-start(f32[4,64,16,128]{3,2,1,0:T(8,128)} %bitcast.18), calls=%async_computation.6 | async-start | bytes 4194304 | tf_op jit(solution)/shard_map/all_to_all | solution.py:519

commit v5 on v4

--- a/solution.py
+++ b/solution.py
@@ -324,8 +324,9 @@
     row = lax.broadcasted_iota(jnp.int32, work_ref.shape, 0)
     col = lax.broadcasted_iota(jnp.int32, work_ref.shape, 1)
     inverse = jnp.where(row >= col, work_ref[...], 0.0)
-    left_ref[...] = exact(mid, inverse, NT) * scale
-    project_ref[...] = exact(inverse, cross, NT)
+    inverse = halves(inverse)
+    left_ref[...] = dot3(halves(mid), inverse, NT) * scale
+    project_ref[...] = dot3(inverse, halves(cross), NT)
 
 
 def factored(mid_sum, gram_left, scale, rank_width):
@@ -500,12 +501,12 @@
     far_down = shifted(far_down, -1)
 
     gram_left = packed_gram(flat_left)
-    gram_left = summed(gram_left, CUTS)
+    right_part = contract_back(rank, [core_right], (), tail_sketch, sketch_right)
+    height = right_part.shape[1]
+    sums = summed(jnp.concatenate([right_part, gram_left], axis=1), CUTS)
+    right_sum, gram_left = sums[:height], sums[height:]
     gram_left = sum([shifted(gram_left, d) for d in range(1, ranks)], gram_left)
     gram_left = copies_of(gram_left, CUTS)
-
-    right_part = contract_back(rank, [core_right], (), tail_sketch, sketch_right)
-    right_sum = summed(right_part, CUTS)
     right_sum = copies_of(right_sum, EVERY)
 
     mid_part = contract_back(rank, stepped, PIECES, right_sum, sketch_mid)

time: 231 us -> 212 us (0.918)
  waiting for transfers between devices: 87.5 us -> 38 us
  blocking collectives: 16.3 us -> 64.5 us
  starting transfers between devices: 60.5 us -> 42.5 us
    all_to_all x0 -> x1, blocking collectives: none -> 41 us  [copies_of(): return lax.all_to_all(copies, axes, 0, 0, tiled=True)]
    ppermute x9, waiting for transfers between devices: 35.9 us -> 9.86 us  [shifted(): lax.ppermute(array, 'rank', [(i, (i + distance) % count) for i in range(c...]
    all_to_all x3 -> x2, waiting for transfers between devices: 10.6 us -> 0.01 us  [copies_of(): return lax.all_to_all(copies, axes, 0, 0, tiled=True)]
    all_to_all x3 -> x2, starting transfers between devices: 20.7 us -> 10.8 us  [copies_of(): return lax.all_to_all(copies, axes, 0, 0, tiled=True)]
    all_to_all x2 -> x1, starting transfers between devices: 18.5 us -> 10.4 us  [summed(): return jnp.sum(lax.all_to_all(pieces, axes, 0, 0, tiled=True), axis=0)]
    all_to_all x2 -> x1, waiting for transfers between devices: 15.8 us -> 7.78 us  [summed(): return jnp.sum(lax.all_to_all(pieces, axes, 0, 0, tiled=True), axis=0)]
    all_to_all x1, blocking collectives: 16.3 us -> 23.6 us  [summed(): return jnp.sum(lax.all_to_all(pieces, axes, 0, 0, tiled=True), axis=0)]
    ppermute x1, waiting for transfers between devices: 3.35 us -> 0.01 us  [neighbours(): above = lax.ppermute(head, CUTS, [(i + 1, i) for i in range(count - 1)])]
  transfers between devices with their start and end apart: 17 -> 15, of which waited for: 7 -> 3; matrix products, arithmetic and copies ran while one was open for 2% -> 1% of each run, Pallas kernels for 13% -> 16%
where the time goes in v5:
time: 212 us; the launch traced here: 211 us
  blocking collectives  64.5 us (30%)
  Pallas kernels  54.7 us (26%)
  starting transfers between devices  42.5 us (20%)
  waiting for transfers between devices  38 us (18%)
  local copies, waits for them, and re-layouts  9.21 us (4%)
    all_to_all x1, blocking collectives, copies_of(): return lax.all_to_all(copies, axes, 0, 0, tiled=True)  41 us
    all_to_all x1, blocking collectives, summed(): return jnp.sum(lax.all_to_all(pieces, axes, 0, 0, tiled=True), axis=0)  23.6 us
    all_to_all x1, waiting for transfers between devices, step(): arrived = lax.all_to_all(blocks, 'rank', 0, 0, tiled=True)  20.3 us
    pallas_call x2, Pallas kernels, contract_back(): pl.pallas_call(functools.partial(contract_kernel, core_parts), in_specs=[...  19.2 us
    ppermute x9, starting transfers between devices, shifted(): lax.ppermute(array, 'rank', [(i, (i + distance) % count) for i in range(c...  15 us
    pallas_call x1, Pallas kernels, factored(): pl.pallas_call(functools.partial(factor_kernel, scale), out_shape=(jax.Sh...  13.7 us
    all_to_all x2, starting transfers between devices, copies_of(): return lax.all_to_all(copies, axes, 0, 0, tiled=True)  10.8 us
    all_to_all x1, starting transfers between devices, summed(): return jnp.sum(lax.all_to_all(pieces, axes, 0, 0, tiled=True), axis=0)  10.4 us
  transfers between devices with their start and end apart: 15, of which 3 were waited for; matrix products, arithmetic and copies ran while one was open for 1% of the time, Pallas kernels for 16%

profile of v5, /device:TPU:0, one launch (start us, length us, event | category | flops | bytes accessed | tf_op | source)
XLA Modules:
  0.0 210.9 jit_solution(4372190139672394258)
XLA Ops:
  0.6 5.9 %gram.1 = f32[32,48,128]{2,1,0:T(8,128)} custom-call(f32[2048,512]{1,0:T(8,128)} %bitcast.16), custom_call_target="tpu_custom_call" | custom-call | tf_op jit(solution)/shard_map/gram/pallas_call | solution.py:379
  6.5 0.0 copy-start
  6.5 9.7 %contract.2 = f32[32,8,128]{2,1,0:T(8,128)} custom-call(s32[1]{0:T(128)} %bitcast.1.rank_ref, f32[512,256]{1,0:T(8,128)} %part_ref.1, f32[128,16,512]{2,1,0:T(8,128)} %refs_0_.1, f32[256,16,256]{2,1,0:T(8,128)} %refs_1_.1), custom_call_target="tpu_custom_call" | custom-call | tf_op jit(solution)/shard_map/contract/pallas_call | solution.py:169
  16.2 1.0 pad_maximum_fusion
  17.2 23.6 %all_to_all.30 = f32[32,56,128]{2,1,0:T(8,128)S(1)} all-to-all(f32[32,56,128]{2,1,0:T(8,128)S(1)} %pad_maximum_fusion), channel_id=1, replica_groups=mesh['cuts_0'=4,'cuts_1'=4,'cuts_2'=2,'rank'=4] {'cuts_0','cuts_1','cuts..., dimensions={0} | all-to-all | bytes 1835008 | tf_op jit(solution)/shard_map/all_to_all | solution.py:463
  40.7 0.1 reduce_sum.18
  40.8 0.8 broadcast_in_dim.9
  41.7 6.9 %all-to-all-start.1 = ((f32[128,8,128]{2,1,0:T(8,128)}), f32[128,8,128]{2,1,0:T(8,128)S(1)}, u32[]{:S(2)}, u32[]{:S(2)}) async-start(f32[128,8,128]{2,1,0:T(8,128)} %broadcast_in_dim.9), calls=%async_computation.1 | async-start | bytes 1048576 | tf_op jit(solution)/shard_map/all_to_all | solution.py:468
  48.5 2.7 %fusion = (f32[128,1,512]{2,1,0:T(1,128)S(1)}, f32[128,1,512]{2,1,0:T(1,128)S(1)}) fusion(f32[128,16,512]{2,1,0:T(8,128)} %core_hbm.1), kind=kLoop, calls=%fused_computation.5 | loop fusion | bytes 1048576 | tf_op jit(solution)/shard_map/slice | solution.py:478
  51.3 1.4 collective-permute-start
  52.7 1.3 collective-permute-start.1
  54.0 3.2 %collective-permute-start.3 = (f32[48,128]{1,0:T(8,128)S(1)}, f32[48,128]{1,0:T(8,128)S(1)}, u32[]{:S(2)}, u32[]{:S(2)}) collective-permute-start(f32[48,128]{1,0:T(8,128)S(1)} %slice.17), channel_id=1, source_target_pairs={{0,2},{1,3},{2,0},{3,1},{4,6},{5,7},{6,4},{7,5},{8,10},{9,11},{10,... | collective-permute-start | bytes 73736 | tf_op jit(solution)/shard_map/ppermute | solution.py:473
  57.2 1.2 collective-permute-start.4
  58.4 0.9 collective-permute-start.2
  59.2 0.0 collective-permute-done.below_ref
  59.3 0.0 collective-permute-done.1.above_ref
  59.3 0.7 copy-done.7
  60.0 0.7 copy-done.8
  60.7 4.7 %stencil.1 = (f32[16,128,128]{2,1,0:T(8,128)}, f32[16,128,128]{2,1,0:T(8,128)}, f32[16,64,128]{2,1,0:T(8,128)}, f32[16,64,128]{2,1,0:T(8,128)}, f32[16,128,128]{2,1,0:T(8,128)}) custom-call(s32[1]{0:T(128)} %bitcast.1.rank_ref, f32[3,16]{1,0:T(4,128)} %coef_ref.1, f32[128,16,512]{2,1,0:T(8,128)} %core_hbm.1, f32[128,512]{1,0:T(8,128)} %copy-done.7, ...), custom_call_target="tpu_custom_call" | custom-call | tf_op jit(solution)/shard_map/stencil/pallas_call | solution.py:234
  65.3 0.0 all-to-all-done.1.part_ref
  65.4 0.8 copy-done.2
  66.2 9.6 %contract.3 = f32[32,8,128]{2,1,0:T(8,128)} custom-call(s32[1]{0:T(128)} %bitcast.1.rank_ref, f32[128,8,128]{2,1,0:T(8,128)} %copy-done.2, f32[16,128,128]{2,1,0:T(8,128)} %get-tuple-element.9.refs_0_, f32[16,128,128]{2,1,0:T(8,128)} %get-tuple-element.10.refs_1_, f32[16,64,128]{2,1,0:T(8,128)} %get-tuple-element.11.refs_2_, ...), custom_call_target="tpu_custom_call" | custom-call | tf_op jit(solution)/shard_map/contract/pallas_call | solution.py:169
  75.7 0.0 copy-start.4
  75.8 10.4 %all-to-all-start.2 = ((f32[32,8,128]{2,1,0:T(8,128)}), f32[32,8,128]{2,1,0:T(8,128)S(1)}, u32[]{:S(2)}, u32[]{:S(2)}) async-start(f32[32,8,128]{2,1,0:T(8,128)} %contract.3), calls=%async_computation.2 | async-start | bytes 262144 | tf_op jit(solution)/shard_map/all_to_all | solution.py:463
  86.2 0.0 collective-permute-done.3
  86.2 0.0 collective-permute-done.4
  86.2 7.8 %all-to-all-done.2 = f32[32,8,128]{2,1,0:T(8,128)S(1)} async-done(((f32[32,8,128]{2,1,0:T(8,128)}), f32[32,8,128]{2,1,0:T(8,128)S(1)}, u32[]{:S(2)}, u32[]{:S(2)}) %all-to-all-start.2) | async-done | bytes 131104 | tf_op jit(solution)/shard_map/all_to_all | solution.py:463
  94.0 0.9 broadcast_in_dim.11
  94.9 3.9 %all-to-all-start.4 = ((f32[32,48,128]{2,1,0:T(8,128)}), f32[32,48,128]{2,1,0:T(8,128)S(1)}, u32[]{:S(2)}, u32[]{:S(2)}) async-start(f32[32,48,128]{2,1,0:T(8,128)} %broadcast_in_dim.11), calls=%async_computation.4 | async-start | bytes 1572864 | tf_op jit(solution)/shard_map/all_to_all | solution.py:468
  98.9 1.6 collective-permute-start.6
  100.4 1.7 collective-permute-start.8
  102.2 0.3 collective-permute-start.5
  102.5 3.0 %collective-permute-start.10 = (f32[16,128,128]{2,1,0:T(8,128)S(1)}, f32[16,128,128]{2,1,0:T(8,128)}, u32[]{:S(2)}, u32[]{:S(2)}) collective-permute-start(f32[16,128,128]{2,1,0:T(8,128)S(1)} %copy-done.3), channel_id=1, source_target_pairs={{0,3},{1,0},{2,1},{3,2},{4,7},{5,4},{6,5},{7,6},{8,11},{9,8},{10,9... | collective-permute-start | bytes 3145736 | tf_op jit(solution)/shard_map/ppermute | solution.py:473
  105.4 9.8 %collective-permute-done.6 = f32[16,64,128]{2,1,0:T(8,128)} collective-permute-done((f32[16,64,128]{2,1,0:T(8,128)}, f32[16,64,128]{2,1,0:T(8,128)}, u32[]{:S(2)}, u32[]{:S(2)}) %collective-permute-start.6) | collective-permute-done | bytes 524320 | tf_op jit(solution)/shard_map/ppermute | solution.py:473
  115.3 0.3 collective-permute-start.7
  115.5 3.0 %collective-permute-start.9 = (f32[16,64,128]{2,1,0:T(8,128)}, f32[16,64,128]{2,1,0:T(8,128)S(1)}, u32[]{:S(2)}, u32[]{:S(2)}) collective-permute-start(f32[16,64,128]{2,1,0:T(8,128)} %collective-permute-done.8), channel_id=1, source_target_pairs={{0,3},{1,0},{2,1},{3,2},{4,7},{5,4},{6,5},{7,6},{8,11},{9,8},{10,9... | collective-permute-start | bytes 1572872 | tf_op jit(solution)/shard_map/ppermute | solution.py:473
  118.5 0.0 all-to-all-done.4.gram_ref
  118.5 0.0 copy-start.1
  118.6 41.0 %all_to_all.31.mid_ref = f32[128,8,128]{2,1,0:T(8,128)} all-to-all(f32[128,8,128]{2,1,0:T(8,128)S(1)} %broadcast_in_dim.10), channel_id=1, replica_groups=mesh['cuts_0'=4,'cuts_1'=4,'cuts_2'=2,'rank'=4] {'rank','cuts_0','cuts_1..., dimensions={0} | all-to-all | bytes 1048576 | tf_op jit(solution)/shard_map/all_to_all | solution.py:468
  159.6 13.7 %factor.1 = (f32[512,256]{1,0:T(8,128)}, f32[256,512]{1,0:T(8,128)}) custom-call(f32[128,8,128]{2,1,0:T(8,128)} %all_to_all.31.mid_ref, f32[32,48,128]{2,1,0:T(8,128)} %copy-done.1), custom_call_target="tpu_custom_call" | custom-call | tf_op jit(solution)/shard_map/factor/pallas_call | solution.py:334
  173.2 0.0 collective-permute-done.7.refs_2_
  173.3 0.0 collective-permute-done.5.refs_1_
  173.3 0.8 copy-done.6
  174.0 5.8 %project.1 = f32[256,16,128]{2,1,0:T(8,128)} custom-call(s32[1]{0:T(128)} %bitcast.1.rank_ref, f32[256,512]{1,0:T(8,128)} %get-tuple-element.15.project_ref, f32[16,128,128]{2,1,0:T(8,128)} %get-tuple-element.9.refs_0_, f32[16,128,128]{2,1,0:T(8,128)} %collective-permute-done.5.refs_1_, f32[16,64,128]{2,1,0:T(8,128)} %collective-permute-done.7.refs_2_, ...), custom_call_target="tpu_custom_call" | custom-call | tf_op jit(solution)/shard_map/project/pallas_call | solution.py:447
  179.9 3.6 %all-to-all-start.5 = ((f32[4,64,16,128]{3,2,1,0:T(8,128)}), f32[4,64,16,128]{3,2,1,0:T(8,128)S(1)}, u32[]{:S(2)}, u32[]{:S(2)}) async-start(f32[4,64,16,128]{3,2,1,0:T(8,128)} %bitcast.18), calls=%async_computation.5 | async-start | bytes 4194304 | tf_op jit(solution)/shard_map/all_to_all | solution.py:520
  183.5 5.4 %ortho.1 = f32[2048,256]{1,0:T(8,128)} custom-call(f32[2048,512]{1,0:T(8,128)} %bitcast.17, f32[512,256]{1,0:T(8,128)} %get-tuple-element.14.right_ref), custom_call_target="tpu_custom_call" | custom-call | tf_op jit(solution)/shard_map/ortho/pallas_call | solution.py:397
  188.9 20.3 %all-to-all-done.5 = f32[4,64,16,128]{3,2,1,0:T(8,128)S(1)} async-done(((f32[4,64,16,128]{3,2,1,0:T(8,128)}), f32[4,64,16,128]{3,2,1,0:T(8,128)S(1)}, u32[]{:S(2)}, u32[]{:S(2)}) %all-to-all-start.5) | async-done | bytes 2097184 | tf_op jit(solution)/shard_map/all_to_all | solution.py:520
  209.2 1.6 copy_bitcast_fusion
  (22 shorter events, 0.2 us)
Async XLA Ops:
  6.5 9.7 %copy-start = (f32[32,48,128]{2,1,0:T(8,128)S(1)}, f32[32,48,128]{2,1,0:T(8,128)}, u32[]{:S(2)}) copy-start(f32[32,48,128]{2,1,0:T(8,128)} %gram.1) | copy-start | bytes 2359300
  41.7 23.7 %all-to-all-start.1 = ((f32[128,8,128]{2,1,0:T(8,128)}), f32[128,8,128]{2,1,0:T(8,128)S(1)}, u32[]{:S(2)}, u32[]{:S(2)}) async-start(f32[128,8,128]{2,1,0:T(8,128)} %broadcast_in_dim.9), calls=%async_computation.1 | async-start | bytes 1048576 | tf_op jit(solution)/shard_map/all_to_all | solution.py:468
  51.3 8.0 %collective-permute-start = (f32[128,512]{1,0:T(8,128)S(1)}, f32[128,512]{1,0:T(8,128)S(1)}, u32[]{:S(2)}, u32[]{:S(2)}) collective-permute-start(f32[128,512]{1,0:T(8,128)S(1)} %bitcast.20), channel_id=1, source_target_pairs={{0,4},{4,8},{8,12},{12,16},{16,20},{20,24},{24,28},{28,32},{32,36}... | collective-permute-start | bytes 786440 | tf_op jit(solution)/shard_map/ppermute | solution.py:479
  52.7 6.6 %collective-permute-start.1 = (f32[128,512]{1,0:T(8,128)S(1)}, f32[128,512]{1,0:T(8,128)S(1)}, u32[]{:S(2)}, u32[]{:S(2)}) collective-permute-start(f32[128,512]{1,0:T(8,128)S(1)} %bitcast.21), channel_id=1, source_target_pairs={{4,0},{8,4},{12,8},{16,12},{20,16},{24,20},{28,24},{32,28},{36,32}... | collective-permute-start | bytes 786440 | tf_op jit(solution)/shard_map/ppermute | solution.py:480
  54.0 32.2 %collective-permute-start.3 = (f32[48,128]{1,0:T(8,128)S(1)}, f32[48,128]{1,0:T(8,128)S(1)}, u32[]{:S(2)}, u32[]{:S(2)}) collective-permute-start(f32[48,128]{1,0:T(8,128)S(1)} %slice.17), channel_id=1, source_target_pairs={{0,2},{1,3},{2,0},{3,1},{4,6},{5,7},{6,4},{7,5},{8,10},{9,11},{10,... | collective-permute-start | bytes 73736 | tf_op jit(solution)/shard_map/ppermute | solution.py:473
  57.2 29.0 %collective-permute-start.4 = (f32[48,128]{1,0:T(8,128)S(1)}, f32[48,128]{1,0:T(8,128)S(1)}, u32[]{:S(2)}, u32[]{:S(2)}) collective-permute-start(f32[48,128]{1,0:T(8,128)S(1)} %slice.17), channel_id=1, source_target_pairs={{0,3},{1,0},{2,1},{3,2},{4,7},{5,4},{6,5},{7,6},{8,11},{9,8},{10,9... | collective-permute-start | bytes 73736 | tf_op jit(solution)/shard_map/ppermute | solution.py:473
  58.4 27.8 %collective-permute-start.2 = (f32[48,128]{1,0:T(8,128)S(1)}, f32[48,128]{1,0:T(8,128)S(1)}, u32[]{:S(2)}, u32[]{:S(2)}) collective-permute-start(f32[48,128]{1,0:T(8,128)S(1)} %slice.17), channel_id=1, source_target_pairs={{0,1},{1,2},{2,3},{3,0},{4,5},{5,6},{6,7},{7,4},{8,9},{9,10},{10,1... | collective-permute-start | bytes 73736 | tf_op jit(solution)/shard_map/ppermute | solution.py:473
  59.3 0.7 copy-start.7
  60.0 0.7 copy-start.8
  65.3 0.8 copy-start.2
  75.7 24.7 %copy-start.5 = (f32[16,64,128]{2,1,0:T(8,128)S(1)}, f32[16,64,128]{2,1,0:T(8,128)}, u32[]{:S(2)}) copy-start(f32[16,64,128]{2,1,0:T(8,128)} %get-tuple-element.12.refs_3_) | copy-start | bytes 1572868
  75.7 26.4 %copy-start.4 = (f32[16,128,128]{2,1,0:T(8,128)S(1)}, f32[16,128,128]{2,1,0:T(8,128)}, u32[]{:S(2)}) copy-start(f32[16,128,128]{2,1,0:T(8,128)} %get-tuple-element.10.refs_1_) | copy-start | bytes 3145732
  75.7 26.7 %copy-start.3 = (f32[16,128,128]{2,1,0:T(8,128)S(1)}, f32[16,128,128]{2,1,0:T(8,128)}, u32[]{:S(2)}) copy-start(f32[16,128,128]{2,1,0:T(8,128)} %get-tuple-element.13.refs_4_) | copy-start | bytes 3145732
  75.8 18.2 %all-to-all-start.2 = ((f32[32,8,128]{2,1,0:T(8,128)}), f32[32,8,128]{2,1,0:T(8,128)S(1)}, u32[]{:S(2)}, u32[]{:S(2)}) async-start(f32[32,8,128]{2,1,0:T(8,128)} %contract.3), calls=%async_computation.2 | async-start | bytes 262144 | tf_op jit(solution)/shard_map/all_to_all | solution.py:463
  94.9 23.6 %all-to-all-start.4 = ((f32[32,48,128]{2,1,0:T(8,128)}), f32[32,48,128]{2,1,0:T(8,128)S(1)}, u32[]{:S(2)}, u32[]{:S(2)}) async-start(f32[32,48,128]{2,1,0:T(8,128)} %broadcast_in_dim.11), calls=%async_computation.4 | async-start | bytes 1572864 | tf_op jit(solution)/shard_map/all_to_all | solution.py:468
  98.9 16.4 %collective-permute-start.6 = (f32[16,64,128]{2,1,0:T(8,128)}, f32[16,64,128]{2,1,0:T(8,128)}, u32[]{:S(2)}, u32[]{:S(2)}) collective-permute-start(f32[16,64,128]{2,1,0:T(8,128)} %get-tuple-element.11.refs_2_), channel_id=1, source_target_pairs={{0,1},{1,2},{2,3},{3,0},{4,5},{5,6},{6,7},{7,4},{8,9},{9,10},{10,1... | collective-permute-start | bytes 1572872 | tf_op jit(solution)/shard_map/ppermute | solution.py:473
  100.4 15.1 %collective-permute-start.8 = (f32[16,64,128]{2,1,0:T(8,128)S(1)}, f32[16,64,128]{2,1,0:T(8,128)}, u32[]{:S(2)}, u32[]{:S(2)}) collective-permute-start(f32[16,64,128]{2,1,0:T(8,128)S(1)} %copy-done.5), channel_id=1, source_target_pairs={{0,3},{1,0},{2,1},{3,2},{4,7},{5,4},{6,5},{7,6},{8,11},{9,8},{10,9... | collective-permute-start | bytes 1572872 | tf_op jit(solution)/shard_map/ppermute | solution.py:473
  102.2 71.1 %collective-permute-start.5 = (f32[16,128,128]{2,1,0:T(8,128)S(1)}, f32[16,128,128]{2,1,0:T(8,128)}, u32[]{:S(2)}, u32[]{:S(2)}) collective-permute-start(f32[16,128,128]{2,1,0:T(8,128)S(1)} %copy-done.4), channel_id=1, source_target_pairs={{0,1},{1,2},{2,3},{3,0},{4,5},{5,6},{6,7},{7,4},{8,9},{9,10},{10,1... | collective-permute-start | bytes 3145736 | tf_op jit(solution)/shard_map/ppermute | solution.py:473
  102.5 70.8 %collective-permute-start.10 = (f32[16,128,128]{2,1,0:T(8,128)S(1)}, f32[16,128,128]{2,1,0:T(8,128)}, u32[]{:S(2)}, u32[]{:S(2)}) collective-permute-start(f32[16,128,128]{2,1,0:T(8,128)S(1)} %copy-done.3), channel_id=1, source_target_pairs={{0,3},{1,0},{2,1},{3,2},{4,7},{5,4},{6,5},{7,6},{8,11},{9,8},{10,9... | collective-permute-start | bytes 3145736 | tf_op jit(solution)/shard_map/ppermute | solution.py:473
  115.3 58.0 %collective-permute-start.7 = (f32[16,64,128]{2,1,0:T(8,128)}, f32[16,64,128]{2,1,0:T(8,128)}, u32[]{:S(2)}, u32[]{:S(2)}) collective-permute-start(f32[16,64,128]{2,1,0:T(8,128)} %collective-permute-done.6), channel_id=1, source_target_pairs={{0,1},{1,2},{2,3},{3,0},{4,5},{5,6},{6,7},{7,4},{8,9},{9,10},{10,1... | collective-permute-start | bytes 1572872 | tf_op jit(solution)/shard_map/ppermute | solution.py:473
  115.5 57.7 %collective-permute-start.9 = (f32[16,64,128]{2,1,0:T(8,128)}, f32[16,64,128]{2,1,0:T(8,128)S(1)}, u32[]{:S(2)}, u32[]{:S(2)}) collective-permute-start(f32[16,64,128]{2,1,0:T(8,128)} %collective-permute-done.8), channel_id=1, source_target_pairs={{0,3},{1,0},{2,1},{3,2},{4,7},{5,4},{6,5},{7,6},{8,11},{9,8},{10,9... | collective-permute-start | bytes 1572872 | tf_op jit(solution)/shard_map/ppermute | solution.py:473
  118.5 41.0 %copy-start.1 = (f32[32,48,128]{2,1,0:T(8,128)}, f32[32,48,128]{2,1,0:T(8,128)S(1)}, u32[]{:S(2)}) copy-start(f32[32,48,128]{2,1,0:T(8,128)S(1)} %all-to-all-done.4.gram_ref) | copy-start | bytes 2359300
  173.2 0.8 copy-start.6
  179.9 29.4 %all-to-all-start.5 = ((f32[4,64,16,128]{3,2,1,0:T(8,128)}), f32[4,64,16,128]{3,2,1,0:T(8,128)S(1)}, u32[]{:S(2)}, u32[]{:S(2)}) async-start(f32[4,64,16,128]{3,2,1,0:T(8,128)} %bitcast.18), calls=%async_computation.5 | async-start | bytes 4194304 | tf_op jit(solution)/shard_map/all_to_all | solution.py:520
